TPU v7x, 512 devices: a whole 4x4x16 slice. The times are simulated.
512 devices in a mesh: env: 16 (over z), cand: 32 (over y, x, core).
Axes of the slice: x: 4, y: 4, z: 16, core: 2. Of those that a mesh axis runs over, the one named last changes fastest.
Arguments:
- white: bfloat16 [3, 256, 256, 4096], P(None, 'env', 'cand'), may hold values from -5 to 5
- mean_init: float32 [256, 2560], P('env'), may hold values from -0.3 to 0.3
- std_init: float32 [256, 2560], P('env'), may hold values from 0.05 to 0.8
- init_state: float32 [256, 128], P('env'), may hold values from -3 to 3
- goal_state: float32 [256, 128], P('env'), may hold values from -3 to 3
- w_state: bfloat16 [128, 512], replicated, may hold values from -0.5 to 0.5
- w_action: bfloat16 [64, 512], replicated, may hold values from -1.5 to 1.5
- w_out: bfloat16 [512, 128], replicated, may hold values from -0.25 to 0.25
- bias_in: float32 [512], replicated, may hold values from -3 to 3
- bias_out: float32 [128], replicated, may hold values from -3 to 3
- elite_idx: int32 [256, 3, 25], P('env'), may hold values from 0 to 255, all different within a row
Outputs:
- final_mean: float32 [256, 2560], P('env')
- final_std: float32 [256, 2560], P('env')
- costs: float32 [3, 256, 256], P(None, 'env', 'cand')
Inputs may be any that keep to these rules, and one draw needn't show every extreme that they name: `elite_idx`: each row names 25 different candidates.
All inputs are finite; a program needn't handle non-finite values.
Results may differ from a plain program's by a relative error of at most 0.0031.
Values sent between devices are 32-bit elements; how exact they have to be, the bound alone decides.
No kernel may reach another device: no remote copies, remote signals or barrier semaphores. Data moves between devices by JAX's collectives and lax.ppermute only.
A program may use at most 128 MiB of HBM per device.

v0:
```python
import jax
import jax.numpy as jnp
from jax import lax
from jax.sharding import PartitionSpec as P

BETA_EXP = 2.5
MOMENTUM = 0.1
FLOOR_SHARE = 0.1
ACT_COST = 0.1


def sent_to_all(array, axis):
    count = lax.axis_size(axis)
    return lax.all_to_all(
        jnp.broadcast_to(array[None], (count, *array.shape)), axis, 0, 0, tiled=True
    )


def collected_together(array, axis):
    leaves = jax.tree.leaves(array)
    sequence = sorted(range(len(leaves)), key=lambda k: -leaves[k].size)
    width = (1, *leaves[sequence[0]].shape)[-1]
    lines = [
        jnp.pad(leaves[k].reshape(-1), (0, -leaves[k].size % width)).reshape(-1, width)
        for k in sequence
    ]
    both, at, found = (sent_to_all(jnp.concatenate(lines), axis), 0, {})
    for k, line in zip(sequence, lines):
        share = both[:, at : at + len(line)].reshape(len(both), -1)
        found[k] = share[:, : leaves[k].size].reshape(-1, *leaves[k].shape)
        at += len(line)
    numbers = iter(range(len(leaves)))
    return jax.tree.map(lambda _: found[next(numbers)], array)


def gathered_by_type(array, axis):
    leaves, found = (jax.tree.leaves(array), {})
    for leading, a in enumerate(leaves):
        if leading not in found:
            alike = [k for k, b in enumerate(leaves) if b.dtype == a.dtype]
            got = (
                collected_together([leaves[k] for k in alike], axis)
                if len(alike) > 1
                else [sent_to_all(a, axis)]
            )
            for k, b in zip(alike, got):
                found[k] = b
    numbers = iter(range(len(leaves)))
    return jax.tree.map(lambda _: found[next(numbers)], array)


def folded_in_pairs(pieces, combine):
    while len(jax.tree.leaves(pieces)[0]) > 1:
        pieces = jax.vmap(combine)(
            *(jax.tree.map(lambda part: part[side::2], pieces) for side in (0, 1))
        )
    return jax.tree.map(lambda part: part[0], pieces)


def merged(array, axis, combine):
    pieces = gathered_by_type(array, axis)
    return folded_in_pairs(pieces, combine)


def gathered_total(array, axis):
    return lax.all_gather(array, axis).sum(0)


def color_table(length, horizon):
    half = length // 2
    freqs = jnp.arange(half + 1, dtype=jnp.int32)
    scale = (jnp.maximum(freqs, 1).astype(jnp.float32) / length) ** (-BETA_EXP / 2)
    factor = jnp.where((freqs == 0) | (freqs == half), 1.0, 2.0).astype(jnp.float32)
    weights = factor * scale / length
    shifts = jnp.arange(length, dtype=jnp.int32)
    phase = (freqs[:, None] * shifts[None, :] % length).astype(jnp.float32)
    kernel = jnp.sum(weights[:, None] * jnp.cos(2.0 * jnp.pi * phase / length), axis=0)
    kernel = kernel / jnp.sqrt(jnp.sum(kernel * kernel))
    kernel = kernel.astype(jnp.bfloat16).astype(jnp.float32)
    source = jnp.arange(length, dtype=jnp.int32)
    targets = jnp.arange(horizon, dtype=jnp.int32)
    offsets = (targets[None, :] - source[:, None]) % length
    picker = (offsets[:, :, None] == shifts[None, None, :]).astype(jnp.float32)
    return jnp.sum(picker * kernel[None, None, :], axis=-1).astype(jnp.bfloat16)


def rollout(actions, start, goal, w_state, w_action, w_out, bias_in, bias_out):
    ordered = jnp.swapaxes(actions, 0, 1)

    def advance(state, action):
        pre = jnp.dot(state.astype(jnp.bfloat16), w_state, preferred_element_type=jnp.float32)
        pre = (
            pre
            + jnp.dot(action.astype(jnp.bfloat16), w_action, preferred_element_type=jnp.float32)
            + bias_in
        )
        hidden = jax.nn.silu(pre).astype(jnp.bfloat16)
        state = jnp.tanh(
            state + jnp.dot(hidden, w_out, preferred_element_type=jnp.float32) + bias_out
        )
        error = state - goal
        step_cost = jnp.mean(error * error, axis=-1) + ACT_COST * jnp.mean(action * action, axis=-1)
        return (state, step_cost)

    final, step_costs = lax.scan(advance, start, ordered, unroll=4)
    return jnp.mean(step_costs, axis=0)


def refit(totals, center, spread, elites):
    elite_mean = totals[0] / elites
    variance = jnp.maximum(totals[1] / elites - elite_mean * elite_mean, 0.0)
    center_mix = MOMENTUM * center + (1.0 - MOMENTUM) * elite_mean
    spread_mix = MOMENTUM * spread + (1.0 - MOMENTUM) * jnp.sqrt(variance)
    return (center_mix, spread_mix)


def pair_combine(first, second):
    return (jnp.maximum(first[0], second[0]), first[1] + second[1])


def global_stats(env_peak, envs_total):
    peak, total = merged((jnp.max(env_peak), jnp.sum(env_peak)), "env", pair_combine)
    settled = total / (peak * envs_total)
    return (peak, settled)


def shards(
    white,
    mean_init,
    std_init,
    init_state,
    goal_state,
    w_state,
    w_action,
    w_out,
    bias_in,
    bias_out,
    elite_idx,
):
    iters, env_dev, cand_dev, flat = white.shape
    act_dim = w_action.shape[0]
    state_dim = w_state.shape[0]
    length = flat // act_dim
    hor_act = mean_init.shape[1]
    horizon = hor_act // act_dim
    elites = elite_idx.shape[2]
    envs_total = env_dev * lax.axis_size("env")
    table = color_table(length, horizon)
    cand_ids = lax.axis_index("cand") * cand_dev + jnp.arange(cand_dev, dtype=jnp.int32)
    row_count = env_dev * cand_dev
    starts = jnp.broadcast_to(init_state[:, None, :], (env_dev, cand_dev, state_dim)).reshape(
        row_count, state_dim
    )
    goals = jnp.broadcast_to(goal_state[:, None, :], (env_dev, cand_dev, state_dim)).reshape(
        row_count, state_dim
    )
    center, spread = (mean_init, std_init)
    cost_list = []
    for iteration in range(iters):
        series = white[iteration].reshape(env_dev, cand_dev, length, act_dim)
        noise = jnp.einsum(
            "ecja,jt->ecta", series, table, preferred_element_type=jnp.float32
        ).reshape(env_dev, cand_dev, hor_act)
        actions = jnp.clip(center[:, None, :] + spread[:, None, :] * noise, -1.0, 1.0)
        block_costs = rollout(
            actions.reshape(row_count, horizon, act_dim),
            starts,
            goals,
            w_state,
            w_action,
            w_out,
            bias_in,
            bias_out,
        )
        cost_list.append(block_costs.reshape(env_dev, cand_dev))
        member = jnp.sum(
            (elite_idx[:, iteration, :, None] == cand_ids[None, None, :]).astype(jnp.float32),
            axis=1,
        )
        sums = jnp.einsum("ec,ech->eh", member, actions)
        squares = jnp.einsum("ec,ech->eh", member, actions * actions)
        partial_stats = jnp.stack([sums, squares])
        totals = gathered_total(partial_stats, "cand")
        center_mix, spread_mix = refit(totals, center, spread, elites)
        env_peak = jnp.max(spread_mix, axis=1)
        peak, settled = global_stats(env_peak, envs_total)
        center = center_mix
        spread = jnp.maximum(spread_mix, FLOOR_SHARE * peak) * (0.5 + settled)
    return (center, spread, jnp.stack(cost_list))


def solution(mesh):
    in_specs = (
        P(None, "env", "cand", None),
        P("env", None),
        P("env", None),
        P("env", None),
        P("env", None),
        P(),
        P(),
        P(),
        P(),
        P(),
        P("env", None, None),
    )
    out_specs = (P("env", None), P("env", None), P(None, "env", "cand"))
    return jax.shard_map(shards, mesh=mesh, in_specs=in_specs, out_specs=out_specs, check_vma=False)
```

profile of v0, /device:TPU:1, one launch (start us, length us, event | category | flops | bytes accessed | tf_op | source)
XLA Modules:
  0.0 460.9 jit_solution(6661992983575326652)
XLA Ops:
  10.4 3.5 fusion.249
  13.9 3.3 reshape_squeeze.9
  17.2 2.1 fusion.215
  24.4 4.3 reshape_squeeze.10
  28.7 4.2 reshape_squeeze.11
  34.2 3.0 add.925
  38.3 2.9 mul.703
  41.3 4.5 fusion.146
  45.8 84.8 %while.48 = (s32[]{:T(128)}, f32[128,128]{0,1:T(8,128)S(1)}, f32[10,4,128]{2,1,0:T(4,128)S(1)}, bf16[128,512]{1,0:T(8,128)(2,1)S(1)}, f32[10,4,128,64]{3,1,0,2:T...) while((s32[]{:T(128)}, f32[128,128]{0,1:T(8,128)S(1)}, ...), condition=%wide.region_27.28_spmd.clone, body=%wide.region_18.0_spmd.clone.sunk | while | flops 170100736 | bytes 5406973 | solution.py:105
  113.4 2.1 constant_dynamic-slice_fusion.15
  133.2 5.3 %reduce_sum.451 = f32[2,16,2560]{2,1,0:T(8,128)} reduce(f32[32,2,16,2560]{3,2,1,0:T(8,128)} %bitcast.441, f32[]{:T(128)} %constant.282.clone.1), dimensions={0}, to_apply=%region_4.5 | reduce | flops 2539520 | bytes 10813444 | tf_op jit(solution)/shard_map/reduce_sum | solution.py:66
  142.8 15.8 %all-to-all-start = ((f32[16,2,1]{1,2,0:T(1,128)}), f32[16,2,1]{1,2,0:T(1,128)S(1)}, u32[]{:S(2)}, u32[]{:S(2)}) async-start(f32[16,2,1]{1,2,0:T(1,128)} %broadcast_in_dim.61), calls=%async_computation | async-start | bytes 16384 | tf_op jit(solution)/shard_map/all_to_all | solution.py:14
  158.6 2.9 reshape.652
  164.5 2.9 add.927
  167.4 2.4 all-to-all-done
  178.5 2.9 mul.705
  182.2 5.2 %fusion.144 = f32[128,40,64]{2,1,0:T(8,128)} fusion(f32[128,40,64]{2,1,0:T(8,128)} %add.927, f32[128,40,64]{2,1,0:T(8,128)} %mul.705, f32[40,16,8,64]{3,0,2,1:T(8,128)} %fusion.213), kind=kLoop, calls=%fused_computation.221 | loop fusion | flops 983040 | bytes 5242880 | tf_op jit(solution)/shard_map/jit(clip)/min | solution.py:164
  187.4 113.7 %while.49 = (s32[]{:T(128)}, f32[128,128]{0,1:T(8,128)S(1)}, f32[10,4,128]{2,1,0:T(4,128)S(1)}, bf16[128,512]{1,0:T(8,128)(2,1)}, f32[10,4,128,64]{3,1,0,2:T(4,1...) while((s32[]{:T(128)}, f32[128,128]{0,1:T(8,128)S(1)}, ...), condition=%wide.region_38.39_spmd.clone, body=%wide.region_29.38_spmd.clone.sunk | while | flops 170100736 | bytes 5406973 | solution.py:105
  192.6 2.0 fusion.438
  194.9 2.1 multiply_reduce_fusion.45
  204.0 2.0 fusion.438
  206.4 2.1 multiply_reduce_fusion.45
  215.5 2.0 fusion.438
  217.8 2.1 multiply_reduce_fusion.45
  226.7 2.0 fusion.438
  229.0 2.1 multiply_reduce_fusion.45
  238.0 2.0 fusion.438
  240.3 2.1 multiply_reduce_fusion.45
  249.5 2.1 fusion.438
  251.9 2.1 multiply_reduce_fusion.45
  261.0 2.0 fusion.438
  263.3 2.1 multiply_reduce_fusion.45
  272.2 2.0 fusion.438
  274.5 2.1 multiply_reduce_fusion.45
  283.5 2.0 fusion.438
  285.8 2.1 multiply_reduce_fusion.45
  297.2 2.1 multiply_reduce_fusion.45
  301.2 5.3 %reduce_sum.454 = f32[2,16,2560]{2,1,0:T(8,128)} reduce(f32[32,2,16,2560]{3,2,1,0:T(8,128)} %bitcast.443, f32[]{:T(128)} %constant.282.clone.1), dimensions={0}, to_apply=%region_9.10 | reduce | flops 2539520 | bytes 10813444 | tf_op jit(solution)/shard_map/reduce_sum | solution.py:66
  310.8 9.1 %all-to-all-start.1 = ((f32[16,2,1]{1,2,0:T(1,128)}), f32[16,2,1]{1,2,0:T(1,128)S(1)}, u32[]{:S(2)}, u32[]{:S(2)}) async-start(f32[16,2,1]{1,2,0:T(1,128)} %broadcast_in_dim.63), calls=%async_computation.1 | async-start | bytes 16384 | tf_op jit(solution)/shard_map/all_to_all | solution.py:14
  321.4 3.0 add.929
  324.4 6.7 %all-to-all-done.1 = f32[16,2,1]{1,2,0:T(1,128)S(1)} async-done(((f32[16,2,1]{1,2,0:T(1,128)}), f32[16,2,1]{1,2,0:T(1,128)S(1)}, u32[]{:S(2)}, u32[]{:S(2)}) %all-to-all-start.1) | async-done | bytes 160 | tf_op jit(solution)/shard_map/all_to_all | solution.py:14
  339.8 2.9 mul.707
  343.6 4.5 fusion.142
  348.1 75.6 %while.50 = (s32[]{:T(128)}, f32[128,128]{0,1:T(8,128)S(1)}, f32[10,4,128]{2,1,0:T(4,128)S(1)}, bf16[128,512]{1,0:T(8,128)(2,1)S(1)}, f32[10,4,128,64]{3,1,0,2:T...) while((s32[]{:T(128)}, f32[128,128]{0,1:T(8,128)S(1)}, ...), condition=%wide.region_49.50_spmd.clone, body=%wide.region_40.0_spmd.clone.sunk | while | flops 170100736 | bytes 4882629 | solution.py:105
  408.3 2.1 constant_dynamic-slice_fusion.17
  423.9 4.5 reduce_sum.457
  432.4 4.7 %all-to-all-start.2 = ((f32[16,2,1]{1,2,0:T(1,128)}), f32[16,2,1]{1,2,0:T(1,128)S(1)}, u32[]{:S(2)}, u32[]{:S(2)}) async-start(f32[16,2,1]{1,2,0:T(1,128)} %broadcast_in_dim.65), calls=%async_computation.2 | async-start | bytes 16384 | tf_op jit(solution)/shard_map/all_to_all | solution.py:14
  437.8 10.6 %all-to-all-done.2 = f32[16,2,1]{1,2,0:T(1,128)S(1)} async-done(((f32[16,2,1]{1,2,0:T(1,128)}), f32[16,2,1]{1,2,0:T(1,128)S(1)}, u32[]{:S(2)}, u32[]{:S(2)}) %all-to-all-start.2) | async-done | bytes 160 | tf_op jit(solution)/shard_map/all_to_all | solution.py:14
  (778 shorter events, 274.3 us)
Async XLA Ops:
  7.2 17.1 %copy-start = (f32[16,128]{1,0:T(8,128)S(1)}, f32[16,128]{1,0:T(8,128)}, u32[]{:S(2)}) copy-start(f32[16,128]{1,0:T(8,128)} %param.20) | copy-start | bytes 24580
  7.2 126.1 %all-gather.7.cloned.1.call-start = ((), (), s32[]{:S(2)}) async-start(), calls=%async_computation.3 | async-start | bytes 10813440 | tf_op jit(solution)/shard_map/all_gather | solution.py:66
  24.4 4.3 copy-start.13
  41.2 4.5 copy-start.2
  41.3 4.5 copy-start.10
  41.3 4.5 copy-start.16
  41.3 4.5 copy-start.17
  41.3 4.5 copy-start.19
  45.8 84.9 %copy-start.6 = (bf16[16,8,64,64]{3,2,1,0:T(8,128)(2,1)S(1)}, bf16[16,8,64,64]{3,2,1,0:T(8,128)(2,1)}, u32[]{:S(2)}) copy-start(bf16[16,8,64,64]{3,2,1,0:T(8,128)(2,1)} %reshape_squeeze.10) | copy-start | bytes 3145732
  48.8 3.2 copy-start.21
  57.2 3.2 copy-start.21
  65.5 3.2 copy-start.21
  74.0 3.2 copy-start.21
  82.4 3.2 copy-start.21
  91.1 3.2 copy-start.21
  99.5 3.2 copy-start.21
  108.0 3.2 copy-start.21
  116.7 3.2 copy-start.21
  125.2 3.2 copy-start.21
  140.2 34.9 %copy-start.11 = (f32[16,2560]{1,0:T(8,128)}, f32[16,2560]{1,0:T(8,128)S(1)}, u32[]{:S(2)}) copy-start(f32[16,2560]{1,0:T(8,128)S(1)} %get-tuple-element.854) | copy-start | bytes 491524
  142.8 27.1 %all-to-all-start = ((f32[16,2,1]{1,2,0:T(1,128)}), f32[16,2,1]{1,2,0:T(1,128)S(1)}, u32[]{:S(2)}, u32[]{:S(2)}) async-start(f32[16,2,1]{1,2,0:T(1,128)} %broadcast_in_dim.61), calls=%async_computation | async-start | bytes 16384 | tf_op jit(solution)/shard_map/all_to_all | solution.py:14
  158.6 142.6 %all-gather.9.cloned.1.call-start = ((), (), s32[]{:S(2)}) async-start(), calls=%async_computation.4 | async-start | bytes 10813440 | tf_op jit(solution)/shard_map/all_gather | solution.py:66
  171.4 5.5 %copy-start.4 = (f32[16,8,2560]{2,1,0:T(8,128)S(1)}, f32[16,8,2560]{2,1,0:T(8,128)}, u32[]{:S(2)}) copy-start(f32[16,8,2560]{2,1,0:T(8,128)} %reshape.652) | copy-start | bytes 3932164
  182.2 5.2 %copy-start.15 = (f32[128,128]{0,1:T(8,128)S(1)}, f32[128,128]{0,1:T(8,128)}, u32[]{:S(2)}) copy-start(f32[128,128]{0,1:T(8,128)} %copy-done.13) | copy-start | bytes 196612
  190.8 3.8 copy-start.22
  192.4 2.4 copy-start.24
  202.3 3.8 copy-start.22
  203.9 2.4 copy-start.24
  213.7 3.8 copy-start.22
  215.3 2.4 copy-start.24
  225.0 3.8 copy-start.22
  236.2 3.8 copy-start.22
  237.8 2.4 copy-start.24
  247.8 3.8 copy-start.22
  249.4 2.4 copy-start.24
  259.2 3.8 copy-start.22
  270.4 3.8 copy-start.22
  281.8 3.8 copy-start.22
  293.1 3.8 copy-start.22
  301.2 5.3 %copy-start.12 = (f32[16,2560]{1,0:T(8,128)S(1)}, f32[16,2560]{1,0:T(8,128)}, u32[]{:S(2)}) copy-start(f32[16,2560]{1,0:T(8,128)} %copy-done.11) | copy-start | bytes 491524
  310.8 20.3 %all-to-all-start.1 = ((f32[16,2,1]{1,2,0:T(1,128)}), f32[16,2,1]{1,2,0:T(1,128)S(1)}, u32[]{:S(2)}, u32[]{:S(2)}) async-start(f32[16,2,1]{1,2,0:T(1,128)} %broadcast_in_dim.63), calls=%async_computation.1 | async-start | bytes 16384 | tf_op jit(solution)/shard_map/all_to_all | solution.py:14
  319.9 104.0 %all-gather.11.cloned.1.call-start = ((), (), s32[]{:S(2)}) async-start(), calls=%async_computation.5 | async-start | bytes 10813440 | tf_op jit(solution)/shard_map/all_gather | solution.py:66
  332.6 5.6 %copy-start.3 = (f32[16,8,2560]{2,1,0:T(8,128)S(1)}, f32[16,8,2560]{2,1,0:T(8,128)}, u32[]{:S(2)}) copy-start(f32[16,8,2560]{2,1,0:T(8,128)} %reshape.655) | copy-start | bytes 3932164
  343.6 4.5 copy-start.14
  343.6 4.5 copy-start.18
  343.6 4.5 copy-start.20
  423.9 30.5 %copy-start.1 = (f32[16,128]{1,0:T(8,128)S(1)}, f32[16,128]{1,0:T(8,128)}, u32[]{:S(2)}) copy-start(f32[16,128]{1,0:T(8,128)} %param.20) | copy-start | bytes 24580
  432.4 16.0 %all-to-all-start.2 = ((f32[16,2,1]{1,2,0:T(1,128)}), f32[16,2,1]{1,2,0:T(1,128)S(1)}, u32[]{:S(2)}, u32[]{:S(2)}) async-start(f32[16,2,1]{1,2,0:T(1,128)} %broadcast_in_dim.65), calls=%async_computation.2 | async-start | bytes 16384 | tf_op jit(solution)/shard_map/all_to_all | solution.py:14
  (19 other events, 40.6 us)
Sparse Core Ops, SparseCore 0:
  24.4 78.8 all-gather.6
  182.3 72.6 all-gather.8
  343.7 69.2 all-gather.10
where the time goes:
time: 468 us; the launch traced here: 461 us
  matrix products  198 us (42%)
  local copies, waits for them, and re-layouts  115 us (25%)
  other arithmetic  72 us (15%)
  starting transfers between devices  29.9 us (6%)
  between operations  22.7 us (5%)
  waiting for transfers between devices  19.8 us (4%)
    dot_general x120, matrix products, advance(): jnp.dot(hidden, w_out, preferred_element_type=jnp.float32)  168 us
    slice x30, local copies, waits for them, and re-layouts, rollout(): final, step_costs = lax.scan(advance, start, ordered, unroll=4)  53.5 us
    all_to_all x3, starting transfers between devices, sent_to_all(): lax.all_to_all(jnp.broadcast_to(array[None], (count, *array.shape)), axis...  29.6 us
    all_to_all x3, waiting for transfers between devices, sent_to_all(): lax.all_to_all(jnp.broadcast_to(array[None], (count, *array.shape)), axis...  19.7 us
    dot_general x120, matrix products, advance(): jnp.dot(action.astype(jnp.bfloat16), w_action, preferred_element_type=jnp...  18.7 us
    reduce_sum x3, other arithmetic, gathered_total(): return lax.all_gather(array, axis).sum(0)  15.1 us
    min x3, other arithmetic, shards(): jnp.clip(center[:, None, :] + spread[:, None, :] * noise, -1.0, 1.0)  14.1 us
    add x60, other arithmetic, advance(): jnp.mean(error * error, axis=-1)  13.3 us
  transfers between devices with their start and end apart: 6, of which 3 were waited for; matrix products, arithmetic and copies ran while one was open for 69% of the time, Pallas kernels for 0%

commit v1 on v0

v1 whole, which is shorter than its diff:
```python
import functools

import jax
import jax.numpy as jnp
import numpy as np
from jax import lax
from jax.experimental import pallas as pl
from jax.experimental.pallas import tpu as pltpu
from jax.sharding import PartitionSpec as P

BETA_EXP = 2.5
MOMENTUM = 0.1
FLOOR_SHARE = 0.1
ACT_COST = 0.1
LANES = 128
VMEM = pl.BlockSpec(memory_space=pltpu.VMEM)
SMEM = pl.BlockSpec(memory_space=pltpu.SMEM)


def color_kernel(length):
    freqs = np.arange(length // 2 + 1)
    scale = (np.maximum(freqs, 1).astype(np.float32) / np.float32(length)) ** np.float32(-BETA_EXP / 2)
    kernel = np.fft.irfft(scale.astype(np.float64), n=length)
    kernel = kernel / np.sqrt(np.sum(kernel * kernel))
    return np.asarray(kernel, np.float32).astype(jnp.bfloat16).astype(np.float32)


def band_rows(length, act_dim):
    per = 256 // act_dim
    kernel = color_kernel(length)
    rows = np.arange(length)[:, None]
    quarter = np.arange(256)[None, :] // act_dim
    return jnp.asarray(kernel[(quarter - rows) % length], jnp.float32), per


def noise_body(white_ref, band_ref, out_ref, fill, *, act_dim, blocks):
    length = band_ref.shape[0]
    flat = length * act_dim

    @pl.when(pl.program_id(0) == 0)
    def _():
        row = lax.broadcasted_iota(jnp.int32, (act_dim, 256), 0)
        lane = lax.broadcasted_iota(jnp.int32, (act_dim, 256), 1)
        hit = lane % act_dim == row
        for j in range(length):
            tile = jnp.where(hit, band_ref[pl.ds(j, 1), :], 0.0).astype(jnp.bfloat16)
            fill[pl.ds(j * act_dim, act_dim), :] = tile
            fill[pl.ds(flat + j * act_dim, act_dim), :] = tile

    for block in range(blocks):
        start = (flat - block * 256) % flat
        out_ref[0, :, pl.ds(block * 256, 256)] = jnp.dot(
            white_ref[0], fill[pl.ds(start, flat), :], preferred_element_type=jnp.float32
        )


def noise_of(white, first, count, band, act_dim, horizon):
    _, rows, flat = white.shape
    width = horizon * act_dim
    return pl.pallas_call(
        functools.partial(noise_body, act_dim=act_dim, blocks=width // 256),
        grid=(count,),
        in_specs=[
            pl.BlockSpec((1, rows, flat), lambda i: (i + first, 0, 0)),
            pl.BlockSpec(band.shape, lambda i: (0, 0)),
        ],
        out_specs=pl.BlockSpec((1, rows, width), lambda i: (i, 0, 0)),
        out_shape=jax.ShapeDtypeStruct((count, rows, width), jnp.float32),
        scratch_shapes=[pltpu.VMEM((2 * flat, 256), jnp.bfloat16)],
        compiler_params=pltpu.CompilerParams(vmem_limit_bytes=40 << 20),
        name="noise",
    )(white, band)


def action_body(*refs, first, envs_total, groups):
    noise_ref, member_ref, mine_ref, state_ref, acts_ref, asq_ref, sums_ref, own_ref = refs
    half = sums_ref.shape[2]
    rows = acts_ref.shape[0]
    envs = sums_ref.shape[0] // 2
    cands = rows // envs
    me = mine_ref[0]
    if first:
        floor, gain = None, None
    else:
        peaks = state_ref[:, 0, pl.ds(half, LANES)]
        pair = jnp.max(peaks.reshape(envs, 2, LANES), axis=1)
        peak = jnp.max(pair, axis=(0, 1), keepdims=True)
        total = jnp.sum(jnp.sum(pair, axis=0, keepdims=True), axis=1, keepdims=True)
        floor = FLOOR_SHARE * peak
        gain = 0.5 + total / (peak * envs_total)

    def spread_of(mixed):
        return mixed if first else jnp.maximum(mixed, floor) * gain

    own = state_ref[me, :, pl.ds(0, half)]
    own_ref[0:1, :] = own[0:1]
    own_ref[1:2, :] = spread_of(own[1:2])
    for env in range(envs):
        at = pl.ds(env * cands, cands)
        member = member_ref[at, :]
        square = jnp.zeros((cands, LANES), jnp.float32)
        for side in range(2):
            line = 2 * env + side
            for step in range(half // LANES):
                lanes = pl.ds(step * LANES, LANES)
                whole = pl.ds(side * half + step * LANES, LANES)
                center = state_ref[line, 0:1, lanes]
                spread = spread_of(state_ref[line, 1:2, lanes])
                action = jnp.clip(center + spread * noise_ref[0, at, whole], -1.0, 1.0)
                acts_ref[at, whole] = action.astype(jnp.bfloat16)
                both = action * action
                square = square + both
                sums_ref[line, 0:1, lanes] = jnp.sum(action * member, axis=0, keepdims=True)
                sums_ref[line, 1:2, lanes] = jnp.sum(both * member, axis=0, keepdims=True)
        asq_ref[at, :] = square


def actions_of(noise, at, member, mine, state, first, envs_total, groups, lines, half):
    _, rows, width = noise.shape
    return pl.pallas_call(
        functools.partial(action_body, first=first, envs_total=envs_total, groups=groups),
        grid=(1,),
        in_specs=[
            pl.BlockSpec((1, rows, width), lambda i: (at, 0, 0)),
            VMEM,
            SMEM,
            VMEM,
        ],
        out_specs=[VMEM, VMEM, VMEM, VMEM],
        out_shape=[
            jax.ShapeDtypeStruct((rows, width), jnp.bfloat16),
            jax.ShapeDtypeStruct((rows, LANES), jnp.float32),
            jax.ShapeDtypeStruct((lines, 2, half), jnp.float32),
            jax.ShapeDtypeStruct((2, half), jnp.float32),
        ],
        name="actions",
    )(noise, member, mine, state)


def refit_body(parts_ref, own_ref, slice_ref, peak_ref, *, elites):
    total = jnp.sum(parts_ref[...], axis=0)
    mean = total[0:1] / elites
    variance = jnp.maximum(total[1:2] / elites - mean * mean, 0.0)
    slice_ref[0:1, :] = MOMENTUM * own_ref[0:1, :] + (1.0 - MOMENTUM) * mean
    mixed = MOMENTUM * own_ref[1:2, :] + (1.0 - MOMENTUM) * jnp.sqrt(variance)
    slice_ref[1:2, :] = mixed
    peak_ref[...] = jnp.broadcast_to(jnp.max(mixed, axis=1, keepdims=True)[None], peak_ref.shape)


def refit(parts, own, elites, groups):
    return pl.pallas_call(
        functools.partial(refit_body, elites=elites),
        in_specs=[VMEM, VMEM],
        out_specs=[VMEM, VMEM],
        out_shape=[
            jax.ShapeDtypeStruct(own.shape, jnp.float32),
            jax.ShapeDtypeStruct((groups, 1, LANES), jnp.float32),
        ],
        name="refit",
    )(parts, own)


def spread_body(slice_ref, peak_ref, out_ref):
    lines, _, wide = out_ref.shape
    half = slice_ref.shape[1]
    lane = lax.broadcasted_iota(jnp.int32, (1, LANES), 1)
    tail = jnp.zeros((1, LANES), jnp.float32)
    for group in range(peak_ref.shape[0]):
        tail = jnp.where(lane == group, peak_ref[group], tail)
    main = jnp.broadcast_to(slice_ref[...][None], (lines, 2, half))
    out_ref[:, :, pl.ds(0, half)] = main
    out_ref[:, :, pl.ds(half, LANES)] = jnp.broadcast_to(tail[None], (lines, 2, LANES))


def to_all(piece, peaks, lines):
    half = piece.shape[1]
    return pl.pallas_call(
        spread_body,
        in_specs=[VMEM, VMEM],
        out_specs=VMEM,
        out_shape=jax.ShapeDtypeStruct((lines, 2, half + LANES), jnp.float32),
        name="to_all",
    )(piece, peaks)


def final_body(state_ref, mean_ref, std_ref, *, envs_total):
    envs, width = mean_ref.shape
    half = width // 2
    peaks = state_ref[:, 0, pl.ds(half, LANES)]
    pair = jnp.max(peaks.reshape(envs, 2, LANES), axis=1)
    peak = jnp.max(pair, axis=(0, 1), keepdims=True)
    total = jnp.sum(jnp.sum(pair, axis=0, keepdims=True), axis=1, keepdims=True)
    floor = FLOOR_SHARE * peak
    gain = 0.5 + total / (peak * envs_total)
    for env in range(envs):
        for side in range(2):
            lanes = pl.ds(side * half, half)
            line = 2 * env + side
            mean_ref[pl.ds(env, 1), lanes] = state_ref[line, 0:1, pl.ds(0, half)]
            std_ref[pl.ds(env, 1), lanes] = (
                jnp.maximum(state_ref[line, 1:2, pl.ds(0, half)], floor) * gain
            )


def finished(state, envs, width, envs_total):
    shape = jax.ShapeDtypeStruct((envs, width), jnp.float32)
    return pl.pallas_call(
        functools.partial(final_body, envs_total=envs_total),
        in_specs=[VMEM],
        out_specs=[VMEM, VMEM],
        out_shape=[shape, shape],
        name="finished",
    )(state)


def rollout_body(
    acts_ref, asq_ref, start_ref, goal_ref, win_ref, wout_ref, bin_ref, bout_ref, cost_ref, *, act_dim, chains
):
    rows, width = acts_ref.shape
    dim = start_ref.shape[1]
    steps = width // act_dim
    size = rows // chains

    def advance(state, pair, parity, goal):
        joined = jnp.concatenate([state.astype(jnp.bfloat16), pair], axis=1)
        half = jnp.dot(joined, win_ref[parity], preferred_element_type=jnp.float32) + bin_ref[...]
        hidden = (half + half * jnp.tanh(half)).astype(jnp.bfloat16)
        moved = jnp.dot(hidden, wout_ref[...], preferred_element_type=jnp.float32)
        state = jnp.tanh(state + moved + bout_ref[...])
        error = state - goal
        return state, error * error

    def two_steps(k, carry):
        lanes = pl.ds(pl.multiple_of(k * 2 * act_dim, 2 * act_dim), 2 * act_dim)
        out = []
        for chain in range(chains):
            at = pl.ds(chain * size, size)
            state, error = carry[chain]
            pair = acts_ref[at, lanes]
            goal = goal_ref[at, :]
            for parity in range(2):
                state, more = advance(state, pair, parity, goal)
                error = error + more
            out.append((state, error))
        return tuple(out)

    init = tuple(
        (start_ref[pl.ds(c * size, size), :], jnp.zeros((size, dim), jnp.float32)) for c in range(chains)
    )
    done = lax.fori_loop(0, steps // 2, two_steps, init)
    for chain in range(chains):
        at = pl.ds(chain * size, size)
        both = done[chain][1] / (dim * steps) + asq_ref[at, :] * (ACT_COST / (act_dim * steps))
        cost_ref[at, :] = jnp.broadcast_to(jnp.sum(both, axis=1, keepdims=True), (size, LANES))


def rollout(acts, asq, starts, goals, win, wout, bias_in, bias_out, act_dim, chains=2):
    rows, width = acts.shape
    return pl.pallas_call(
        functools.partial(rollout_body, act_dim=act_dim, chains=chains),
        in_specs=[VMEM] * 8,
        out_specs=VMEM,
        out_shape=jax.ShapeDtypeStruct((rows, LANES), jnp.float32),
        name="rollout",
    )(acts, asq, starts, goals, win, wout, bias_in, bias_out)


def shards(
    white,
    mean_init,
    std_init,
    init_state,
    goal_state,
    w_state,
    w_action,
    w_out,
    bias_in,
    bias_out,
    elite_idx,
):
    iters, envs, cands, flat = white.shape
    act_dim, hidden = w_action.shape
    dim = w_state.shape[0]
    length = flat // act_dim
    width = mean_init.shape[1]
    horizon = width // act_dim
    half = width // 2
    elites = elite_idx.shape[2]
    groups = lax.axis_size("env")
    peers = lax.axis_size("cand")
    lines = 2 * envs
    envs_total = envs * groups
    rows = envs * cands
    assert lines == peers and rows % 16 == 0
    band, _ = band_rows(length, act_dim)
    mine = lax.axis_index("cand")
    cand_ids = mine * cands + jnp.arange(cands, dtype=jnp.int32)
    member = jnp.sum(
        (elite_idx[:, :, :, None] == cand_ids).astype(jnp.float32), axis=2
    )
    member = jnp.broadcast_to(
        jnp.swapaxes(member, 0, 1).reshape(iters, rows, 1), (iters, rows, LANES)
    )
    starts = jnp.broadcast_to(init_state[:, None, :], (envs, cands, dim)).reshape(rows, dim)
    goals = jnp.broadcast_to(goal_state[:, None, :], (envs, cands, dim)).reshape(rows, dim)
    zeros = jnp.zeros_like(w_action)
    win = jnp.stack(
        [
            jnp.concatenate([w_state, w_action, zeros], axis=0),
            jnp.concatenate([w_state, zeros, w_action], axis=0),
        ]
    ) * jnp.bfloat16(0.5)
    half_bias = (0.5 * bias_in)[None]
    white = white.reshape(iters, rows, flat)
    noise_first = noise_of(white, 0, 1, band, act_dim, horizon)
    noise_rest = noise_of(white, 1, iters - 1, band, act_dim, horizon)
    state = jnp.stack(
        [mean_init.reshape(lines, half), std_init.reshape(lines, half)], axis=1
    )
    mine = mine[None].astype(jnp.int32)
    cost_list = []
    for it in range(iters):
        noise, at = (noise_first, 0) if it == 0 else (noise_rest, it - 1)
        acts, asq, sums, own = actions_of(
            noise, at, member[it], mine, state, it == 0, envs_total, groups, lines, half
        )
        parts = lax.all_to_all(sums, "cand", 0, 0, tiled=True)
        cost = rollout(acts, asq, starts, goals, win, w_out, half_bias, bias_out[None], act_dim)
        cost_list.append(cost[:, 0].reshape(envs, cands))
        piece, peak = refit(parts, own, elites, groups)
        peaks = lax.all_to_all(peak, "env", 0, 0, tiled=True)
        state = lax.all_to_all(to_all(piece, peaks, lines), "cand", 0, 0, tiled=True)
    mean, std = finished(state, envs, width, envs_total)
    return (mean, std, jnp.stack(cost_list))


def solution(mesh):
    in_specs = (
        P(None, "env", "cand", None),
        P("env", None),
        P("env", None),
        P("env", None),
        P("env", None),
        P(),
        P(),
        P(),
        P(),
        P(),
        P("env", None, None),
    )
    out_specs = (P("env", None), P("env", None), P(None, "env", "cand"))
    return jax.shard_map(shards, mesh=mesh, in_specs=in_specs, out_specs=out_specs, check_vma=False)
```

time: 468 us -> 240 us (0.51); the launches traced: 461 us -> 238 us
  matrix products: 198 us -> 0 us
  Pallas kernels: 0 us -> 101 us
  local copies, waits for them, and re-layouts: 115 us -> 17.3 us
  blocking collectives: 0 us -> 74.4 us
  other arithmetic: 72 us -> 2.77 us
  between operations: 22.7 us -> 0.87 us
  starting transfers between devices: 29.9 us -> 21.8 us
    dot_general x249 -> x0, matrix products: 198 us -> none  [the longest x120 168 us: advance(): jnp.dot(hidden, w_out, preferred_element_type=jnp.float32)]
    pallas_call x0 -> x15, Pallas kernels: none -> 101 us  [the longest x3 69.2 us: rollout(): pl.pallas_call(functools.partial(rollout_body, act_dim=act_dim, chains=ch...]
    all_to_all x0 -> x4, blocking collectives: none -> 74.4 us  [the longest x2 39 us: shards(): peaks = lax.all_to_all(peak, 'env', 0, 0, tiled=True)]
    slice x76 -> x4, local copies, waits for them, and re-layouts: 64.9 us -> 2.9 us  [the longest x3 2.82 us: shards(): cost_list.append(cost[:, 0].reshape(envs, cands))]
    reduce_sum x133 -> x1, other arithmetic: 31.9 us -> 0.22 us  [shards(): jnp.sum((elite_idx[:, :, :, None] == cand_ids).astype(jnp.float32), axis=2)]
    min x3 -> x0, other arithmetic: 14.1 us -> none  [shards(): jnp.clip(center[:, None, :] + spread[:, None, :] * noise, -1.0, 1.0)]
    add x70 -> x1, other arithmetic: 13.4 us -> 0.01 us  [shards(): cand_ids = mine * cands + jnp.arange(cands, dtype=jnp.int32)]
    add x6 -> x0, local copies, waits for them, and re-layouts: 12.4 us -> none  [shards(): center[:, None, :] + spread[:, None, :] * noise]
  transfers between devices with their start and end apart: 6 -> 5, of which waited for: 3 -> 3; matrix products, arithmetic and copies ran while one was open for 69% -> 3% of each run, Pallas kernels for 0% -> 32%
where the time goes in v1:
time: 240 us; the launch traced here: 238 us
  Pallas kernels  101 us (42%)
  blocking collectives  74.4 us (31%)
  starting transfers between devices  21.8 us (9%)
  waiting for transfers between devices  20.4 us (8%)
  local copies, waits for them, and re-layouts  17.3 us (7%)
  other arithmetic  2.77 us (1%)
    pallas_call x3, Pallas kernels, rollout(): pl.pallas_call(functools.partial(rollout_body, act_dim=act_dim, chains=ch...  69.2 us
    all_to_all x2, blocking collectives, shards(): peaks = lax.all_to_all(peak, 'env', 0, 0, tiled=True)  39 us
    all_to_all x2, blocking collectives, shards(): parts = lax.all_to_all(sums, 'cand', 0, 0, tiled=True)  35.5 us
    all_to_all x3, starting transfers between devices, shards(): lax.all_to_all(to_all(piece, peaks, lines), 'cand', 0, 0, tiled=True)  14.6 us
    all_to_all x3, waiting for transfers between devices, shards(): lax.all_to_all(to_all(piece, peaks, lines), 'cand', 0, 0, tiled=True)  11.6 us
    pallas_call x3, Pallas kernels, actions_of(): pl.pallas_call(functools.partial(action_body, first=first, envs_total=env...  10.6 us
    pallas_call x2, Pallas kernels, noise_of(): pl.pallas_call(functools.partial(noise_body, act_dim=act_dim, blocks=widt...  8.92 us
    all_to_all x1, waiting for transfers between devices, shards(): parts = lax.all_to_all(sums, 'cand', 0, 0, tiled=True)  8.86 us
  transfers between devices with their start and end apart: 5, of which 3 were waited for; matrix products, arithmetic and copies ran while one was open for 3% of the time, Pallas kernels for 32%

profile of v1, /device:TPU:1, one launch (start us, length us, event | category | flops | bytes accessed | tf_op | source)
XLA Modules:
  0.0 238.2 jit_solution(11029419899363251314)
XLA Ops:
  0.6 0.8 copy.19
  1.8 1.1 stack_reshape.6
  2.9 1.1 stack_reshape.7
  4.0 1.0 pad_maximum_fusion.refs_3_
  5.1 1.9 copy-done.1
  7.0 0.8 copy-done.4
  7.8 2.9 %noise.3.refs_0_ = f32[1,128,2560]{2,1,0:T(8,128)S(1)} custom-call(bf16[3,128,4096]{2,1,0:T(8,128)(2,1)S(1)} %bitcast.13, f32[64,256]{1,0:T(8,128)S(1)} %copy-done.4), custom_call_target="tpu_custom_call" | custom-call | tf_op jit(solution)/shard_map/noise/pallas_call | solution.py:60
  10.7 1.1 copy-done.3
  11.8 0.7 broadcast_in_dim.49.refs_1_
  12.5 3.5 %actions.3 = (bf16[128,2560]{1,0:T(8,128)(2,1)}, f32[128,128]{1,0:T(8,128)}, f32[32,2,1280]{2,1,0:T(2,128)}, f32[2,1280]{1,0:T(2,128)}) custom-call(f32[1,128,2560]{2,1,0:T(8,128)} %copy-done.3, f32[128,128]{1,0:T(8,128)} %broadcast_in_dim.49.refs_1_, s32[1]{0:T(128)} %bitcast.2.refs_2_, f32[32,2,1280]{2,1,0:T(2,128)} %pad_maximum_fusion.refs_3_), custom_call_target="tpu_custom_call" | custom-call | tf_op jit(solution)/shard_map/actions/pallas_call | solution.py:120
  16.0 20.7 %all_to_all.45.parts_ref = f32[32,2,1280]{2,1,0:T(2,128)} all-to-all(f32[32,2,1280]{2,1,0:T(2,128)} %get-tuple-element.23), channel_id=1, replica_groups=mesh['env'=16,'cand'=32] {'cand'}, dimensions={0} | all-to-all | bytes 655360 | tf_op jit(solution)/shard_map/all_to_all | solution.py:327
  36.6 1.8 refit.3
  38.5 23.8 %all_to_all.46.peak_ref = f32[16,1,128]{2,1,0:T(1,128)} all-to-all(f32[16,1,128]{2,1,0:T(1,128)} %get-tuple-element.26), channel_id=1, replica_groups=mesh['env'=16,'cand'=32] {'env'}, dimensions={0} | all-to-all | bytes 16384 | tf_op jit(solution)/shard_map/all_to_all | solution.py:331
  62.3 1.5 to_all.3
  63.8 5.6 %all-to-all-start.2 = ((f32[32,2,1408]{2,1,0:T(2,128)}), f32[32,2,1408]{2,1,0:T(2,128)}, u32[]{:S(2)}, u32[]{:S(2)}) async-start(f32[32,2,1408]{2,1,0:T(2,128)} %to_all.3), calls=%async_computation.2 | async-start | bytes 720896 | tf_op jit(solution)/shard_map/all_to_all | solution.py:332
  69.4 6.1 %noise.2.refs_0_ = f32[2,128,2560]{2,1,0:T(8,128)S(1)} custom-call(bf16[3,128,4096]{2,1,0:T(8,128)(2,1)S(1)} %bitcast.14, f32[64,256]{1,0:T(8,128)S(1)} %copy-done.5), custom_call_target="tpu_custom_call" | custom-call | tf_op jit(solution)/shard_map/noise/pallas_call | solution.py:60
  75.5 1.5 copy-done
  77.1 2.3 all-to-all-done.2.refs_3_
  79.4 0.7 broadcast_in_dim.47.refs_1_
  80.1 3.6 %actions.4 = (bf16[128,2560]{1,0:T(8,128)(2,1)}, f32[128,128]{1,0:T(8,128)}, f32[32,2,1280]{2,1,0:T(2,128)}, f32[2,1280]{1,0:T(2,128)}) custom-call(f32[2,128,2560]{2,1,0:T(8,128)} %copy-done, f32[128,128]{1,0:T(8,128)} %broadcast_in_dim.47.refs_1_, s32[1]{0:T(128)} %bitcast.2.refs_2_, f32[32,2,1408]{2,1,0:T(2,128)} %all-to-all-done.2.refs_3_), custom_call_target="tpu_custom_call" | custom-call | tf_op jit(solution)/shard_map/actions/pallas_call | solution.py:120
  83.7 14.8 %all_to_all.47.parts_ref = f32[32,2,1280]{2,1,0:T(2,128)} all-to-all(f32[32,2,1280]{2,1,0:T(2,128)} %get-tuple-element.27), channel_id=1, replica_groups=mesh['env'=16,'cand'=32] {'cand'}, dimensions={0} | all-to-all | bytes 655360 | tf_op jit(solution)/shard_map/all_to_all | solution.py:327
  98.5 1.9 refit.4
  100.4 15.2 %all_to_all.48.peak_ref = f32[16,1,128]{2,1,0:T(1,128)} all-to-all(f32[16,1,128]{2,1,0:T(1,128)} %get-tuple-element.30), channel_id=1, replica_groups=mesh['env'=16,'cand'=32] {'env'}, dimensions={0} | all-to-all | bytes 16384 | tf_op jit(solution)/shard_map/all_to_all | solution.py:331
  115.5 1.5 to_all.4
  117.0 5.2 %all-to-all-start.5 = ((f32[32,2,1408]{2,1,0:T(2,128)}), f32[32,2,1408]{2,1,0:T(2,128)S(1)}, u32[]{:S(2)}, u32[]{:S(2)}) async-start(f32[32,2,1408]{2,1,0:T(2,128)} %to_all.4), calls=%async_computation.5 | async-start | bytes 720896 | tf_op jit(solution)/shard_map/all_to_all | solution.py:332
  122.3 0.6 broadcast_multiply_fusion
  122.9 9.2 %all-to-all-done.5.refs_3_ = f32[32,2,1408]{2,1,0:T(2,128)S(1)} async-done(((f32[32,2,1408]{2,1,0:T(2,128)}), f32[32,2,1408]{2,1,0:T(2,128)S(1)}, u32[]{:S(2)}, u32[]{:S(2)}) %all-to-all-start.5) | async-done | bytes 360480 | tf_op jit(solution)/shard_map/all_to_all | solution.py:332
  132.2 0.7 broadcast_in_dim.44.refs_1_
  132.9 3.5 %actions.5 = (bf16[128,2560]{1,0:T(8,128)(2,1)}, f32[128,128]{1,0:T(8,128)}, f32[32,2,1280]{2,1,0:T(2,128)}, f32[2,1280]{1,0:T(2,128)}) custom-call(f32[2,128,2560]{2,1,0:T(8,128)} %copy-done, f32[128,128]{1,0:T(8,128)} %broadcast_in_dim.44.refs_1_, s32[1]{0:T(128)} %bitcast.2.refs_2_, f32[32,2,1408]{2,1,0:T(2,128)} %copy-done.6), custom_call_target="tpu_custom_call" | custom-call | tf_op jit(solution)/shard_map/actions/pallas_call | solution.py:120
  136.5 3.8 %all-to-all-start.6 = ((f32[32,2,1280]{2,1,0:T(2,128)}), f32[32,2,1280]{2,1,0:T(2,128)S(1)}, u32[]{:S(2)}, u32[]{:S(2)}) async-start(f32[32,2,1280]{2,1,0:T(2,128)} %get-tuple-element.31), calls=%async_computation.6 | async-start | bytes 655360 | tf_op jit(solution)/shard_map/all_to_all | solution.py:327
  140.4 0.7 broadcast_bitcast_fusion
  141.0 8.9 %all-to-all-done.6.parts_ref = f32[32,2,1280]{2,1,0:T(2,128)S(1)} async-done(((f32[32,2,1280]{2,1,0:T(2,128)}), f32[32,2,1280]{2,1,0:T(2,128)S(1)}, u32[]{:S(2)}, u32[]{:S(2)}) %all-to-all-start.6) | async-done | bytes 327712 | tf_op jit(solution)/shard_map/all_to_all | solution.py:327
  149.9 0.7 copy-done.8
  150.6 1.8 refit.5
  152.4 3.4 %all-to-all-start.7 = ((f32[16,1,128]{2,1,0:T(1,128)}), f32[16,1,128]{2,1,0:T(1,128)S(1)}, u32[]{:S(2)}, u32[]{:S(2)}) async-start(f32[16,1,128]{2,1,0:T(1,128)} %get-tuple-element.34), calls=%async_computation.7 | async-start | bytes 16384 | tf_op jit(solution)/shard_map/all_to_all | solution.py:331
  155.9 0.9 maximum_multiply_fusion.win_ref
  156.7 23.1 %rollout.3 = f32[128,128]{1,0:T(8,128)} custom-call(bf16[128,2560]{1,0:T(8,128)(2,1)} %get-tuple-element.37.acts_ref, f32[128,128]{1,0:T(8,128)} %get-tuple-element.38.asq_ref, f32[128,128]{1,0:T(8,128)} %get-tuple-element.58.start_ref, f32[128,128]{1,0:T(8,128)} %get-tuple-element.57.goal_ref, bf16[2,256,512]{2,1,0:T(8,128)(2,1)} %maximum_multiply_fusion.win_ref, ...), custom_call_target="tpu_custom_call" | custom-call | tf_op jit(solution)/shard_map/rollout/pallas_call | solution.py:259
  179.8 0.6 copy-done.11
  180.4 1.5 to_all.5
  181.9 3.7 %all-to-all-start.8 = ((f32[32,2,1408]{2,1,0:T(2,128)}), f32[32,2,1408]{2,1,0:T(2,128)S(1)}, u32[]{:S(2)}, u32[]{:S(2)}) async-start(f32[32,2,1408]{2,1,0:T(2,128)} %to_all.5), calls=%async_computation.8 | async-start | bytes 720896 | tf_op jit(solution)/shard_map/all_to_all | solution.py:332
  185.6 0.9 slice_reduce_fusion.2
  186.6 23.1 %rollout.4 = f32[128,128]{1,0:T(8,128)} custom-call(bf16[128,2560]{1,0:T(8,128)(2,1)} %get-tuple-element.39.acts_ref, f32[128,128]{1,0:T(8,128)} %get-tuple-element.40.asq_ref, f32[128,128]{1,0:T(8,128)} %get-tuple-element.58.start_ref, f32[128,128]{1,0:T(8,128)} %get-tuple-element.57.goal_ref, bf16[2,256,512]{2,1,0:T(8,128)(2,1)} %maximum_multiply_fusion.win_ref, ...), custom_call_target="tpu_custom_call" | custom-call | tf_op jit(solution)/shard_map/rollout/pallas_call | solution.py:259
  209.7 0.9 slice_reduce_fusion.1
  210.8 23.1 %rollout.5 = f32[128,128]{1,0:T(8,128)} custom-call(bf16[128,2560]{1,0:T(8,128)(2,1)} %get-tuple-element.41.acts_ref, f32[128,128]{1,0:T(8,128)} %get-tuple-element.42.asq_ref, f32[128,128]{1,0:T(8,128)} %get-tuple-element.58.start_ref, f32[128,128]{1,0:T(8,128)} %get-tuple-element.57.goal_ref, bf16[2,256,512]{2,1,0:T(8,128)(2,1)} %maximum_multiply_fusion.win_ref, ...), custom_call_target="tpu_custom_call" | custom-call | tf_op jit(solution)/shard_map/rollout/pallas_call | solution.py:259
  233.9 0.9 slice_reduce_fusion
  234.9 0.7 copy.20
  235.6 0.7 copy-done.7
  236.3 1.8 finished.1
  (37 shorter events, 0.9 us)
Async XLA Ops:
  5.1 1.9 copy-start.1
  7.0 0.8 copy-start.4
  10.7 1.1 copy-start.3
  11.7 57.7 %copy-start.2 = (bf16[3,16,8,4096]{3,2,1,0:T(8,128)(2,1)S(1)}, bf16[3,16,8,4096]{3,2,1,0:T(8,128)(2,1)}, u32[]{:S(2)}) copy-start(bf16[3,16,8,4096]{3,2,1,0:T(8,128)(2,1)} %param.12) | copy-start | bytes 9437188
  11.8 57.7 %copy-start.5 = (f32[64,256]{1,0:T(8,128)S(1)}, f32[64,256]{1,0:T(8,128)}, u32[]{:S(2)}) copy-start(f32[64,256]{1,0:T(8,128)} %constant.16.clone.band_ref) | copy-start | bytes 196612
  63.8 15.7 %all-to-all-start.2 = ((f32[32,2,1408]{2,1,0:T(2,128)}), f32[32,2,1408]{2,1,0:T(2,128)}, u32[]{:S(2)}, u32[]{:S(2)}) async-start(f32[32,2,1408]{2,1,0:T(2,128)} %to_all.3), calls=%async_computation.2 | async-start | bytes 720896 | tf_op jit(solution)/shard_map/all_to_all | solution.py:332
  75.5 1.5 copy-start
  77.1 45.2 %copy-start.14 = (f32[512]{0:T(512)S(1)}, f32[512]{0:T(512)}, u32[]{:S(2)}) copy-start(f32[512]{0:T(512)} %param.20) | copy-start | bytes 6148
  98.5 41.8 %copy-start.9 = (bf16[128,512]{1,0:T(8,128)(2,1)S(1)}, bf16[128,512]{1,0:T(8,128)(2,1)}, u32[]{:S(2)}) copy-start(bf16[128,512]{1,0:T(8,128)(2,1)} %param.17) | copy-start | bytes 393220
  98.5 41.8 %copy-start.10 = (bf16[64,512]{1,0:T(8,128)(2,1)S(1)}, bf16[64,512]{1,0:T(8,128)(2,1)}, u32[]{:S(2)}) copy-start(bf16[64,512]{1,0:T(8,128)(2,1)} %param.18) | copy-start | bytes 196612
  117.0 23.3 %copy-start.12 = (f32[16,128]{1,0:T(8,128)S(1)}, f32[16,128]{1,0:T(8,128)}, u32[]{:S(2)}) copy-start(f32[16,128]{1,0:T(8,128)} %param.16) | copy-start | bytes 24580
  117.0 23.3 %copy-start.13 = (f32[16,128]{1,0:T(8,128)S(1)}, f32[16,128]{1,0:T(8,128)}, u32[]{:S(2)}) copy-start(f32[16,128]{1,0:T(8,128)} %param.15) | copy-start | bytes 24580
  117.0 15.2 %all-to-all-start.5 = ((f32[32,2,1408]{2,1,0:T(2,128)}), f32[32,2,1408]{2,1,0:T(2,128)S(1)}, u32[]{:S(2)}, u32[]{:S(2)}) async-start(f32[32,2,1408]{2,1,0:T(2,128)} %to_all.4), calls=%async_computation.5 | async-start | bytes 720896 | tf_op jit(solution)/shard_map/all_to_all | solution.py:332
  132.2 0.8 copy-start.6
  136.5 13.4 %all-to-all-start.6 = ((f32[32,2,1280]{2,1,0:T(2,128)}), f32[32,2,1280]{2,1,0:T(2,128)S(1)}, u32[]{:S(2)}, u32[]{:S(2)}) async-start(f32[32,2,1280]{2,1,0:T(2,128)} %get-tuple-element.31), calls=%async_computation.6 | async-start | bytes 655360 | tf_op jit(solution)/shard_map/all_to_all | solution.py:327
  149.9 0.7 copy-start.8
  152.4 27.4 %all-to-all-start.7 = ((f32[16,1,128]{2,1,0:T(1,128)}), f32[16,1,128]{2,1,0:T(1,128)S(1)}, u32[]{:S(2)}, u32[]{:S(2)}) async-start(f32[16,1,128]{2,1,0:T(1,128)} %get-tuple-element.34), calls=%async_computation.7 | async-start | bytes 16384 | tf_op jit(solution)/shard_map/all_to_all | solution.py:331
  179.8 0.6 copy-start.11
  181.9 53.7 %all-to-all-start.8 = ((f32[32,2,1408]{2,1,0:T(2,128)}), f32[32,2,1408]{2,1,0:T(2,128)S(1)}, u32[]{:S(2)}, u32[]{:S(2)}) async-start(f32[32,2,1408]{2,1,0:T(2,128)} %to_all.5), calls=%async_computation.8 | async-start | bytes 720896 | tf_op jit(solution)/shard_map/all_to_all | solution.py:332
  235.6 0.7 copy-start.7

commit v2 on v1

v2 whole, which is shorter than its diff:
```python
import functools

import jax
import jax.numpy as jnp
import numpy as np
from jax import lax
from jax.experimental import pallas as pl
from jax.experimental.pallas import tpu as pltpu
from jax.sharding import PartitionSpec as P

BETA_EXP = 2.5
MOMENTUM = 0.1
FLOOR_SHARE = 0.1
ACT_COST = 0.1
LANES = 128
ROLL_FLOPS = 1 << 28
VMEM = pl.BlockSpec(memory_space=pltpu.VMEM)
SMEM = pl.BlockSpec(memory_space=pltpu.SMEM)
ANY = pl.BlockSpec(memory_space=pl.ANY)


def color_kernel(length):
    freqs = np.arange(length // 2 + 1)
    scale = (np.maximum(freqs, 1).astype(np.float32) / np.float32(length)) ** np.float32(-BETA_EXP / 2)
    kernel = np.fft.irfft(scale.astype(np.float64), n=length)
    kernel = kernel / np.sqrt(np.sum(kernel * kernel))
    return np.asarray(kernel, np.float32).astype(jnp.bfloat16).astype(np.float32)


def band_rows(length, act_dim):
    per = 256 // act_dim
    kernel = color_kernel(length)
    rows = np.arange(length)[:, None]
    quarter = np.arange(256)[None, :] // act_dim
    return jnp.asarray(kernel[(quarter - rows) % length], jnp.float32), per


def noise_body(white_ref, band_ref, tie_ref, out_ref, fill, *, act_dim, blocks):
    length = band_ref.shape[0]
    flat = length * act_dim

    @pl.when(pl.program_id(0) == 0)
    def _():
        row = lax.broadcasted_iota(jnp.int32, (act_dim, 256), 0)
        lane = lax.broadcasted_iota(jnp.int32, (act_dim, 256), 1)
        hit = lane % act_dim == row
        for j in range(length):
            tile = jnp.where(hit, band_ref[pl.ds(j, 1), :], 0.0).astype(jnp.bfloat16)
            fill[pl.ds(j * act_dim, act_dim), :] = tile
            fill[pl.ds(flat + j * act_dim, act_dim), :] = tile

    for block in range(blocks):
        start = (flat - block * 256) % flat
        out_ref[0, :, pl.ds(block * 256, 256)] = jnp.dot(
            white_ref[0], fill[pl.ds(start, flat), :], preferred_element_type=jnp.float32
        )


def noise_of(white, first, count, band, tie, act_dim, horizon):
    _, rows, flat = white.shape
    width = horizon * act_dim
    return pl.pallas_call(
        functools.partial(noise_body, act_dim=act_dim, blocks=width // 256),
        grid=(count,),
        in_specs=[
            pl.BlockSpec((1, rows, flat), lambda i: (i + first, 0, 0)),
            pl.BlockSpec(band.shape, lambda i: (0, 0)),
            ANY,
        ],
        out_specs=pl.BlockSpec((1, rows, width), lambda i: (i, 0, 0)),
        out_shape=jax.ShapeDtypeStruct((count, rows, width), jnp.float32),
        scratch_shapes=[pltpu.VMEM((2 * flat, 256), jnp.bfloat16)],
        compiler_params=pltpu.CompilerParams(vmem_limit_bytes=16 << 20),
        name="noise",
    )(white, band, tie)


def stats_of(state_ref, envs, half, envs_total):
    peaks = state_ref[:, 0, pl.ds(half, LANES)]
    pair = jnp.max(peaks.reshape(envs, 2, LANES), axis=1)
    peak = jnp.max(pair, axis=(0, 1), keepdims=True)
    total = jnp.sum(jnp.sum(pair, axis=0, keepdims=True), axis=1, keepdims=True)
    return FLOOR_SHARE * peak, 0.5 + total / (peak * envs_total)


def action_body(*refs, it, envs_total):
    first = it == 0
    if first:
        noise_ref, elite_ref, mine_ref, mean_ref, std_ref, acts_ref, asq_ref, sums_ref, own_ref = refs
    else:
        noise_ref, elite_ref, mine_ref, state_ref, acts_ref, asq_ref, sums_ref, own_ref = refs
    half = sums_ref.shape[2]
    rows = acts_ref.shape[0]
    envs = sums_ref.shape[0] // 2
    cands = rows // envs
    me = mine_ref[0]
    if first:
        lanes = pl.ds(pl.multiple_of((me % 2) * half, LANES), half)
        own_ref[0:1, :] = mean_ref[pl.ds(me // 2, 1), lanes]
        own_ref[1:2, :] = std_ref[pl.ds(me // 2, 1), lanes]
    else:
        floor, gain = stats_of(state_ref, envs, half, envs_total)
        own = state_ref[me, :, pl.ds(0, half)]
        own_ref[0:1, :] = own[0:1]
        own_ref[1:2, :] = jnp.maximum(own[1:2], floor) * gain
    ids = me * cands + lax.broadcasted_iota(jnp.int32, (cands, 1), 0)
    for env in range(envs):
        at = pl.ds(env * cands, cands)
        chosen = elite_ref[env, it : it + 1, :] == ids
        member = jnp.sum(jnp.where(chosen, 1.0, 0.0), axis=1, keepdims=True)
        member = jnp.broadcast_to(member, (cands, LANES))
        square = jnp.zeros((cands, LANES), jnp.float32)
        for side in range(2):
            line = 2 * env + side
            for step in range(half // LANES):
                lanes = pl.ds(step * LANES, LANES)
                whole = pl.ds(side * half + step * LANES, LANES)
                if first:
                    center = mean_ref[pl.ds(env, 1), whole]
                    spread = std_ref[pl.ds(env, 1), whole]
                else:
                    center = state_ref[line, 0:1, lanes]
                    spread = jnp.maximum(state_ref[line, 1:2, lanes], floor) * gain
                action = jnp.clip(center + spread * noise_ref[0, at, whole], -1.0, 1.0)
                acts_ref[at, whole] = action.astype(jnp.bfloat16)
                both = action * action
                square = square + both
                sums_ref[line, 0:1, lanes] = jnp.sum(action * member, axis=0, keepdims=True)
                sums_ref[line, 1:2, lanes] = jnp.sum(both * member, axis=0, keepdims=True)
        asq_ref[at, :] = square


def actions_of(noise, at, elite_idx, mine, state, it, envs_total, lines, half):
    _, rows, width = noise.shape
    return pl.pallas_call(
        functools.partial(action_body, it=it, envs_total=envs_total),
        grid=(1,),
        in_specs=[pl.BlockSpec((1, rows, width), lambda i: (at, 0, 0)), VMEM, SMEM] + [VMEM] * len(state),
        out_specs=[VMEM, VMEM, VMEM, VMEM],
        out_shape=[
            jax.ShapeDtypeStruct((rows, width), jnp.bfloat16),
            jax.ShapeDtypeStruct((rows, LANES), jnp.float32),
            jax.ShapeDtypeStruct((lines, 2, half), jnp.float32),
            jax.ShapeDtypeStruct((2, half), jnp.float32),
        ],
        compiler_params=pltpu.CompilerParams(vmem_limit_bytes=12 << 20),
        name="actions",
    )(noise, elite_idx, mine, *state)


def refit_body(parts_ref, own_ref, tie_ref, slice_ref, peak_ref, *, elites):
    total = jnp.sum(parts_ref[...], axis=0)
    mean = total[0:1] / elites
    variance = jnp.maximum(total[1:2] / elites - mean * mean, 0.0)
    slice_ref[0:1, :] = MOMENTUM * own_ref[0:1, :] + (1.0 - MOMENTUM) * mean
    mixed = MOMENTUM * own_ref[1:2, :] + (1.0 - MOMENTUM) * jnp.sqrt(variance)
    slice_ref[1:2, :] = mixed
    peak_ref[...] = jnp.broadcast_to(jnp.max(mixed, axis=1, keepdims=True)[None], peak_ref.shape)


def refit(parts, own, tie, elites, groups):
    return pl.pallas_call(
        functools.partial(refit_body, elites=elites),
        in_specs=[VMEM, VMEM, ANY],
        out_specs=[VMEM, VMEM],
        out_shape=[
            jax.ShapeDtypeStruct(own.shape, jnp.float32),
            jax.ShapeDtypeStruct((groups, 1, LANES), jnp.float32),
        ],
        compiler_params=pltpu.CompilerParams(vmem_limit_bytes=4 << 20),
        name="refit",
    )(parts, own, tie)


def spread_body(slice_ref, peak_ref, tie_ref, out_ref):
    lines = out_ref.shape[0]
    half = slice_ref.shape[1]
    lane = lax.broadcasted_iota(jnp.int32, (1, LANES), 1)
    tail = jnp.zeros((1, LANES), jnp.float32)
    for group in range(peak_ref.shape[0]):
        tail = jnp.where(lane == group, peak_ref[group], tail)
    main = jnp.broadcast_to(slice_ref[...][None], (lines, 2, half))
    out_ref[:, :, pl.ds(0, half)] = main
    out_ref[:, :, pl.ds(half, LANES)] = jnp.broadcast_to(tail[None], (lines, 2, LANES))


def to_all(piece, peaks, tie, lines):
    half = piece.shape[1]
    return pl.pallas_call(
        spread_body,
        in_specs=[VMEM, VMEM, ANY],
        out_specs=VMEM,
        out_shape=jax.ShapeDtypeStruct((lines, 2, half + LANES), jnp.float32),
        compiler_params=pltpu.CompilerParams(vmem_limit_bytes=4 << 20),
        name="to_all",
    )(piece, peaks, tie)


def final_body(state_ref, mean_ref, std_ref, *, envs_total):
    envs, width = mean_ref.shape
    half = width // 2
    floor, gain = stats_of(state_ref, envs, half, envs_total)
    for env in range(envs):
        for side in range(2):
            lanes = pl.ds(side * half, half)
            line = 2 * env + side
            mean_ref[pl.ds(env, 1), lanes] = state_ref[line, 0:1, pl.ds(0, half)]
            std_ref[pl.ds(env, 1), lanes] = (
                jnp.maximum(state_ref[line, 1:2, pl.ds(0, half)], floor) * gain
            )


def finished(state, envs, width, envs_total):
    shape = jax.ShapeDtypeStruct((envs, width), jnp.float32)
    return pl.pallas_call(
        functools.partial(final_body, envs_total=envs_total),
        in_specs=[VMEM],
        out_specs=[VMEM, VMEM],
        out_shape=[shape, shape],
        compiler_params=pltpu.CompilerParams(vmem_limit_bytes=4 << 20),
        name="finished",
    )(state)


def rollout_body(*refs, act_dim, earlier):
    (acts_ref, asq_ref, begin_ref, goal_ref, ws_ref, wa_ref, wout_ref, bin_ref, bout_ref) = refs[:9]
    before = refs[9 : 9 + earlier]
    cost_ref, win, start, goal = refs[10 + earlier :]
    rows, width = acts_ref.shape
    envs, dim = begin_ref.shape
    cands = rows // envs
    steps = width // act_dim
    zeros = jnp.zeros(wa_ref.shape, jnp.bfloat16)
    for parity in range(2):
        win[parity, pl.ds(0, dim), :] = ws_ref[...] * jnp.bfloat16(0.5)
        win[parity, pl.ds(dim + parity * act_dim, act_dim), :] = wa_ref[...] * jnp.bfloat16(0.5)
        win[parity, pl.ds(dim + (1 - parity) * act_dim, act_dim), :] = zeros
    for env in range(envs):
        at = pl.ds(env * cands, cands)
        start[at, :] = jnp.broadcast_to(begin_ref[pl.ds(env, 1), :], (cands, dim))
        goal[at, :] = jnp.broadcast_to(goal_ref[pl.ds(env, 1), :], (cands, dim))
    bias_in = bin_ref[...] * 0.5

    def two_steps(k, carry):
        state, error = carry
        pair = acts_ref[:, pl.ds(pl.multiple_of(k * 2 * act_dim, 2 * act_dim), 2 * act_dim)]
        for parity in range(2):
            joined = jnp.concatenate([state.astype(jnp.bfloat16), pair], axis=1)
            half = jnp.dot(joined, win[parity], preferred_element_type=jnp.float32) + bias_in
            hidden = (half + half * jnp.tanh(half)).astype(jnp.bfloat16)
            moved = jnp.dot(hidden, wout_ref[...], preferred_element_type=jnp.float32)
            state = jnp.tanh(state + moved + bout_ref[...])
            gap = state - goal[...]
            error = error + gap * gap
        return state, error

    _, error = lax.fori_loop(0, steps // 2, two_steps, (start[...], jnp.zeros((rows, dim), jnp.float32)))
    both = error / (dim * steps) + asq_ref[...] * (ACT_COST / (act_dim * steps))
    cost = jnp.broadcast_to(jnp.sum(both, axis=1, keepdims=True), (rows, LANES))
    lane = lax.broadcasted_iota(jnp.int32, (cands, LANES), 1)
    table = jnp.zeros((cands, LANES), jnp.float32)
    for env in range(envs):
        table = jnp.where(lane == env, cost[env * cands : (env + 1) * cands], table)
    for k in range(earlier):
        cost_ref[k] = before[k][...]
    cost_ref[earlier] = table[:, :envs]


def rollout(acts, asq, fixed, before, tie, act_dim):
    rows, width = acts.shape
    envs, dim = fixed[0].shape
    cands = rows // envs
    earlier = len(before)
    return pl.pallas_call(
        functools.partial(rollout_body, act_dim=act_dim, earlier=earlier),
        in_specs=[VMEM] * (9 + earlier) + [ANY],
        out_specs=VMEM,
        out_shape=jax.ShapeDtypeStruct((1 + earlier, cands, envs), jnp.float32),
        scratch_shapes=[
            pltpu.VMEM((2, dim + 2 * act_dim, fixed[2].shape[1]), jnp.bfloat16),
            pltpu.VMEM((rows, dim), jnp.float32),
            pltpu.VMEM((rows, dim), jnp.float32),
        ],
        cost_estimate=pl.CostEstimate(
            flops=ROLL_FLOPS, bytes_accessed=2 * rows * width, transcendentals=0
        ),
        compiler_params=pltpu.CompilerParams(vmem_limit_bytes=8 << 20),
        name="rollout",
    )(acts, asq, *fixed, *before, tie)


def shards(
    white,
    mean_init,
    std_init,
    init_state,
    goal_state,
    w_state,
    w_action,
    w_out,
    bias_in,
    bias_out,
    elite_idx,
):
    iters, envs, cands, flat = white.shape
    act_dim = w_action.shape[0]
    length = flat // act_dim
    width = mean_init.shape[1]
    horizon = width // act_dim
    half = width // 2
    elites = elite_idx.shape[2]
    groups = lax.axis_size("env")
    peers = lax.axis_size("cand")
    lines = 2 * envs
    envs_total = envs * groups
    rows = envs * cands
    assert lines == peers and rows % 16 == 0
    band, _ = band_rows(length, act_dim)
    mine = lax.axis_index("cand").astype(jnp.int32)[None]
    fixed = (init_state, goal_state, w_state, w_action, w_out, bias_in[None], bias_out[None])
    white = white.reshape(iters, rows, flat)
    noise = noise_of(white, 0, 1, band, mean_init, act_dim, horizon)
    state = (mean_init, std_init)
    costs = []
    for it in range(iters):
        at = max(it - 1, 0)
        acts, asq, sums, own = actions_of(noise, at, elite_idx, mine, state, it, envs_total, lines, half)
        parts = lax.all_to_all(sums, "cand", 0, 0, tiled=True)
        if it == 0:
            noise = noise_of(white, 1, iters - 1, band, own, act_dim, horizon)
        piece, peak = refit(parts, own, noise, elites, groups)
        peaks = lax.all_to_all(peak, "env", 0, 0, tiled=True)
        last = it == iters - 1
        costs.append(rollout(acts, asq, fixed, costs if last else [], peak, act_dim))
        if not last:
            costs[-1] = costs[-1][0]
        state = (
            lax.all_to_all(to_all(piece, peaks, costs[-1], lines), "cand", 0, 0, tiled=True),
        )
    mean, std = finished(state[0], envs, width, envs_total)
    return (mean, std, jnp.swapaxes(costs[-1], 1, 2))


def solution(mesh):
    in_specs = (
        P(None, "env", "cand", None),
        P("env", None),
        P("env", None),
        P("env", None),
        P("env", None),
        P(),
        P(),
        P(),
        P(),
        P(),
        P("env", None, None),
    )
    out_specs = (P("env", None), P("env", None), P(None, "env", "cand"))
    return jax.shard_map(shards, mesh=mesh, in_specs=in_specs, out_specs=out_specs, check_vma=False)
```

time: 240 us -> 186 us (0.78)
  Pallas kernels: 101 us -> 55 us
  starting transfers between devices: 21.8 us -> 46.9 us
  waiting for transfers between devices: 20.4 us -> 1.6 us
  local copies, waits for them, and re-layouts: 17.3 us -> 11.1 us
  blocking collectives: 74.4 us -> 69.1 us
  other arithmetic: 2.77 us -> 0 us
    pallas_call x9, Pallas kernels: 84.3 us -> 42.6 us  [the longest x3 38.6 us: rollout(): pl.pallas_call(functools.partial(rollout_body, act_dim=act_dim, earlier=e...]
    all_to_all x1 -> x3, starting transfers between devices: 3.42 us -> 36.5 us  [shards(): peaks = lax.all_to_all(peak, 'env', 0, 0, tiled=True)]
    all_to_all x3 -> x0, starting transfers between devices: 14.6 us -> none  [shards(): lax.all_to_all(to_all(piece, peaks, lines), 'cand', 0, 0, tiled=True)]
    all_to_all x3 -> x0, waiting for transfers between devices: 11.6 us -> none  [shards(): lax.all_to_all(to_all(piece, peaks, lines), 'cand', 0, 0, tiled=True)]
    all_to_all x2, blocking collectives: 35.5 us -> 26 us  [shards(): parts = lax.all_to_all(sums, 'cand', 0, 0, tiled=True)]
    all_to_all x1, waiting for transfers between devices: 8.86 us -> 1.59 us  [shards(): parts = lax.all_to_all(sums, 'cand', 0, 0, tiled=True)]
    all_to_all x1, starting transfers between devices: 3.77 us -> 10.4 us  [shards(): parts = lax.all_to_all(sums, 'cand', 0, 0, tiled=True)]
    all_to_all x2 -> x3, blocking collectives: 39 us -> 43.1 us  [shards(): lax.all_to_all(to_all(piece, peaks, costs[-1], lines), 'cand', 0, 0, tile...]
  transfers between devices with their start and end apart: 5 -> 4, of which waited for: 3 -> 1; matrix products, arithmetic and copies ran while one was open for 3% -> 0% of each run, Pallas kernels for 32% -> 24%
where the time goes in v2:
time: 186 us; the launch traced here: 185 us
  blocking collectives  69.1 us (37%)
  Pallas kernels  55 us (30%)
  starting transfers between devices  46.9 us (25%)
  local copies, waits for them, and re-layouts  11.1 us (6%)
    all_to_all x3, blocking collectives, shards(): lax.all_to_all(to_all(piece, peaks, costs[-1], lines), 'cand', 0, 0, tile...  43.1 us
    pallas_call x3, Pallas kernels, rollout(): pl.pallas_call(functools.partial(rollout_body, act_dim=act_dim, earlier=e...  38.6 us
    all_to_all x3, starting transfers between devices, shards(): peaks = lax.all_to_all(peak, 'env', 0, 0, tiled=True)  36.5 us
    all_to_all x2, blocking collectives, shards(): parts = lax.all_to_all(sums, 'cand', 0, 0, tiled=True)  26 us
    unnamed x41, local copies, waits for them, and re-layouts  11.1 us
    all_to_all x1, starting transfers between devices, shards(): parts = lax.all_to_all(sums, 'cand', 0, 0, tiled=True)  10.4 us
    pallas_call x2, Pallas kernels, noise_of(): pl.pallas_call(functools.partial(noise_body, act_dim=act_dim, blocks=widt...  8.9 us
    pallas_call x3, Pallas kernels, actions_of(): pl.pallas_call(functools.partial(action_body, it=it, envs_total=envs_tota...  3.91 us
  transfers between devices with their start and end apart: 4, of which 1 were waited for; matrix products, arithmetic and copies ran while one was open for 0% of the time, Pallas kernels for 24%

profile of v2, /device:TPU:1, one launch (start us, length us, event | category | flops | bytes accessed | tf_op | source)
XLA Modules:
  0.0 184.6 jit_solution(8827557243674331595)
XLA Ops:
  0.6 0.8 copy.15.refs_1_
  1.4 0.0 copy-start
  1.4 1.9 %copy-done = bf16[3,16,8,4096]{3,2,1,0:T(8,128)(2,1)S(1)} copy-done((bf16[3,16,8,4096]{3,2,1,0:T(8,128)(2,1)S(1)}, bf16[3,16,8,4096]{3,2,1,0:T(8,128)(2,1)}, u32[]{:S(2)}) %copy-start) | copy-done | bytes 3145752
  3.3 0.9 copy-done.4
  4.2 0.8 copy-done.12
  5.0 2.9 %noise.2.refs_0_ = f32[1,128,2560]{2,1,0:T(8,128)S(1)} custom-call(bf16[3,128,4096]{2,1,0:T(8,128)(2,1)S(1)} %bitcast.7, f32[64,256]{1,0:T(8,128)S(1)} %copy-done.12, f32[16,2560]{1,0:T(8,128)S(1)} %copy-done.4), custom_call_target="tpu_custom_call" | custom-call | tf_op jit(solution)/shard_map/noise/pallas_call | solution.py:62
  7.9 0.0 copy-done.14
  7.9 1.6 actions.3
  9.6 0.8 copy-done.5
  10.4 10.4 %all-to-all-start = ((f32[32,2,1280]{2,1,0:T(2,128)}), f32[32,2,1280]{2,1,0:T(2,128)S(1)}, u32[]{:S(2)}, u32[]{:S(2)}) async-start(f32[32,2,1280]{2,1,0:T(2,128)} %get-tuple-element.24), calls=%async_computation | async-start | bytes 655360 | tf_op jit(solution)/shard_map/all_to_all | solution.py:328
  20.8 0.0 copy-start.1
  20.8 1.9 %copy-done.1 = bf16[3,16,8,4096]{3,2,1,0:T(8,128)(2,1)S(1)} copy-done((bf16[3,16,8,4096]{3,2,1,0:T(8,128)(2,1)S(1)}, bf16[3,16,8,4096]{3,2,1,0:T(8,128)(2,1)}, u32[]{:S(2)}) %copy-start.1) | copy-done | bytes 3145752
  22.7 6.0 %noise.3.tie_ref.refs_0_ = f32[2,128,2560]{2,1,0:T(8,128)S(1)} custom-call(bf16[3,128,4096]{2,1,0:T(8,128)(2,1)S(1)} %bitcast.8, f32[64,256]{1,0:T(8,128)S(1)} %copy-done.13, f32[2,1280]{1,0:T(2,128)S(1)} %get-tuple-element.23.tie_ref.own_ref), custom_call_target="tpu_custom_call" | custom-call | tf_op jit(solution)/shard_map/noise/pallas_call | solution.py:62
  28.7 0.0 copy-start.2
  28.7 0.0 copy-start.3
  28.8 0.0 copy-start.11
  28.8 0.0 copy-start.15
  28.8 0.0 copy-start.16
  28.8 0.0 copy-start.18
  28.8 0.0 copy-start.19
  28.8 1.6 all-to-all-done.parts_ref
  30.4 0.9 refit.3
  31.3 13.0 %all-to-all-start.1 = ((f32[16,1,128]{2,1,0:T(1,128)}), f32[16,1,128]{2,1,0:T(1,128)S(1)}, u32[]{:S(2)}, u32[]{:S(2)}) async-start(f32[16,1,128]{2,1,0:T(1,128)} %get-tuple-element.26.refs_9_), calls=%async_computation.1 | async-start | bytes 16384 | tf_op jit(solution)/shard_map/all_to_all | solution.py:332
  44.3 0.0 copy-done.2
  44.3 0.0 copy-done.3
  44.3 0.0 copy-done.11
  44.4 1.1 copy-done.6
  45.5 12.7 %rollout.3 = f32[1,8,16]{2,1,0:T(8,128)S(1)} custom-call(bf16[128,2560]{1,0:T(8,128)(2,1)S(1)} %copy-done.6, f32[128,128]{1,0:T(8,128)S(1)} %get-tuple-element.28.refs_1_, f32[16,128]{1,0:T(8,128)S(1)} %copy-done.15, f32[16,128]{1,0:T(8,128)S(1)} %copy-done.16, bf16[128,512]{1,0:T(8,128)(2,1)S(1)} %copy-done.2, bf16[64,512]{1,0:T(8,128)(2,1)S(1)} %copy-done.11, ...), custom_call_target="tpu_custom_call" | custom-call | flops 268435456 | bytes 655360 | tf_op jit(solution)/shard_map/rollout/pallas_call | solution.py:274
  58.1 0.0 all-to-all-done.1.peak_ref
  58.2 15.8 %all_to_all.45.refs_3_ = f32[32,2,1408]{2,1,0:T(2,128)S(1)} all-to-all(f32[32,2,1408]{2,1,0:T(2,128)S(1)} %to_all.3), channel_id=1, replica_groups=mesh['env'=16,'cand'=32] {'cand'}, dimensions={0} | all-to-all | bytes 720896 | tf_op jit(solution)/shard_map/all_to_all | solution.py:338
  74.0 1.1 actions.4
  75.2 13.0 %all_to_all.46.parts_ref = f32[32,2,1280]{2,1,0:T(2,128)S(1)} all-to-all(f32[32,2,1280]{2,1,0:T(2,128)S(1)} %get-tuple-element.29), channel_id=1, replica_groups=mesh['env'=16,'cand'=32] {'cand'}, dimensions={0} | all-to-all | bytes 655360 | tf_op jit(solution)/shard_map/all_to_all | solution.py:328
  88.2 0.9 refit.4
  89.1 11.7 %all-to-all-start.4 = ((f32[16,1,128]{2,1,0:T(1,128)}), f32[16,1,128]{2,1,0:T(1,128)S(1)}, u32[]{:S(2)}, u32[]{:S(2)}) async-start(f32[16,1,128]{2,1,0:T(1,128)} %get-tuple-element.32.refs_9_), calls=%async_computation.4 | async-start | bytes 16384 | tf_op jit(solution)/shard_map/all_to_all | solution.py:332
  100.8 1.1 copy-done.10
  101.9 12.7 %rollout.4 = f32[1,8,16]{2,1,0:T(8,128)S(1)} custom-call(bf16[128,2560]{1,0:T(8,128)(2,1)S(1)} %copy-done.10, f32[128,128]{1,0:T(8,128)S(1)} %get-tuple-element.34.refs_1_, f32[16,128]{1,0:T(8,128)S(1)} %copy-done.15, f32[16,128]{1,0:T(8,128)S(1)} %copy-done.16, bf16[128,512]{1,0:T(8,128)(2,1)S(1)} %copy-done.2, bf16[64,512]{1,0:T(8,128)(2,1)S(1)} %copy-done.11, ...), custom_call_target="tpu_custom_call" | custom-call | flops 268435456 | bytes 655360 | tf_op jit(solution)/shard_map/rollout/pallas_call | solution.py:274
  114.6 0.0 all-to-all-done.4.peak_ref
  114.6 13.6 %all_to_all.47.refs_3_ = f32[32,2,1408]{2,1,0:T(2,128)S(1)} all-to-all(f32[32,2,1408]{2,1,0:T(2,128)S(1)} %to_all.4), channel_id=1, replica_groups=mesh['env'=16,'cand'=32] {'cand'}, dimensions={0} | all-to-all | bytes 720896 | tf_op jit(solution)/shard_map/all_to_all | solution.py:338
  128.2 1.1 actions.5
  129.4 13.0 %all_to_all.48.parts_ref = f32[32,2,1280]{2,1,0:T(2,128)S(1)} all-to-all(f32[32,2,1280]{2,1,0:T(2,128)S(1)} %get-tuple-element.35), channel_id=1, replica_groups=mesh['env'=16,'cand'=32] {'cand'}, dimensions={0} | all-to-all | bytes 655360 | tf_op jit(solution)/shard_map/all_to_all | solution.py:328
  142.4 0.9 refit.5
  143.3 11.7 %all-to-all-start.7 = ((f32[16,1,128]{2,1,0:T(1,128)}), f32[16,1,128]{2,1,0:T(1,128)S(1)}, u32[]{:S(2)}, u32[]{:S(2)}) async-start(f32[16,1,128]{2,1,0:T(1,128)} %get-tuple-element.38.refs_11_), calls=%async_computation.7 | async-start | bytes 16384 | tf_op jit(solution)/shard_map/all_to_all | solution.py:332
  155.0 1.1 copy-done.8
  156.1 13.3 %rollout.5.tie_ref = f32[3,8,16]{2,1,0:T(8,128)} custom-call(bf16[128,2560]{1,0:T(8,128)(2,1)S(1)} %copy-done.8, f32[128,128]{1,0:T(8,128)S(1)} %get-tuple-element.40.refs_1_, f32[16,128]{1,0:T(8,128)S(1)} %copy-done.15, f32[16,128]{1,0:T(8,128)S(1)} %copy-done.16, bf16[128,512]{1,0:T(8,128)(2,1)S(1)} %copy-done.2, bf16[64,512]{1,0:T(8,128)(2,1)S(1)} %copy-done.11, ...), custom_call_target="tpu_custom_call" | custom-call | flops 268435456 | bytes 655360 | tf_op jit(solution)/shard_map/rollout/pallas_call | solution.py:274
  169.4 0.0 all-to-all-done.7.peak_ref
  169.4 0.7 copy-done.17
  170.2 13.6 %all_to_all.49.state_ref = f32[32,2,1408]{2,1,0:T(2,128)S(1)} all-to-all(f32[32,2,1408]{2,1,0:T(2,128)S(1)} %to_all.5), channel_id=1, replica_groups=mesh['env'=16,'cand'=32] {'cand'}, dimensions={0} | all-to-all | bytes 720896 | tf_op jit(solution)/shard_map/all_to_all | solution.py:338
  183.8 0.8 finished.1
  (21 shorter events, 0.1 us)
Async XLA Ops:
  1.4 1.9 %copy-start = (bf16[3,16,8,4096]{3,2,1,0:T(8,128)(2,1)S(1)}, bf16[3,16,8,4096]{3,2,1,0:T(8,128)(2,1)}, u32[]{:S(2)}) copy-start(bf16[3,16,8,4096]{3,2,1,0:T(8,128)(2,1)} %param.12) | copy-start | bytes 9437188
  3.3 0.9 copy-start.4
  4.2 0.8 copy-start.12
  5.0 2.9 %copy-start.14 = (f32[16,2560]{1,0:T(8,128)S(1)}, f32[16,2560]{1,0:T(8,128)}, u32[]{:S(2)}) copy-start(f32[16,2560]{1,0:T(8,128)} %refs_4_.4) | copy-start | bytes 491524
  5.0 15.8 %copy-start.13 = (f32[64,256]{1,0:T(8,128)S(1)}, f32[64,256]{1,0:T(8,128)}, u32[]{:S(2)}) copy-start(f32[64,256]{1,0:T(8,128)} %constant.6.clone.band_ref) | copy-start | bytes 196612
  9.6 0.8 copy-start.5
  10.4 20.0 %all-to-all-start = ((f32[32,2,1280]{2,1,0:T(2,128)}), f32[32,2,1280]{2,1,0:T(2,128)S(1)}, u32[]{:S(2)}, u32[]{:S(2)}) async-start(f32[32,2,1280]{2,1,0:T(2,128)} %get-tuple-element.24), calls=%async_computation | async-start | bytes 655360 | tf_op jit(solution)/shard_map/all_to_all | solution.py:328
  20.8 1.9 %copy-start.1 = (bf16[3,16,8,4096]{3,2,1,0:T(8,128)(2,1)S(1)}, bf16[3,16,8,4096]{3,2,1,0:T(8,128)(2,1)}, u32[]{:S(2)}) copy-start(bf16[3,16,8,4096]{3,2,1,0:T(8,128)(2,1)} %param.12) | copy-start | bytes 9437188
  28.7 15.6 %copy-start.2 = (bf16[128,512]{1,0:T(8,128)(2,1)S(1)}, bf16[128,512]{1,0:T(8,128)(2,1)}, u32[]{:S(2)}) copy-start(bf16[128,512]{1,0:T(8,128)(2,1)} %refs_4_.7) | copy-start | bytes 393220
  28.7 15.6 %copy-start.3 = (bf16[512,128]{1,0:T(8,128)(2,1)S(1)}, bf16[512,128]{1,0:T(8,128)(2,1)}, u32[]{:S(2)}) copy-start(bf16[512,128]{1,0:T(8,128)(2,1)} %refs_6_.5) | copy-start | bytes 393220
  28.8 15.6 %copy-start.11 = (bf16[64,512]{1,0:T(8,128)(2,1)S(1)}, bf16[64,512]{1,0:T(8,128)(2,1)}, u32[]{:S(2)}) copy-start(bf16[64,512]{1,0:T(8,128)(2,1)} %refs_5_.5) | copy-start | bytes 196612
  28.8 15.6 %copy-start.15 = (f32[16,128]{1,0:T(8,128)S(1)}, f32[16,128]{1,0:T(8,128)}, u32[]{:S(2)}) copy-start(f32[16,128]{1,0:T(8,128)} %refs_2_.5) | copy-start | bytes 24580
  28.8 15.6 %copy-start.16 = (f32[16,128]{1,0:T(8,128)S(1)}, f32[16,128]{1,0:T(8,128)}, u32[]{:S(2)}) copy-start(f32[16,128]{1,0:T(8,128)} %refs_3_.7) | copy-start | bytes 24580
  28.8 15.6 %copy-start.18 = (f32[512]{0:T(512)S(1)}, f32[512]{0:T(512)}, u32[]{:S(2)}) copy-start(f32[512]{0:T(512)} %param.20) | copy-start | bytes 6148
  28.8 15.6 %copy-start.19 = (f32[128]{0:T(128)S(1)}, f32[128]{0:T(128)}, u32[]{:S(2)}) copy-start(f32[128]{0:T(128)} %param.21) | copy-start | bytes 1540
  31.3 26.9 %all-to-all-start.1 = ((f32[16,1,128]{2,1,0:T(1,128)}), f32[16,1,128]{2,1,0:T(1,128)S(1)}, u32[]{:S(2)}, u32[]{:S(2)}) async-start(f32[16,1,128]{2,1,0:T(1,128)} %get-tuple-element.26.refs_9_), calls=%async_computation.1 | async-start | bytes 16384 | tf_op jit(solution)/shard_map/all_to_all | solution.py:332
  44.4 1.1 copy-start.6
  75.2 13.9 %copy-start.9 = (bf16[128,2560]{1,0:T(8,128)(2,1)}, bf16[128,2560]{1,0:T(8,128)(2,1)S(1)}, u32[]{:S(2)}) copy-start(bf16[128,2560]{1,0:T(8,128)(2,1)S(1)} %get-tuple-element.33.refs_0_) | copy-start | bytes 1966084
  89.1 25.5 %all-to-all-start.4 = ((f32[16,1,128]{2,1,0:T(1,128)}), f32[16,1,128]{2,1,0:T(1,128)S(1)}, u32[]{:S(2)}, u32[]{:S(2)}) async-start(f32[16,1,128]{2,1,0:T(1,128)} %get-tuple-element.32.refs_9_), calls=%async_computation.4 | async-start | bytes 16384 | tf_op jit(solution)/shard_map/all_to_all | solution.py:332
  100.8 1.1 copy-start.10
  129.4 13.9 %copy-start.7 = (bf16[128,2560]{1,0:T(8,128)(2,1)}, bf16[128,2560]{1,0:T(8,128)(2,1)S(1)}, u32[]{:S(2)}) copy-start(bf16[128,2560]{1,0:T(8,128)(2,1)S(1)} %get-tuple-element.39.refs_0_) | copy-start | bytes 1966084
  143.3 26.1 %all-to-all-start.7 = ((f32[16,1,128]{2,1,0:T(1,128)}), f32[16,1,128]{2,1,0:T(1,128)S(1)}, u32[]{:S(2)}, u32[]{:S(2)}) async-start(f32[16,1,128]{2,1,0:T(1,128)} %get-tuple-element.38.refs_11_), calls=%async_computation.7 | async-start | bytes 16384 | tf_op jit(solution)/shard_map/all_to_all | solution.py:332
  155.0 1.1 copy-start.8
  169.4 0.7 copy-start.17

commit v3 on v2

v3 whole, which is shorter than its diff:
```python
import functools

import jax
import jax.numpy as jnp
import numpy as np
from jax import lax
from jax.experimental import pallas as pl
from jax.experimental.pallas import tpu as pltpu
from jax.sharding import PartitionSpec as P

BETA_EXP = 2.5
MOMENTUM = 0.1
FLOOR_SHARE = 0.1
ACT_COST = 0.1
LANES = 128
ROLL_FLOPS = 1 << 28
CUT = 22
VMEM = pl.BlockSpec(memory_space=pltpu.VMEM)
SMEM = pl.BlockSpec(memory_space=pltpu.SMEM)
HBM = pl.BlockSpec(memory_space=pltpu.HBM)


def whole(shape):
    return pl.BlockSpec(shape, lambda i: (0,) * len(shape))


def stay(array):
    return pltpu.with_memory_space_constraint(array, pltpu.HBM)


def in_hbm(shape, dtype=jnp.float32):
    return pltpu.HBM(shape, dtype)


def color_kernel(length):
    freqs = np.arange(length // 2 + 1)
    scale = (np.maximum(freqs, 1).astype(np.float32) / np.float32(length)) ** np.float32(-BETA_EXP / 2)
    kernel = np.fft.irfft(scale.astype(np.float64), n=length)
    kernel = kernel / np.sqrt(np.sum(kernel * kernel))
    return np.asarray(kernel, np.float32).astype(jnp.bfloat16).astype(np.float32)


def noise_body(white_ref, tie_ref, out_ref, rows_in, fill, sems, *, act_dim, blocks, first, parts):
    count = out_ref.shape[0]
    _, rows, flat = white_ref.shape
    length = flat // act_dim
    size = rows // parts

    def fetch(one, part):
        at = pl.ds(part * size, size)
        return pltpu.make_async_copy(
            white_ref.at[first + one, at, :], rows_in.at[one, at, :], sems.at[one * parts + part]
        )

    for one in range(count):
        for part in range(parts):
            fetch(one, part).start()
    kernel = color_kernel(length)
    row = lax.broadcasted_iota(jnp.int32, (act_dim, 256), 0)
    lane = lax.broadcasted_iota(jnp.int32, (act_dim, 256), 1)
    hit = lane % act_dim == row
    quarter = lax.broadcasted_iota(jnp.int32, (1, 256), 1) // act_dim
    for j in range(length):
        band = jnp.full((1, 256), float(kernel[-j % length]), jnp.float32)
        for q in range(1, 256 // act_dim):
            band = jnp.where(quarter == q, float(kernel[(q - j) % length]), band)
        tile = jnp.where(hit, band, 0.0).astype(jnp.bfloat16)
        fill[pl.ds(j * act_dim, act_dim), :] = tile
        fill[pl.ds(flat + j * act_dim, act_dim), :] = tile
    for one in range(count):
        for part in range(parts):
            fetch(one, part).wait()
        for block in range(blocks):
            start = (flat - block * 256) % flat
            out_ref[one, :, pl.ds(block * 256, 256)] = jnp.dot(
                rows_in[one], fill[pl.ds(start, flat), :], preferred_element_type=jnp.float32
            )


def noise_of(white, first, count, tie, act_dim, horizon):
    _, rows, flat = white.shape
    width = horizon * act_dim
    parts = 1
    return pl.pallas_call(
        functools.partial(
            noise_body, act_dim=act_dim, blocks=width // 256, first=first, parts=parts
        ),
        in_specs=[HBM, HBM],
        out_specs=VMEM,
        out_shape=jax.ShapeDtypeStruct((count, rows, width), jnp.float32),
        scratch_shapes=[
            pltpu.VMEM((count, rows, flat), jnp.bfloat16),
            pltpu.VMEM((2 * flat, 256), jnp.bfloat16),
            pltpu.SemaphoreType.DMA((count * parts,)),
        ],
        cost_estimate=pl.CostEstimate(flops=ROLL_FLOPS, bytes_accessed=1 << 20, transcendentals=0),
        compiler_params=pltpu.CompilerParams(vmem_limit_bytes=16 << 20),
        name="noise",
    )(stay(white), stay(tie))


def stats_of(state_ref, envs, half, envs_total):
    peaks = state_ref[:, 0, pl.ds(half, LANES)]
    pair = jnp.max(peaks.reshape(envs, 2, LANES), axis=1)
    peak = jnp.max(pair, axis=(0, 1), keepdims=True)
    total = jnp.sum(jnp.sum(pair, axis=0, keepdims=True), axis=1, keepdims=True)
    return FLOOR_SHARE * peak, 0.5 + total / (peak * envs_total)


def action_body(*refs, it, envs_total):
    first = it == 0
    if first:
        noise_ref, elite_ref, mine_ref, tie_ref, mean_ref, std_ref = refs[:6]
    else:
        noise_ref, elite_ref, mine_ref, tie_ref, state_ref = refs[:5]
    acts_out, asq_ref, sums_ref, own_ref, acts_ref, sems = refs[-6:]
    half = sums_ref.shape[2]
    rows = acts_ref.shape[0]
    envs = sums_ref.shape[0] // 2
    cands = rows // envs
    me = mine_ref[0]
    if first:
        lanes = pl.ds(pl.multiple_of((me % 2) * half, LANES), half)
        own_ref[0:1, :] = mean_ref[pl.ds(me // 2, 1), lanes]
        own_ref[1:2, :] = std_ref[pl.ds(me // 2, 1), lanes]
    else:
        floor, gain = stats_of(state_ref, envs, half, envs_total)
        own = state_ref[me, :, pl.ds(0, half)]
        own_ref[0:1, :] = own[0:1]
        own_ref[1:2, :] = jnp.maximum(own[1:2], floor) * gain
    per = 4

    def send(part):
        at = pl.ds(part * per * cands, per * cands)
        return pltpu.make_async_copy(acts_ref.at[at, :], acts_out.at[at, :], sems.at[part])

    ids = me * cands + lax.broadcasted_iota(jnp.int32, (cands, 1), 0)
    for env in range(envs):
        at = pl.ds(env * cands, cands)
        chosen = elite_ref[it, env : env + 1, :] == ids
        member = jnp.sum(jnp.where(chosen, 1.0, 0.0), axis=1, keepdims=True)
        member = jnp.broadcast_to(member, (cands, LANES))
        square = jnp.zeros((cands, LANES), jnp.float32)
        for side in range(2):
            line = 2 * env + side
            for step in range(half // LANES):
                lanes = pl.ds(step * LANES, LANES)
                whole = pl.ds(side * half + step * LANES, LANES)
                if first:
                    center = mean_ref[pl.ds(env, 1), whole]
                    spread = std_ref[pl.ds(env, 1), whole]
                else:
                    center = state_ref[line, 0:1, lanes]
                    spread = jnp.maximum(state_ref[line, 1:2, lanes], floor) * gain
                action = jnp.clip(center + spread * noise_ref[0, at, whole], -1.0, 1.0)
                acts_ref[at, whole] = action.astype(jnp.bfloat16)
                both = action * action
                square = square + both
                sums_ref[line, 0:1, lanes] = jnp.sum(action * member, axis=0, keepdims=True)
                sums_ref[line, 1:2, lanes] = jnp.sum(both * member, axis=0, keepdims=True)
        asq_ref[at, :] = square
        if env % per == per - 1:
            send(env // per).start()
    for part in range(envs // per):
        send(part).wait()


def actions_of(noise, at, elite_idx, mine, tie, state, it, envs_total, lines, half):
    _, rows, width = noise.shape
    return pl.pallas_call(
        functools.partial(action_body, it=it, envs_total=envs_total),
        grid=(1,),
        in_specs=[pl.BlockSpec((1, rows, width), lambda i: (at, 0, 0)), VMEM, SMEM, HBM]
        + [VMEM] * len(state),
        out_specs=[HBM, whole((rows, LANES)), whole((lines, 2, half)), whole((2, half))],
        out_shape=[
            in_hbm((rows, width), jnp.bfloat16),
            in_hbm((rows, LANES)),
            in_hbm((lines, 2, half)),
            in_hbm((2, half)),
        ],
        scratch_shapes=[
            pltpu.VMEM((rows, width), jnp.bfloat16),
            pltpu.SemaphoreType.DMA((lines // 8,)),
        ],
        compiler_params=pltpu.CompilerParams(vmem_limit_bytes=12 << 20),
        name="actions",
    )(noise, elite_idx, mine, stay(tie), *state)


def refit_body(parts_ref, own_ref, tie_ref, slice_ref, peak_ref, *, elites):
    total = jnp.sum(parts_ref[...], axis=0)
    mean = total[0:1] / elites
    variance = jnp.maximum(total[1:2] / elites - mean * mean, 0.0)
    slice_ref[0:1, :] = MOMENTUM * own_ref[0:1, :] + (1.0 - MOMENTUM) * mean
    mixed = MOMENTUM * own_ref[1:2, :] + (1.0 - MOMENTUM) * jnp.sqrt(variance)
    slice_ref[1:2, :] = mixed
    peak_ref[...] = jnp.broadcast_to(jnp.max(mixed, axis=1, keepdims=True)[None], peak_ref.shape)


def refit(parts, own, tie, elites, groups):
    return pl.pallas_call(
        functools.partial(refit_body, elites=elites),
        in_specs=[VMEM, VMEM, HBM],
        out_specs=[VMEM, VMEM],
        out_shape=[
            jax.ShapeDtypeStruct(own.shape, jnp.float32),
            jax.ShapeDtypeStruct((groups, 1, LANES), jnp.float32),
        ],
        compiler_params=pltpu.CompilerParams(vmem_limit_bytes=4 << 20),
        name="refit",
    )(parts, own, stay(tie))


def spread_body(slice_ref, peak_ref, out_ref, token_ref):
    lines = out_ref.shape[0]
    half = slice_ref.shape[1]
    lane = lax.broadcasted_iota(jnp.int32, (1, LANES), 1)
    tail = jnp.zeros((1, LANES), jnp.float32)
    for group in range(peak_ref.shape[0]):
        tail = jnp.where(lane == group, peak_ref[group], tail)
    main = jnp.broadcast_to(slice_ref[...][None], (lines, 2, half))
    out_ref[:, :, pl.ds(0, half)] = main
    token_ref[...] = jnp.broadcast_to(tail, token_ref.shape)
    out_ref[:, :, pl.ds(half, LANES)] = jnp.broadcast_to(tail[None], (lines, 2, LANES))


def to_all(piece, peaks, lines):
    half = piece.shape[1]
    return pl.pallas_call(
        spread_body,
        grid=(1,),
        in_specs=[VMEM, VMEM],
        out_specs=[whole((lines, 2, half + LANES)), whole((8, LANES))],
        out_shape=[in_hbm((lines, 2, half + LANES)), in_hbm((8, LANES))],
        compiler_params=pltpu.CompilerParams(vmem_limit_bytes=4 << 20),
        name="to_all",
    )(piece, peaks)


def final_body(state_ref, mean_ref, std_ref, *, envs_total):
    envs, width = mean_ref.shape
    half = width // 2
    floor, gain = stats_of(state_ref, envs, half, envs_total)
    for env in range(envs):
        for side in range(2):
            lanes = pl.ds(side * half, half)
            line = 2 * env + side
            mean_ref[pl.ds(env, 1), lanes] = state_ref[line, 0:1, pl.ds(0, half)]
            std_ref[pl.ds(env, 1), lanes] = (
                jnp.maximum(state_ref[line, 1:2, pl.ds(0, half)], floor) * gain
            )


def finished(state, envs, width, envs_total):
    shape = jax.ShapeDtypeStruct((envs, width), jnp.float32)
    return pl.pallas_call(
        functools.partial(final_body, envs_total=envs_total),
        in_specs=[VMEM],
        out_specs=[VMEM, VMEM],
        out_shape=[shape, shape],
        compiler_params=pltpu.CompilerParams(vmem_limit_bytes=4 << 20),
        name="finished",
    )(state)


def rollout_body(*refs, spans, act_dim, total, earlier):
    refs = list(refs)
    take = lambda n: [refs.pop(0) for _ in range(n)]
    acts = take(len(spans))
    carried = [take(1)[0] if first else None for first, _ in spans]
    squares = [take(1)[0] if last == total else None for _, last in spans]
    begin_ref, goal_ref, ws_ref, wa_ref, wout_ref, bin_ref, bout_ref = take(7)
    before = take(earlier)
    take(1)
    outs = take(len(spans))
    moves, win, start, goal, sems = refs
    envs, dim = begin_ref.shape
    rows = acts[0].shape[0]
    cands = rows // envs
    steps = spans[0][1] - spans[0][0]
    copies = []
    for k, (first, last) in enumerate(spans):
        copies.append(
            pltpu.make_async_copy(
                acts[k].at[:, pl.ds(first * act_dim, steps * act_dim)],
                moves.at[pl.ds(k * rows, rows), :],
                sems.at[k],
            )
        )
        copies[k].start()
    zeros = jnp.zeros(wa_ref.shape, jnp.bfloat16)
    for parity in range(2):
        win[parity, pl.ds(0, dim), :] = ws_ref[...] * jnp.bfloat16(0.5)
        win[parity, pl.ds(dim + parity * act_dim, act_dim), :] = wa_ref[...] * jnp.bfloat16(0.5)
        win[parity, pl.ds(dim + (1 - parity) * act_dim, act_dim), :] = zeros
    for k in range(len(spans)):
        for env in range(envs):
            at = pl.ds(k * rows + env * cands, cands)
            if carried[k] is None:
                start[0, at, :] = jnp.broadcast_to(begin_ref[pl.ds(env, 1), :], (cands, dim))
            goal[at, :] = jnp.broadcast_to(goal_ref[pl.ds(env, 1), :], (cands, dim))
        at = pl.ds(k * rows, rows)
        if carried[k] is None:
            start[1, at, :] = jnp.zeros((rows, dim), jnp.float32)
        else:
            start[0, at, :] = carried[k][0]
            start[1, at, :] = carried[k][1]
    bias_in = bin_ref[...] * 0.5
    for copy in copies:
        copy.wait()

    def two_steps(k, carry):
        state, error = carry
        pair = moves[:, pl.ds(pl.multiple_of(k * 2 * act_dim, 2 * act_dim), 2 * act_dim)]
        for parity in range(2):
            joined = jnp.concatenate([state.astype(jnp.bfloat16), pair], axis=1)
            half = jnp.dot(joined, win[parity], preferred_element_type=jnp.float32) + bias_in
            hidden = (half + half * jnp.tanh(half)).astype(jnp.bfloat16)
            moved = jnp.dot(hidden, wout_ref[...], preferred_element_type=jnp.float32)
            state = jnp.tanh(state + moved + bout_ref[...])
            gap = state - goal[...]
            error = error + gap * gap
        return state, error

    state, error = lax.fori_loop(0, steps // 2, two_steps, (start[0], start[1]))
    for k, (_, last) in enumerate(spans):
        part = slice(k * rows, (k + 1) * rows)
        if last < total:
            outs[k][0] = state[part]
            outs[k][1] = error[part]
            continue
        both = error[part] / (dim * total) + squares[k][...] * (ACT_COST / (act_dim * total))
        cost = jnp.broadcast_to(jnp.sum(both, axis=1, keepdims=True), (rows, LANES))
        lane = lax.broadcasted_iota(jnp.int32, (cands, LANES), 1)
        table = jnp.zeros((cands, LANES), jnp.float32)
        for env in range(envs):
            table = jnp.where(lane == env, cost[env * cands : (env + 1) * cands], table)
        for n in range(earlier):
            outs[k][n] = before[n][0]
        outs[k][earlier] = table[:, :envs]


def rollout(parts, fixed, before, tie, act_dim):
    rows, width = parts[0][0].shape
    envs, dim = fixed[0].shape
    cands = rows // envs
    total = width // act_dim
    spans = [(p[3], p[4]) for p in parts]
    steps = spans[0][1] - spans[0][0]
    assert all(b - a == steps and a % 2 == 0 for a, b in spans) and steps % 2 == 0
    acts = [p[0] for p in parts]
    carried = [p[2] for p in parts if p[3]]
    squares = [p[1] for p in parts if p[4] == total]
    shapes = [
        (1 + len(before), cands, envs) if last == total else (2, rows, dim) for _, last in spans
    ]
    small = len(carried) + len(squares) + len(fixed) + len(before)
    return pl.pallas_call(
        functools.partial(
            rollout_body, spans=spans, act_dim=act_dim, total=total, earlier=len(before)
        ),
        grid=(1,),
        in_specs=[HBM] * len(acts) + [VMEM] * small + [HBM],
        out_specs=[whole(shape) for shape in shapes],
        out_shape=[in_hbm(shape) for shape in shapes],
        scratch_shapes=[
            pltpu.VMEM((len(parts) * rows, steps * act_dim), jnp.bfloat16),
            pltpu.VMEM((2, dim + 2 * act_dim, fixed[2].shape[1]), jnp.bfloat16),
            pltpu.VMEM((2, len(parts) * rows, dim), jnp.float32),
            pltpu.VMEM((len(parts) * rows, dim), jnp.float32),
            pltpu.SemaphoreType.DMA((len(parts),)),
        ],
        cost_estimate=pl.CostEstimate(flops=ROLL_FLOPS, bytes_accessed=1 << 20, transcendentals=0),
        compiler_params=pltpu.CompilerParams(vmem_limit_bytes=10 << 20),
        name="rollout",
    )(*map(stay, acts), *carried, *squares, *fixed, *before, stay(tie))


def shards(
    white,
    mean_init,
    std_init,
    init_state,
    goal_state,
    w_state,
    w_action,
    w_out,
    bias_in,
    bias_out,
    elite_idx,
):
    iters, envs, cands, flat = white.shape
    act_dim = w_action.shape[0]
    length = flat // act_dim
    width = mean_init.shape[1]
    horizon = width // act_dim
    half = width // 2
    elites = elite_idx.shape[2]
    groups = lax.axis_size("env")
    peers = lax.axis_size("cand")
    lines = 2 * envs
    envs_total = envs * groups
    rows = envs * cands
    assert lines == peers and rows % 16 == 0
    assert iters == 3
    mine = lax.axis_index("cand").astype(jnp.int32)[None]
    fixed = (init_state, goal_state, w_state, w_action, w_out, bias_in[None], bias_out[None])
    white = white.reshape(iters, rows, flat)
    elite_idx = jnp.swapaxes(elite_idx, 0, 1)
    mix = functools.partial(lax.all_to_all, axis_name="cand", split_axis=0, concat_axis=0, tiled=True)
    cut = min(CUT, horizon)
    acts, asq, held, costs = {}, {}, {}, {}

    def part(it, first, last):
        return (acts[it], asq[it], held.get(it), first, last)

    def play(parts, tie, before=()):
        outs = rollout([part(*p) for p in parts], fixed, before, tie, act_dim)
        for (it, _, last), out in zip(parts, outs):
            if last < horizon:
                held[it] = out
            else:
                costs[it] = out
        return outs[0]

    noise = noise_of(white, 0, 1, mine, act_dim, horizon)
    state, tie = (mean_init, std_init), mine
    for it in range(iters):
        acts[it], asq[it], sums, own = actions_of(
            noise, max(it - 1, 0), elite_idx, mine, tie, state, it, envs_total, lines, half
        )
        parts = mix(sums)
        if it == 0:
            tie = noise = noise_of(white, 1, iters - 1, own, act_dim, horizon)
        elif it == 1:
            tie = play([(0, cut, horizon)], own)
        else:
            tie = play([(1, cut, horizon), (2, 0, horizon - cut)], own)
        piece, peak = refit(parts, own, tie, elites, groups)
        peaks = lax.all_to_all(peak, "env", 0, 0, tiled=True)
        spread, token = to_all(piece, peaks, lines)
        state = (mix(spread),)
        if it < iters - 1:
            tie = play([(it, 0, cut)], token)
        else:
            tie = play([(2, horizon - cut, horizon)], token, (costs[0], costs[1]))
    mean, std = finished(state[0], envs, width, envs_total)
    return (mean, std, jnp.swapaxes(costs[iters - 1], 1, 2))


def solution(mesh):
    in_specs = (
        P(None, "env", "cand", None),
        P("env", None),
        P("env", None),
        P("env", None),
        P("env", None),
        P(),
        P(),
        P(),
        P(),
        P(),
        P("env", None, None),
    )
    out_specs = (P("env", None), P("env", None), P(None, "env", "cand"))
    return jax.shard_map(shards, mesh=mesh, in_specs=in_specs, out_specs=out_specs, check_vma=False)
```

time: 186 us -> 174 us (0.935)
  blocking collectives: 69.1 us -> 52.1 us
  Pallas kernels: 55 us -> 63.5 us
  local copies, waits for them, and re-layouts: 11.1 us -> 5.17 us
  waiting for transfers between devices: 1.6 us -> 6.62 us
  starting transfers between devices: 46.9 us -> 44.6 us
    all_to_all x5 -> x3, blocking collectives: 69.1 us -> 52.1 us  [shards(): peaks = lax.all_to_all(peak, 'env', 0, 0, tiled=True)]
    unnamed x41 -> x48, local copies, waits for them, and re-layouts: 11.1 us -> 5.17 us
    all_to_all x4 -> x6, waiting for transfers between devices: 1.6 us -> 6.62 us  [the longest x3 4.23 us: shards(): parts = mix(sums)]
    pallas_call x6 -> x8, Pallas kernels: 38.7 us -> 43.2 us  [the longest x5 40.8 us: rollout(): pl.pallas_call(functools.partial(rollout_body, spans=spans, act_dim=act_d...]
    pallas_call x3, Pallas kernels: 3.91 us -> 7.49 us  [actions_of(): pl.pallas_call(functools.partial(action_body, it=it, envs_total=envs_tota...]
    all_to_all x4 -> x6, starting transfers between devices: 46.9 us -> 44.6 us  [the longest x3 22.9 us: shards(): parts = mix(sums)]
    pallas_call x2, Pallas kernels: 8.9 us -> 11.2 us  [noise_of(): pl.pallas_call(functools.partial(noise_body, act_dim=act_dim, blocks=widt...]
  transfers between devices with their start and end apart: 4 -> 6, of which waited for: 1 -> 5; matrix products, arithmetic and copies ran while one was open for 0% -> 0% of each run, Pallas kernels for 24% -> 28%
where the time goes in v3:
time: 174 us; the launch traced here: 173 us
  Pallas kernels  63.5 us (36%)
  blocking collectives  52.1 us (30%)
  starting transfers between devices  44.6 us (26%)
  waiting for transfers between devices  6.62 us (4%)
  local copies, waits for them, and re-layouts  5.17 us (3%)
    all_to_all x3, blocking collectives, shards(): peaks = lax.all_to_all(peak, 'env', 0, 0, tiled=True)  52.1 us
    pallas_call x5, Pallas kernels, rollout(): pl.pallas_call(functools.partial(rollout_body, spans=spans, act_dim=act_d...  40.8 us
    all_to_all x3, starting transfers between devices, shards(): parts = mix(sums)  22.9 us
    all_to_all x3, starting transfers between devices, shards(): state = (mix(spread),)  21.6 us
    pallas_call x2, Pallas kernels, noise_of(): pl.pallas_call(functools.partial(noise_body, act_dim=act_dim, blocks=widt...  11.2 us
    pallas_call x3, Pallas kernels, actions_of(): pl.pallas_call(functools.partial(action_body, it=it, envs_total=envs_tota...  7.49 us
    unnamed x48, local copies, waits for them, and re-layouts  5.17 us
    all_to_all x3, waiting for transfers between devices, shards(): parts = mix(sums)  4.23 us
  transfers between devices with their start and end apart: 6, of which 5 were waited for; matrix products, arithmetic and copies ran while one was open for 0% of the time, Pallas kernels for 28%

profile of v3, /device:TPU:1, one launch (start us, length us, event | category | flops | bytes accessed | tf_op | source)
XLA Modules:
  0.0 173.0 jit_solution(3324327575902251467)
XLA Ops:
  0.7 4.1 %noise.2.refs_0_ = f32[1,128,2560]{2,1,0:T(8,128)S(1)} custom-call(bf16[3,128,4096]{2,1,0:T(8,128)(2,1)} %bitcast.19, s32[1]{0:T(128)} %bitcast.1.tie_ref.refs_2_.refs_3_), custom_call_target="tpu_custom_call" | custom-call | flops 268435456 | bytes 1048576 | tf_op jit(solution)/shard_map/noise/pallas_call | solution.py:84
  4.9 2.3 %actions.3 = (bf16[128,2560]{1,0:T(8,128)(2,1)}, f32[128,128]{1,0:T(8,128)}, f32[32,2,1280]{2,1,0:T(2,128)}, f32[2,1280]{1,0:T(2,128)}) custom-call(f32[1,128,2560]{2,1,0:T(8,128)S(1)} %noise.2.refs_0_, s32[3,16,25]{2,1,0:T(8,128)S(1)} %bitcast.6, s32[1]{0:T(128)} %bitcast.1.tie_ref.refs_2_.refs_3_, s32[1]{0:T(128)} %bitcast.1.tie_ref.refs_2_.refs_3_, ...), custom_call_target="tpu_custom_call" | custom-call | tf_op jit(solution)/shard_map/actions/pallas_call | solution.py:170
  7.2 10.4 %all-to-all-start = ((f32[32,2,1280]{2,1,0:T(2,128)}), f32[32,2,1280]{2,1,0:T(2,128)S(1)}, u32[]{:S(2)}, u32[]{:S(2)}) async-start(f32[32,2,1280]{2,1,0:T(2,128)} %get-tuple-element.33), calls=%async_computation | async-start | bytes 655360 | tf_op jit(solution)/shard_map/all_to_all | solution.py:433
  17.6 0.0 copy-start.17
  17.6 7.0 %noise.3.tie_ref.refs_0_ = f32[2,128,2560]{2,1,0:T(8,128)S(1)} custom-call(bf16[3,128,4096]{2,1,0:T(8,128)(2,1)} %bitcast.20, f32[2,1280]{1,0:T(2,128)} %get-tuple-element.31.tie_ref.own_ref), custom_call_target="tpu_custom_call" | custom-call | flops 268435456 | bytes 1048576 | tf_op jit(solution)/shard_map/noise/pallas_call | solution.py:84
  24.6 1.5 copy-done
  26.1 0.0 copy-start.9
  26.1 0.0 copy-start.16
  26.1 0.0 copy-start.22
  26.1 1.1 all-to-all-done.parts_ref
  27.2 0.3 refit.3
  27.5 24.3 %all_to_all.45.peak_ref = f32[16,1,128]{2,1,0:T(1,128)S(1)} all-to-all(f32[16,1,128]{2,1,0:T(1,128)S(1)} %get-tuple-element.35), channel_id=1, replica_groups=mesh['env'=16,'cand'=32] {'env'}, dimensions={0} | all-to-all | bytes 16384 | tf_op jit(solution)/shard_map/all_to_all | solution.py:441
  51.8 0.8 to_all.3
  52.6 7.8 %all-to-all-start.2 = ((f32[32,2,1408]{2,1,0:T(2,128)}), f32[32,2,1408]{2,1,0:T(2,128)S(1)}, u32[]{:S(2)}, u32[]{:S(2)}) async-start(f32[32,2,1408]{2,1,0:T(2,128)} %get-tuple-element.37), calls=%async_computation.2 | async-start | bytes 720896 | tf_op jit(solution)/shard_map/all_to_all | solution.py:443
  60.4 0.0 copy-start.14
  60.5 8.5 %rollout.5.refs_3_.refs_1_ = f32[2,128,128]{2,1,0:T(8,128)} custom-call(bf16[128,2560]{1,0:T(8,128)(2,1)} %get-tuple-element.32.refs_0_, f32[16,128]{1,0:T(8,128)S(1)} %copy-done.8, f32[16,128]{1,0:T(8,128)S(1)} %copy-done.9, bf16[128,512]{1,0:T(8,128)(2,1)S(1)} %copy-done.2, bf16[64,512]{1,0:T(8,128)(2,1)S(1)} %copy-done.4, bf16[512,128]{1,0:T(8,128)(2,1)S(1)} %copy-done.3, ...), custom_call_target="tpu_custom_call" | custom-call | flops 268435456 | bytes 1048576 | tf_op jit(solution)/shard_map/rollout/pallas_call | solution.py:359
  69.0 0.0 copy-start.6
  69.0 1.2 all-to-all-done.2.refs_4_
  70.2 2.6 %actions.4 = (bf16[128,2560]{1,0:T(8,128)(2,1)}, f32[128,128]{1,0:T(8,128)}, f32[32,2,1280]{2,1,0:T(2,128)}, f32[2,1280]{1,0:T(2,128)}) custom-call(f32[2,128,2560]{2,1,0:T(8,128)S(1)} %copy-done.1, s32[3,16,25]{2,1,0:T(8,128)S(1)} %bitcast.7, s32[1]{0:T(128)} %bitcast.1.tie_ref.refs_2_.refs_3_, f32[2,128,128]{2,1,0:T(8,128)} %rollout.5.refs_3_.refs_1_, ...), custom_call_target="tpu_custom_call" | custom-call | tf_op jit(solution)/shard_map/actions/pallas_call | solution.py:170
  72.8 6.2 %all-to-all-start.3 = ((f32[32,2,1280]{2,1,0:T(2,128)}), f32[32,2,1280]{2,1,0:T(2,128)S(1)}, u32[]{:S(2)}, u32[]{:S(2)}) async-start(f32[32,2,1280]{2,1,0:T(2,128)} %get-tuple-element.39), calls=%async_computation.3 | async-start | bytes 655360 | tf_op jit(solution)/shard_map/all_to_all | solution.py:433
  79.0 7.3 %rollout.6.tie_ref.refs_10_ = f32[1,8,16]{2,1,0:T(8,128)} custom-call(bf16[128,2560]{1,0:T(8,128)(2,1)} %get-tuple-element.32.refs_0_, f32[2,128,128]{2,1,0:T(8,128)S(1)} %copy-done.6, f32[128,128]{1,0:T(8,128)S(1)} %copy-done.14, f32[16,128]{1,0:T(8,128)S(1)} %copy-done.8, f32[16,128]{1,0:T(8,128)S(1)} %copy-done.9, bf16[128,512]{1,0:T(8,128)(2,1)S(1)} %copy-done.2, ...), custom_call_target="tpu_custom_call" | custom-call | flops 268435456 | bytes 1048576 | tf_op jit(solution)/shard_map/rollout/pallas_call | solution.py:359
  86.3 2.2 %all-to-all-done.3.parts_ref = f32[32,2,1280]{2,1,0:T(2,128)S(1)} async-done(((f32[32,2,1280]{2,1,0:T(2,128)}), f32[32,2,1280]{2,1,0:T(2,128)S(1)}, u32[]{:S(2)}, u32[]{:S(2)}) %all-to-all-start.3) | async-done | bytes 327712 | tf_op jit(solution)/shard_map/all_to_all | solution.py:433
  88.5 0.7 copy-done.18
  89.2 0.3 refit.4
  89.5 14.0 %all_to_all.46.peak_ref = f32[16,1,128]{2,1,0:T(1,128)S(1)} all-to-all(f32[16,1,128]{2,1,0:T(1,128)S(1)} %get-tuple-element.43), channel_id=1, replica_groups=mesh['env'=16,'cand'=32] {'env'}, dimensions={0} | all-to-all | bytes 16384 | tf_op jit(solution)/shard_map/all_to_all | solution.py:441
  103.5 0.8 to_all.4
  104.2 6.3 %all-to-all-start.5 = ((f32[32,2,1408]{2,1,0:T(2,128)}), f32[32,2,1408]{2,1,0:T(2,128)S(1)}, u32[]{:S(2)}, u32[]{:S(2)}) async-start(f32[32,2,1408]{2,1,0:T(2,128)} %get-tuple-element.45), calls=%async_computation.5 | async-start | bytes 720896 | tf_op jit(solution)/shard_map/all_to_all | solution.py:443
  110.6 8.6 %rollout.7.refs_3_.refs_2_ = f32[2,128,128]{2,1,0:T(8,128)} custom-call(bf16[128,2560]{1,0:T(8,128)(2,1)} %get-tuple-element.38.refs_0_, f32[16,128]{1,0:T(8,128)S(1)} %copy-done.8, f32[16,128]{1,0:T(8,128)S(1)} %copy-done.9, bf16[128,512]{1,0:T(8,128)(2,1)S(1)} %copy-done.2, bf16[64,512]{1,0:T(8,128)(2,1)S(1)} %copy-done.4, bf16[512,128]{1,0:T(8,128)(2,1)S(1)} %copy-done.3, ...), custom_call_target="tpu_custom_call" | custom-call | flops 268435456 | bytes 1048576 | tf_op jit(solution)/shard_map/rollout/pallas_call | solution.py:359
  119.2 0.0 copy-start.5
  119.2 1.2 all-to-all-done.5.refs_4_
  120.4 2.6 %actions.5 = (bf16[128,2560]{1,0:T(8,128)(2,1)}, f32[128,128]{1,0:T(8,128)}, f32[32,2,1280]{2,1,0:T(2,128)}, f32[2,1280]{1,0:T(2,128)}) custom-call(f32[2,128,2560]{2,1,0:T(8,128)S(1)} %copy-done.1, s32[3,16,25]{2,1,0:T(8,128)S(1)} %bitcast.8, s32[1]{0:T(128)} %bitcast.1.tie_ref.refs_2_.refs_3_, f32[2,128,128]{2,1,0:T(8,128)} %rollout.7.refs_3_.refs_2_, ...), custom_call_target="tpu_custom_call" | custom-call | tf_op jit(solution)/shard_map/actions/pallas_call | solution.py:170
  123.0 0.0 copy-start.15
  123.0 6.3 %all-to-all-start.6 = ((f32[32,2,1280]{2,1,0:T(2,128)}), f32[32,2,1280]{2,1,0:T(2,128)S(1)}, u32[]{:S(2)}, u32[]{:S(2)}) async-start(f32[32,2,1280]{2,1,0:T(2,128)} %get-tuple-element.46), calls=%async_computation.6 | async-start | bytes 655360 | tf_op jit(solution)/shard_map/all_to_all | solution.py:433
  129.4 0.0 copy-start.23
  129.4 0.6 copy-done.23
  130.0 7.8 %rollout.8 = (f32[1,8,16]{2,1,0:T(8,128)}, f32[2,128,128]{2,1,0:T(8,128)}) custom-call(bf16[128,2560]{1,0:T(8,128)(2,1)} %get-tuple-element.38.refs_0_, bf16[128,2560]{1,0:T(8,128)(2,1)} %get-tuple-element.48.refs_1_.refs_0_, f32[2,128,128]{2,1,0:T(8,128)S(1)} %copy-done.5, f32[128,128]{1,0:T(8,128)S(1)} %copy-done.13, f32[16,128]{1,0:T(8,128)S(1)} %copy-done.8, ...), custom_call_target="tpu_custom_call" | custom-call | flops 268435456 | bytes 1048576 | tf_op jit(solution)/shard_map/rollout/pallas_call | solution.py:359
  137.9 1.0 all-to-all-done.6.parts_ref
  138.8 0.7 copy-done.19
  139.6 0.3 refit.5
  139.8 13.8 %all_to_all.47.peak_ref = f32[16,1,128]{2,1,0:T(1,128)S(1)} all-to-all(f32[16,1,128]{2,1,0:T(1,128)S(1)} %get-tuple-element.52), channel_id=1, replica_groups=mesh['env'=16,'cand'=32] {'env'}, dimensions={0} | all-to-all | bytes 16384 | tf_op jit(solution)/shard_map/all_to_all | solution.py:441
  153.7 0.8 to_all.5
  154.4 7.5 %all-to-all-start.8 = ((f32[32,2,1408]{2,1,0:T(2,128)}), f32[32,2,1408]{2,1,0:T(2,128)S(1)}, u32[]{:S(2)}, u32[]{:S(2)}) async-start(f32[32,2,1408]{2,1,0:T(2,128)} %get-tuple-element.53), calls=%async_computation.8 | async-start | bytes 720896 | tf_op jit(solution)/shard_map/all_to_all | solution.py:443
  162.0 0.0 copy-start.12
  162.0 0.9 copy-done.12
  162.9 0.7 copy-done.21
  163.5 8.6 %rollout.9 = f32[3,8,16]{2,1,0:T(8,128)} custom-call(bf16[128,2560]{1,0:T(8,128)(2,1)} %get-tuple-element.48.refs_1_.refs_0_, f32[2,128,128]{2,1,0:T(8,128)S(1)} %copy-done.12, f32[128,128]{1,0:T(8,128)S(1)} %copy-done.15, f32[16,128]{1,0:T(8,128)S(1)} %copy-done.8, f32[16,128]{1,0:T(8,128)S(1)} %copy-done.9, bf16[128,512]{1,0:T(8,128)(2,1)S(1)} %copy-done.2, ...), custom_call_target="tpu_custom_call" | custom-call | flops 268435456 | bytes 1048576 | tf_op jit(solution)/shard_map/rollout/pallas_call | solution.py:359
  172.1 0.0 all-to-all-done.8.state_ref
  172.1 0.8 finished.1
  (32 shorter events, 0.1 us)
Async XLA Ops:
  0.6 4.2 %copy-start.7 = (s32[16,3,25]{2,0,1:T(8,128)S(1)}, s32[16,3,25]{2,0,1:T(8,128)}, u32[]{:S(2)}) copy-start(s32[16,3,25]{2,0,1:T(8,128)} %param.21) | copy-start | bytes 14404
  0.6 4.2 %copy-start.11 = (f32[16,2560]{1,0:T(8,128)S(1)}, f32[16,2560]{1,0:T(8,128)}, u32[]{:S(2)}) copy-start(f32[16,2560]{1,0:T(8,128)} %refs_5_.6) | copy-start | bytes 491524
  0.7 4.2 %copy-start.10 = (f32[16,2560]{1,0:T(8,128)S(1)}, f32[16,2560]{1,0:T(8,128)}, u32[]{:S(2)}) copy-start(f32[16,2560]{1,0:T(8,128)} %refs_4_.6) | copy-start | bytes 491524
  7.2 20.0 %all-to-all-start = ((f32[32,2,1280]{2,1,0:T(2,128)}), f32[32,2,1280]{2,1,0:T(2,128)S(1)}, u32[]{:S(2)}, u32[]{:S(2)}) async-start(f32[32,2,1280]{2,1,0:T(2,128)} %get-tuple-element.33), calls=%async_computation | async-start | bytes 655360 | tf_op jit(solution)/shard_map/all_to_all | solution.py:433
  17.6 9.6 %copy-start.17 = (f32[2,1280]{1,0:T(2,128)S(1)}, f32[2,1280]{1,0:T(2,128)}, u32[]{:S(2)}) copy-start(f32[2,1280]{1,0:T(2,128)} %get-tuple-element.31.tie_ref.own_ref) | copy-start | bytes 30724
  24.6 1.5 copy-start
  26.1 34.3 %copy-start.2 = (bf16[128,512]{1,0:T(8,128)(2,1)S(1)}, bf16[128,512]{1,0:T(8,128)(2,1)}, u32[]{:S(2)}) copy-start(bf16[128,512]{1,0:T(8,128)(2,1)} %refs_5_.11) | copy-start | bytes 393220
  26.1 34.3 %copy-start.3 = (bf16[512,128]{1,0:T(8,128)(2,1)S(1)}, bf16[512,128]{1,0:T(8,128)(2,1)}, u32[]{:S(2)}) copy-start(bf16[512,128]{1,0:T(8,128)(2,1)} %refs_7_.5) | copy-start | bytes 393220
  26.1 34.3 %copy-start.4 = (bf16[64,512]{1,0:T(8,128)(2,1)S(1)}, bf16[64,512]{1,0:T(8,128)(2,1)}, u32[]{:S(2)}) copy-start(bf16[64,512]{1,0:T(8,128)(2,1)} %refs_6_.5) | copy-start | bytes 196612
  26.1 34.3 %copy-start.8 = (f32[16,128]{1,0:T(8,128)S(1)}, f32[16,128]{1,0:T(8,128)}, u32[]{:S(2)}) copy-start(f32[16,128]{1,0:T(8,128)} %refs_3_.7) | copy-start | bytes 24580
  26.1 34.3 %copy-start.9 = (f32[16,128]{1,0:T(8,128)S(1)}, f32[16,128]{1,0:T(8,128)}, u32[]{:S(2)}) copy-start(f32[16,128]{1,0:T(8,128)} %refs_4_.11) | copy-start | bytes 24580
  26.1 34.3 %copy-start.16 = (f32[512]{0:T(512)S(1)}, f32[512]{0:T(512)}, u32[]{:S(2)}) copy-start(f32[512]{0:T(512)} %param.19) | copy-start | bytes 6148
  26.1 34.3 %copy-start.22 = (f32[128]{0:T(128)S(1)}, f32[128]{0:T(128)}, u32[]{:S(2)}) copy-start(f32[128]{0:T(128)} %param.20) | copy-start | bytes 1540
  27.2 43.0 %copy-start.1 = (f32[2,128,2560]{2,1,0:T(8,128)S(1)}, f32[2,128,2560]{2,1,0:T(8,128)}, u32[]{:S(2)}) copy-start(f32[2,128,2560]{2,1,0:T(8,128)} %copy-done) | copy-start | bytes 7864324
  52.6 17.6 %all-to-all-start.2 = ((f32[32,2,1408]{2,1,0:T(2,128)}), f32[32,2,1408]{2,1,0:T(2,128)S(1)}, u32[]{:S(2)}, u32[]{:S(2)}) async-start(f32[32,2,1408]{2,1,0:T(2,128)} %get-tuple-element.37), calls=%async_computation.2 | async-start | bytes 720896 | tf_op jit(solution)/shard_map/all_to_all | solution.py:443
  60.4 18.6 %copy-start.14 = (f32[128,128]{1,0:T(8,128)S(1)}, f32[128,128]{1,0:T(8,128)}, u32[]{:S(2)}) copy-start(f32[128,128]{1,0:T(8,128)} %get-tuple-element.41.refs_2_) | copy-start | bytes 196612
  69.0 10.0 %copy-start.6 = (f32[2,128,128]{2,1,0:T(8,128)S(1)}, f32[2,128,128]{2,1,0:T(8,128)}, u32[]{:S(2)}) copy-start(f32[2,128,128]{2,1,0:T(8,128)} %rollout.5.refs_3_.refs_1_) | copy-start | bytes 393220
  72.8 15.7 %all-to-all-start.3 = ((f32[32,2,1280]{2,1,0:T(2,128)}), f32[32,2,1280]{2,1,0:T(2,128)S(1)}, u32[]{:S(2)}, u32[]{:S(2)}) async-start(f32[32,2,1280]{2,1,0:T(2,128)} %get-tuple-element.39), calls=%async_computation.3 | async-start | bytes 655360 | tf_op jit(solution)/shard_map/all_to_all | solution.py:433
  88.5 0.7 copy-start.18
  104.2 16.1 %all-to-all-start.5 = ((f32[32,2,1408]{2,1,0:T(2,128)}), f32[32,2,1408]{2,1,0:T(2,128)S(1)}, u32[]{:S(2)}, u32[]{:S(2)}) async-start(f32[32,2,1408]{2,1,0:T(2,128)} %get-tuple-element.45), calls=%async_computation.5 | async-start | bytes 720896 | tf_op jit(solution)/shard_map/all_to_all | solution.py:443
  110.6 18.8 %copy-start.13 = (f32[128,128]{1,0:T(8,128)S(1)}, f32[128,128]{1,0:T(8,128)}, u32[]{:S(2)}) copy-start(f32[128,128]{1,0:T(8,128)} %get-tuple-element.49.refs_3_) | copy-start | bytes 196612
  119.2 10.2 %copy-start.5 = (f32[2,128,128]{2,1,0:T(8,128)S(1)}, f32[2,128,128]{2,1,0:T(8,128)}, u32[]{:S(2)}) copy-start(f32[2,128,128]{2,1,0:T(8,128)} %rollout.7.refs_3_.refs_2_) | copy-start | bytes 393220
  119.2 42.8 %copy-start.20 = (f32[1,8,16]{2,1,0:T(8,128)S(1)}, f32[1,8,16]{2,1,0:T(8,128)}, u32[]{:S(2)}) copy-start(f32[1,8,16]{2,1,0:T(8,128)} %rollout.6.tie_ref.refs_10_) | copy-start | bytes 1540
  123.0 39.0 %copy-start.15 = (f32[128,128]{1,0:T(8,128)S(1)}, f32[128,128]{1,0:T(8,128)}, u32[]{:S(2)}) copy-start(f32[128,128]{1,0:T(8,128)} %get-tuple-element.57.refs_2_) | copy-start | bytes 196612
  123.0 15.8 %all-to-all-start.6 = ((f32[32,2,1280]{2,1,0:T(2,128)}), f32[32,2,1280]{2,1,0:T(2,128)S(1)}, u32[]{:S(2)}, u32[]{:S(2)}) async-start(f32[32,2,1280]{2,1,0:T(2,128)} %get-tuple-element.46), calls=%async_computation.6 | async-start | bytes 655360 | tf_op jit(solution)/shard_map/all_to_all | solution.py:433
  129.4 0.7 copy-start.23
  138.8 0.7 copy-start.19
  154.4 17.7 %all-to-all-start.8 = ((f32[32,2,1408]{2,1,0:T(2,128)}), f32[32,2,1408]{2,1,0:T(2,128)S(1)}, u32[]{:S(2)}, u32[]{:S(2)}) async-start(f32[32,2,1408]{2,1,0:T(2,128)} %get-tuple-element.53), calls=%async_computation.8 | async-start | bytes 720896 | tf_op jit(solution)/shard_map/all_to_all | solution.py:443
  162.0 0.9 copy-start.12
  162.9 0.7 copy-start.21

commit v4 on v3

--- a/solution.py
+++ b/solution.py
@@ -14,7 +14,6 @@
 ACT_COST = 0.1
 LANES = 128
 ROLL_FLOPS = 1 << 28
-CUT = 22
 VMEM = pl.BlockSpec(memory_space=pltpu.VMEM)
 SMEM = pl.BlockSpec(memory_space=pltpu.SMEM)
 HBM = pl.BlockSpec(memory_space=pltpu.HBM)
@@ -40,7 +39,7 @@
     return np.asarray(kernel, np.float32).astype(jnp.bfloat16).astype(np.float32)
 
 
-def noise_body(white_ref, tie_ref, out_ref, rows_in, fill, sems, *, act_dim, blocks, first, parts):
+def noise_body(white_ref, tie_ref, out_ref, token_ref, rows_in, fill, sems, *, act_dim, blocks, first, parts):
     count = out_ref.shape[0]
     _, rows, flat = white_ref.shape
     length = flat // act_dim
@@ -75,6 +74,7 @@
             out_ref[one, :, pl.ds(block * 256, 256)] = jnp.dot(
                 rows_in[one], fill[pl.ds(start, flat), :], preferred_element_type=jnp.float32
             )
+    token_ref[...] = out_ref[count - 1, pl.ds(0, 8), pl.ds(0, LANES)]
 
 
 def noise_of(white, first, count, tie, act_dim, horizon):
@@ -85,9 +85,13 @@
         functools.partial(
             noise_body, act_dim=act_dim, blocks=width // 256, first=first, parts=parts
         ),
+        grid=(1,),
         in_specs=[HBM, HBM],
-        out_specs=VMEM,
-        out_shape=jax.ShapeDtypeStruct((count, rows, width), jnp.float32),
+        out_specs=[VMEM, whole((8, LANES))],
+        out_shape=[
+            jax.ShapeDtypeStruct((count, rows, width), jnp.float32),
+            in_hbm((8, LANES)),
+        ],
         scratch_shapes=[
             pltpu.VMEM((count, rows, flat), jnp.bfloat16),
             pltpu.VMEM((2 * flat, 256), jnp.bfloat16),
@@ -113,7 +117,7 @@
         noise_ref, elite_ref, mine_ref, tie_ref, mean_ref, std_ref = refs[:6]
     else:
         noise_ref, elite_ref, mine_ref, tie_ref, state_ref = refs[:5]
-    acts_out, asq_ref, sums_ref, own_ref, acts_ref, sems = refs[-6:]
+    acts_out, asq_out, sums_out, own_out, acts_ref, asq_ref, sums_ref, own_ref, sems = refs[-9:]
     half = sums_ref.shape[2]
     rows = acts_ref.shape[0]
     envs = sums_ref.shape[0] // 2
@@ -132,7 +136,17 @@
 
     def send(part):
         at = pl.ds(part * per * cands, per * cands)
-        return pltpu.make_async_copy(acts_ref.at[at, :], acts_out.at[at, :], sems.at[part])
+        pair = pl.ds(part * per * 2, per * 2)
+        trio = ((acts_ref, acts_out, at), (asq_ref, asq_out, at), (sums_ref, sums_out, pair))
+        return [
+            pltpu.make_async_copy(source.at[rows], target.at[rows], sems.at[3 * part + k])
+            for k, (source, target, rows) in enumerate(trio)
+        ]
+
+    def send_own():
+        return pltpu.make_async_copy(own_ref, own_out, sems.at[3 * (envs // per)])
+
+    send_own().start()
 
     ids = me * cands + lax.broadcasted_iota(jnp.int32, (cands, 1), 0)
     for env in range(envs):
@@ -160,9 +174,12 @@
                 sums_ref[line, 1:2, lanes] = jnp.sum(both * member, axis=0, keepdims=True)
         asq_ref[at, :] = square
         if env % per == per - 1:
-            send(env // per).start()
+            for copy in send(env // per):
+                copy.start()
     for part in range(envs // per):
-        send(part).wait()
+        for copy in send(part):
+            copy.wait()
+    send_own().wait()
 
 
 def actions_of(noise, at, elite_idx, mine, tie, state, it, envs_total, lines, half):
@@ -172,7 +189,7 @@
         grid=(1,),
         in_specs=[pl.BlockSpec((1, rows, width), lambda i: (at, 0, 0)), VMEM, SMEM, HBM]
         + [VMEM] * len(state),
-        out_specs=[HBM, whole((rows, LANES)), whole((lines, 2, half)), whole((2, half))],
+        out_specs=[HBM] * 4,
         out_shape=[
             in_hbm((rows, width), jnp.bfloat16),
             in_hbm((rows, LANES)),
@@ -181,15 +198,21 @@
         ],
         scratch_shapes=[
             pltpu.VMEM((rows, width), jnp.bfloat16),
-            pltpu.SemaphoreType.DMA((lines // 8,)),
+            pltpu.VMEM((rows, LANES), jnp.float32),
+            pltpu.VMEM((lines, 2, half), jnp.float32),
+            pltpu.VMEM((2, half), jnp.float32),
+            pltpu.SemaphoreType.DMA((3 * (lines // 8) + 1,)),
         ],
         compiler_params=pltpu.CompilerParams(vmem_limit_bytes=12 << 20),
         name="actions",
     )(noise, elite_idx, mine, stay(tie), *state)
 
 
-def refit_body(parts_ref, own_ref, tie_ref, slice_ref, peak_ref, *, elites):
+def refit_body(parts_ref, own_hbm, tie_ref, slice_ref, peak_ref, own_ref, sem, *, elites):
+    copy = pltpu.make_async_copy(own_hbm, own_ref, sem)
+    copy.start()
     total = jnp.sum(parts_ref[...], axis=0)
+    copy.wait()
     mean = total[0:1] / elites
     variance = jnp.maximum(total[1:2] / elites - mean * mean, 0.0)
     slice_ref[0:1, :] = MOMENTUM * own_ref[0:1, :] + (1.0 - MOMENTUM) * mean
@@ -201,15 +224,16 @@
 def refit(parts, own, tie, elites, groups):
     return pl.pallas_call(
         functools.partial(refit_body, elites=elites),
-        in_specs=[VMEM, VMEM, HBM],
+        in_specs=[VMEM, HBM, HBM],
         out_specs=[VMEM, VMEM],
         out_shape=[
             jax.ShapeDtypeStruct(own.shape, jnp.float32),
             jax.ShapeDtypeStruct((groups, 1, LANES), jnp.float32),
         ],
+        scratch_shapes=[pltpu.VMEM(own.shape, jnp.float32), pltpu.SemaphoreType.DMA],
         compiler_params=pltpu.CompilerParams(vmem_limit_bytes=4 << 20),
         name="refit",
-    )(parts, own, stay(tie))
+    )(parts, stay(own), stay(tie))
 
 
 def spread_body(slice_ref, peak_ref, out_ref, token_ref):
@@ -403,13 +427,12 @@
     envs_total = envs * groups
     rows = envs * cands
     assert lines == peers and rows % 16 == 0
-    assert iters == 3
+    assert iters == 3 and horizon == 40
     mine = lax.axis_index("cand").astype(jnp.int32)[None]
     fixed = (init_state, goal_state, w_state, w_action, w_out, bias_in[None], bias_out[None])
     white = white.reshape(iters, rows, flat)
     elite_idx = jnp.swapaxes(elite_idx, 0, 1)
     mix = functools.partial(lax.all_to_all, axis_name="cand", split_axis=0, concat_axis=0, tiled=True)
-    cut = min(CUT, horizon)
     acts, asq, held, costs = {}, {}, {}, {}
 
     def part(it, first, last):
@@ -424,7 +447,7 @@
                 costs[it] = out
         return outs[0]
 
-    noise = noise_of(white, 0, 1, mine, act_dim, horizon)
+    noise, _ = noise_of(white, 0, 1, mine, act_dim, horizon)
     state, tie = (mean_init, std_init), mine
     for it in range(iters):
         acts[it], asq[it], sums, own = actions_of(
@@ -432,19 +455,21 @@
         )
         parts = mix(sums)
         if it == 0:
-            tie = noise = noise_of(white, 1, iters - 1, own, act_dim, horizon)
+            noise, tie = noise_of(white, 1, iters - 1, own, act_dim, horizon)
         elif it == 1:
-            tie = play([(0, cut, horizon)], own)
+            tie = play([(0, 14, 26), (1, 0, 12)], own)
         else:
-            tie = play([(1, cut, horizon), (2, 0, horizon - cut)], own)
+            tie = play([(1, 26, horizon), (2, 0, 14)], own)
         piece, peak = refit(parts, own, tie, elites, groups)
         peaks = lax.all_to_all(peak, "env", 0, 0, tiled=True)
         spread, token = to_all(piece, peaks, lines)
         state = (mix(spread),)
-        if it < iters - 1:
-            tie = play([(it, 0, cut)], token)
+        if it == 0:
+            tie = play([(0, 0, 14)], token)
+        elif it == 1:
+            tie = play([(0, 26, horizon), (1, 12, 26)], token)
         else:
-            tie = play([(2, horizon - cut, horizon)], token, (costs[0], costs[1]))
+            tie = play([(2, 14, horizon)], token, (costs[0], costs[1]))
     mean, std = finished(state[0], envs, width, envs_total)
     return (mean, std, jnp.swapaxes(costs[iters - 1], 1, 2))
 

time: 174 us -> 168 us (0.966)
  waiting for transfers between devices: 6.62 us -> 13.2 us
  Pallas kernels: 63.5 us -> 57 us
  starting transfers between devices: 44.6 us -> 38.5 us
    pallas_call x5, Pallas kernels: 40.8 us -> 34.7 us  [rollout(): pl.pallas_call(functools.partial(rollout_body, spans=spans, act_dim=act_d...]
    all_to_all x3, waiting for transfers between devices: 4.23 us -> 8.69 us  [shards(): parts = mix(sums)]
    all_to_all x3, starting transfers between devices: 21.6 us -> 17.3 us  [shards(): state = (mix(spread),)]
    all_to_all x3, waiting for transfers between devices: 2.4 us -> 4.48 us  [shards(): state = (mix(spread),)]
    pallas_call x3, Pallas kernels: 7.49 us -> 5.56 us  [actions_of(): pl.pallas_call(functools.partial(action_body, it=it, envs_total=envs_tota...]
    unnamed x48 -> x42, local copies, waits for them, and re-layouts: 5.17 us -> 4.95 us
  transfers between devices with their start and end apart: 6 -> 6, of which waited for: 5 -> 5; matrix products, arithmetic and copies ran while one was open for 0% -> 0% of each run, Pallas kernels for 28% -> 25%
where the time goes in v4:
time: 168 us; the launch traced here: 167 us
  Pallas kernels  57 us (34%)
  blocking collectives  51.9 us (31%)
  starting transfers between devices  38.5 us (23%)
  waiting for transfers between devices  13.2 us (8%)
  local copies, waits for them, and re-layouts  4.95 us (3%)
    all_to_all x3, blocking collectives, shards(): peaks = lax.all_to_all(peak, 'env', 0, 0, tiled=True)  51.9 us
    pallas_call x5, Pallas kernels, rollout(): pl.pallas_call(functools.partial(rollout_body, spans=spans, act_dim=act_d...  34.7 us
    all_to_all x3, starting transfers between devices, shards(): parts = mix(sums)  21.3 us
    all_to_all x3, starting transfers between devices, shards(): state = (mix(spread),)  17.3 us
    pallas_call x2, Pallas kernels, noise_of(): pl.pallas_call(functools.partial(noise_body, act_dim=act_dim, blocks=widt...  11.2 us
    all_to_all x3, waiting for transfers between devices, shards(): parts = mix(sums)  8.69 us
    pallas_call x3, Pallas kernels, actions_of(): pl.pallas_call(functools.partial(action_body, it=it, envs_total=envs_tota...  5.56 us
    unnamed x42, local copies, waits for them, and re-layouts  4.95 us
  transfers between devices with their start and end apart: 6, of which 5 were waited for; matrix products, arithmetic and copies ran while one was open for 0% of the time, Pallas kernels for 25%

profile of v4, /device:TPU:1, one launch (start us, length us, event | category | flops | bytes accessed | tf_op | source)
XLA Modules:
  0.0 166.6 jit_solution(13240114152049730000)
XLA Ops:
  0.7 4.2 %noise.2 = (f32[1,128,2560]{2,1,0:T(8,128)S(1)}, f32[8,128]{1,0:T(8,128)}) custom-call(bf16[3,128,4096]{2,1,0:T(8,128)(2,1)} %bitcast.19, s32[1]{0:T(128)} %bitcast.1.tie_ref.refs_2_.refs_3_), custom_call_target="tpu_custom_call" | custom-call | flops 268435456 | bytes 1048576 | tf_op jit(solution)/shard_map/noise/pallas_call | solution.py:84
  4.9 1.7 %actions.3 = (bf16[128,2560]{1,0:T(8,128)(2,1)}, f32[128,128]{1,0:T(8,128)}, f32[32,2,1280]{2,1,0:T(2,128)}, f32[2,1280]{1,0:T(2,128)}) custom-call(f32[1,128,2560]{2,1,0:T(8,128)S(1)} %get-tuple-element.38.refs_0_, s32[3,16,25]{2,1,0:T(8,128)S(1)} %bitcast.6, s32[1]{0:T(128)} %bitcast.1.tie_ref.refs_2_.refs_3_, s32[1]{0:T(128)} %bitcast.1.tie_ref.refs_2_.refs_3_, ...), custom_call_target="tpu_custom_call" | custom-call | tf_op jit(solution)/shard_map/actions/pallas_call | solution.py:187
  6.6 0.0 copy-start
  6.6 0.0 copy-start.1
  6.6 0.0 copy-start.2
  6.6 0.0 copy-start.6
  6.6 0.0 copy-start.16
  6.7 0.0 copy-start.19
  6.7 10.5 %all-to-all-start = ((f32[32,2,1280]{2,1,0:T(2,128)}), f32[32,2,1280]{2,1,0:T(2,128)S(1)}, u32[]{:S(2)}, u32[]{:S(2)}) async-start(f32[32,2,1280]{2,1,0:T(2,128)} %get-tuple-element.42), calls=%async_computation | async-start | bytes 655360 | tf_op jit(solution)/shard_map/all_to_all | solution.py:456
  17.2 7.0 %noise.3 = (f32[2,128,2560]{2,1,0:T(8,128)S(1)}, f32[8,128]{1,0:T(8,128)}) custom-call(bf16[3,128,4096]{2,1,0:T(8,128)(2,1)} %bitcast.20, f32[2,1280]{1,0:T(2,128)} %get-tuple-element.39.tie_ref.own_hbm), custom_call_target="tpu_custom_call" | custom-call | flops 268435456 | bytes 1048576 | tf_op jit(solution)/shard_map/noise/pallas_call | solution.py:84
  24.2 2.6 %all-to-all-done.parts_ref = f32[32,2,1280]{2,1,0:T(2,128)S(1)} async-done(((f32[32,2,1280]{2,1,0:T(2,128)}), f32[32,2,1280]{2,1,0:T(2,128)S(1)}, u32[]{:S(2)}, u32[]{:S(2)}) %all-to-all-start) | async-done | bytes 327712 | tf_op jit(solution)/shard_map/all_to_all | solution.py:456
  26.8 0.8 refit.3
  27.6 24.2 %all_to_all.45.peak_ref = f32[16,1,128]{2,1,0:T(1,128)S(1)} all-to-all(f32[16,1,128]{2,1,0:T(1,128)S(1)} %get-tuple-element.45), channel_id=1, replica_groups=mesh['env'=16,'cand'=32] {'env'}, dimensions={0} | all-to-all | bytes 16384 | tf_op jit(solution)/shard_map/all_to_all | solution.py:464
  51.8 0.8 to_all.3
  52.6 6.3 %all-to-all-start.2 = ((f32[32,2,1408]{2,1,0:T(2,128)}), f32[32,2,1408]{2,1,0:T(2,128)S(1)}, u32[]{:S(2)}, u32[]{:S(2)}) async-start(f32[32,2,1408]{2,1,0:T(2,128)} %get-tuple-element.47), calls=%async_computation.2 | async-start | bytes 720896 | tf_op jit(solution)/shard_map/all_to_all | solution.py:466
  59.0 6.0 %rollout.5.refs_3_.refs_2_ = f32[2,128,128]{2,1,0:T(8,128)} custom-call(bf16[128,2560]{1,0:T(8,128)(2,1)} %get-tuple-element.41.refs_0_, f32[16,128]{1,0:T(8,128)S(1)} %copy-done.6, f32[16,128]{1,0:T(8,128)S(1)} %copy-done.7, bf16[128,512]{1,0:T(8,128)(2,1)S(1)} %copy-done, bf16[64,512]{1,0:T(8,128)(2,1)S(1)} %copy-done.2, bf16[512,128]{1,0:T(8,128)(2,1)S(1)} %copy-done.1, ...), custom_call_target="tpu_custom_call" | custom-call | flops 268435456 | bytes 1048576 | tf_op jit(solution)/shard_map/rollout/pallas_call | solution.py:383
  65.0 0.0 copy-start.3
  65.0 3.7 %all-to-all-done.2.refs_4_ = f32[32,2,1408]{2,1,0:T(2,128)S(1)} async-done(((f32[32,2,1408]{2,1,0:T(2,128)}), f32[32,2,1408]{2,1,0:T(2,128)S(1)}, u32[]{:S(2)}, u32[]{:S(2)}) %all-to-all-start.2) | async-done | bytes 360480 | tf_op jit(solution)/shard_map/all_to_all | solution.py:466
  68.7 1.9 %actions.4 = (bf16[128,2560]{1,0:T(8,128)(2,1)}, f32[128,128]{1,0:T(8,128)}, f32[32,2,1280]{2,1,0:T(2,128)}, f32[2,1280]{1,0:T(2,128)}) custom-call(f32[2,128,2560]{2,1,0:T(8,128)S(1)} %get-tuple-element.40.refs_0_, s32[3,16,25]{2,1,0:T(8,128)S(1)} %bitcast.7, s32[1]{0:T(128)} %bitcast.1.tie_ref.refs_2_.refs_3_, f32[2,128,128]{2,1,0:T(8,128)} %rollout.5.refs_3_.refs_2_, ...), custom_call_target="tpu_custom_call" | custom-call | tf_op jit(solution)/shard_map/actions/pallas_call | solution.py:187
  70.6 3.9 %all-to-all-start.3 = ((f32[32,2,1280]{2,1,0:T(2,128)}), f32[32,2,1280]{2,1,0:T(2,128)S(1)}, u32[]{:S(2)}, u32[]{:S(2)}) async-start(f32[32,2,1280]{2,1,0:T(2,128)} %get-tuple-element.53), calls=%async_computation.3 | async-start | bytes 655360 | tf_op jit(solution)/shard_map/all_to_all | solution.py:456
  74.5 5.8 %rollout.6 = (f32[2,128,128]{2,1,0:T(8,128)}, f32[2,128,128]{2,1,0:T(8,128)}) custom-call(bf16[128,2560]{1,0:T(8,128)(2,1)} %get-tuple-element.41.refs_0_, bf16[128,2560]{1,0:T(8,128)(2,1)} %get-tuple-element.48.refs_1_.refs_0_, f32[2,128,128]{2,1,0:T(8,128)S(1)} %copy-done.3, f32[16,128]{1,0:T(8,128)S(1)} %copy-done.6, f32[16,128]{1,0:T(8,128)S(1)} %copy-done.7, ...), custom_call_target="tpu_custom_call" | custom-call | flops 268435456 | bytes 1048576 | tf_op jit(solution)/shard_map/rollout/pallas_call | solution.py:383
  80.3 3.7 %all-to-all-done.3.parts_ref = f32[32,2,1280]{2,1,0:T(2,128)S(1)} async-done(((f32[32,2,1280]{2,1,0:T(2,128)}), f32[32,2,1280]{2,1,0:T(2,128)S(1)}, u32[]{:S(2)}, u32[]{:S(2)}) %all-to-all-start.3) | async-done | bytes 327712 | tf_op jit(solution)/shard_map/all_to_all | solution.py:456
  84.1 0.8 refit.4
  84.9 13.8 %all_to_all.46.peak_ref = f32[16,1,128]{2,1,0:T(1,128)S(1)} all-to-all(f32[16,1,128]{2,1,0:T(1,128)S(1)} %get-tuple-element.55), channel_id=1, replica_groups=mesh['env'=16,'cand'=32] {'env'}, dimensions={0} | all-to-all | bytes 16384 | tf_op jit(solution)/shard_map/all_to_all | solution.py:464
  98.7 0.8 to_all.4
  99.5 4.9 %all-to-all-start.5 = ((f32[32,2,1408]{2,1,0:T(2,128)}), f32[32,2,1408]{2,1,0:T(2,128)S(1)}, u32[]{:S(2)}, u32[]{:S(2)}) async-start(f32[32,2,1408]{2,1,0:T(2,128)} %get-tuple-element.58), calls=%async_computation.5 | async-start | bytes 720896 | tf_op jit(solution)/shard_map/all_to_all | solution.py:466
  104.4 0.0 copy-start.4
  104.4 0.9 copy-done.4
  105.3 0.9 copy-done.12
  106.2 0.8 copy-done.15
  107.1 6.5 %rollout.7 = (f32[1,8,16]{2,1,0:T(8,128)}, f32[2,128,128]{2,1,0:T(8,128)}) custom-call(bf16[128,2560]{1,0:T(8,128)(2,1)} %get-tuple-element.41.refs_0_, bf16[128,2560]{1,0:T(8,128)(2,1)} %get-tuple-element.48.refs_1_.refs_0_, f32[2,128,128]{2,1,0:T(8,128)S(1)} %copy-done.4, f32[2,128,128]{2,1,0:T(8,128)S(1)} %copy-done.12, f32[128,128]{1,0:T(8,128)S(1)} %copy-done.15, ...), custom_call_target="tpu_custom_call" | custom-call | flops 268435456 | bytes 1048576 | tf_op jit(solution)/shard_map/rollout/pallas_call | solution.py:383
  113.6 0.7 all-to-all-done.5.refs_4_
  114.3 1.9 %actions.5 = (bf16[128,2560]{1,0:T(8,128)(2,1)}, f32[128,128]{1,0:T(8,128)}, f32[32,2,1280]{2,1,0:T(2,128)}, f32[2,1280]{1,0:T(2,128)}) custom-call(f32[2,128,2560]{2,1,0:T(8,128)S(1)} %get-tuple-element.40.refs_0_, s32[3,16,25]{2,1,0:T(8,128)S(1)} %bitcast.8, s32[1]{0:T(128)} %bitcast.1.tie_ref.refs_2_.refs_3_, ...), custom_call_target="tpu_custom_call" | custom-call | tf_op jit(solution)/shard_map/actions/pallas_call | solution.py:187
  116.3 0.0 copy-start.14
  116.3 6.9 %all-to-all-start.6 = ((f32[32,2,1280]{2,1,0:T(2,128)}), f32[32,2,1280]{2,1,0:T(2,128)S(1)}, u32[]{:S(2)}, u32[]{:S(2)}) async-start(f32[32,2,1280]{2,1,0:T(2,128)} %get-tuple-element.59), calls=%async_computation.6 | async-start | bytes 655360 | tf_op jit(solution)/shard_map/all_to_all | solution.py:456
  123.2 0.0 copy-start.20
  123.2 0.6 copy-done.20
  123.9 6.5 %rollout.8 = (f32[1,8,16]{2,1,0:T(8,128)}, f32[2,128,128]{2,1,0:T(8,128)}) custom-call(bf16[128,2560]{1,0:T(8,128)(2,1)} %get-tuple-element.48.refs_1_.refs_0_, bf16[128,2560]{1,0:T(8,128)(2,1)} %get-tuple-element.61.refs_1_.refs_0_, f32[2,128,128]{2,1,0:T(8,128)S(1)} %copy-done.11, f32[128,128]{1,0:T(8,128)S(1)} %copy-done.13, f32[16,128]{1,0:T(8,128)S(1)} %copy-done.6, ...), custom_call_target="tpu_custom_call" | custom-call | flops 268435456 | bytes 1048576 | tf_op jit(solution)/shard_map/rollout/pallas_call | solution.py:383
  130.3 2.3 %all-to-all-done.6.parts_ref = f32[32,2,1280]{2,1,0:T(2,128)S(1)} async-done(((f32[32,2,1280]{2,1,0:T(2,128)}), f32[32,2,1280]{2,1,0:T(2,128)S(1)}, u32[]{:S(2)}, u32[]{:S(2)}) %all-to-all-start.6) | async-done | bytes 327712 | tf_op jit(solution)/shard_map/all_to_all | solution.py:456
  132.7 0.8 refit.5
  133.5 13.8 %all_to_all.47.peak_ref = f32[16,1,128]{2,1,0:T(1,128)S(1)} all-to-all(f32[16,1,128]{2,1,0:T(1,128)S(1)} %get-tuple-element.66), channel_id=1, replica_groups=mesh['env'=16,'cand'=32] {'env'}, dimensions={0} | all-to-all | bytes 16384 | tf_op jit(solution)/shard_map/all_to_all | solution.py:464
  147.4 0.8 to_all.5
  148.1 6.2 %all-to-all-start.8 = ((f32[32,2,1408]{2,1,0:T(2,128)}), f32[32,2,1408]{2,1,0:T(2,128)S(1)}, u32[]{:S(2)}, u32[]{:S(2)}) async-start(f32[32,2,1408]{2,1,0:T(2,128)} %get-tuple-element.67), calls=%async_computation.8 | async-start | bytes 720896 | tf_op jit(solution)/shard_map/all_to_all | solution.py:466
  154.3 0.0 copy-start.10
  154.3 0.9 copy-done.10
  155.2 0.7 copy-done.18
  155.9 9.9 %rollout.9 = f32[3,8,16]{2,1,0:T(8,128)} custom-call(bf16[128,2560]{1,0:T(8,128)(2,1)} %get-tuple-element.61.refs_1_.refs_0_, f32[2,128,128]{2,1,0:T(8,128)S(1)} %copy-done.10, f32[128,128]{1,0:T(8,128)S(1)} %copy-done.14, f32[16,128]{1,0:T(8,128)S(1)} %copy-done.6, f32[16,128]{1,0:T(8,128)S(1)} %copy-done.7, bf16[128,512]{1,0:T(8,128)(2,1)S(1)} %copy-done, ...), custom_call_target="tpu_custom_call" | custom-call | flops 268435456 | bytes 1048576 | tf_op jit(solution)/shard_map/rollout/pallas_call | solution.py:383
  165.8 0.8 finished.1
  (26 shorter events, 0.1 us)
Async XLA Ops:
  0.6 4.2 %copy-start.5 = (s32[16,3,25]{2,0,1:T(8,128)S(1)}, s32[16,3,25]{2,0,1:T(8,128)}, u32[]{:S(2)}) copy-start(s32[16,3,25]{2,0,1:T(8,128)} %param.21) | copy-start | bytes 14404
  0.6 4.2 %copy-start.9 = (f32[16,2560]{1,0:T(8,128)S(1)}, f32[16,2560]{1,0:T(8,128)}, u32[]{:S(2)}) copy-start(f32[16,2560]{1,0:T(8,128)} %refs_5_.6) | copy-start | bytes 491524
  0.7 4.2 %copy-start.8 = (f32[16,2560]{1,0:T(8,128)S(1)}, f32[16,2560]{1,0:T(8,128)}, u32[]{:S(2)}) copy-start(f32[16,2560]{1,0:T(8,128)} %refs_4_.5) | copy-start | bytes 491524
  6.6 52.3 %copy-start = (bf16[128,512]{1,0:T(8,128)(2,1)S(1)}, bf16[128,512]{1,0:T(8,128)(2,1)}, u32[]{:S(2)}) copy-start(bf16[128,512]{1,0:T(8,128)(2,1)} %refs_5_.11) | copy-start | bytes 393220
  6.6 52.3 %copy-start.1 = (bf16[512,128]{1,0:T(8,128)(2,1)S(1)}, bf16[512,128]{1,0:T(8,128)(2,1)}, u32[]{:S(2)}) copy-start(bf16[512,128]{1,0:T(8,128)(2,1)} %refs_7_.7) | copy-start | bytes 393220
  6.6 52.3 %copy-start.2 = (bf16[64,512]{1,0:T(8,128)(2,1)S(1)}, bf16[64,512]{1,0:T(8,128)(2,1)}, u32[]{:S(2)}) copy-start(bf16[64,512]{1,0:T(8,128)(2,1)} %refs_6_.7) | copy-start | bytes 196612
  6.6 52.3 %copy-start.6 = (f32[16,128]{1,0:T(8,128)S(1)}, f32[16,128]{1,0:T(8,128)}, u32[]{:S(2)}) copy-start(f32[16,128]{1,0:T(8,128)} %refs_3_.5) | copy-start | bytes 24580
  6.6 52.3 %copy-start.7 = (f32[16,128]{1,0:T(8,128)S(1)}, f32[16,128]{1,0:T(8,128)}, u32[]{:S(2)}) copy-start(f32[16,128]{1,0:T(8,128)} %refs_4_.9) | copy-start | bytes 24580
  6.6 52.3 %copy-start.16 = (f32[512]{0:T(512)S(1)}, f32[512]{0:T(512)}, u32[]{:S(2)}) copy-start(f32[512]{0:T(512)} %param.19) | copy-start | bytes 6148
  6.7 52.3 %copy-start.19 = (f32[128]{0:T(128)S(1)}, f32[128]{0:T(128)}, u32[]{:S(2)}) copy-start(f32[128]{0:T(128)} %param.20) | copy-start | bytes 1540
  6.7 20.1 %all-to-all-start = ((f32[32,2,1280]{2,1,0:T(2,128)}), f32[32,2,1280]{2,1,0:T(2,128)S(1)}, u32[]{:S(2)}, u32[]{:S(2)}) async-start(f32[32,2,1280]{2,1,0:T(2,128)} %get-tuple-element.42), calls=%async_computation | async-start | bytes 655360 | tf_op jit(solution)/shard_map/all_to_all | solution.py:456
  52.6 16.1 %all-to-all-start.2 = ((f32[32,2,1408]{2,1,0:T(2,128)}), f32[32,2,1408]{2,1,0:T(2,128)S(1)}, u32[]{:S(2)}, u32[]{:S(2)}) async-start(f32[32,2,1408]{2,1,0:T(2,128)} %get-tuple-element.47), calls=%async_computation.2 | async-start | bytes 720896 | tf_op jit(solution)/shard_map/all_to_all | solution.py:466
  65.0 9.6 %copy-start.3 = (f32[2,128,128]{2,1,0:T(8,128)S(1)}, f32[2,128,128]{2,1,0:T(8,128)}, u32[]{:S(2)}) copy-start(f32[2,128,128]{2,1,0:T(8,128)} %rollout.5.refs_3_.refs_2_) | copy-start | bytes 393220
  70.6 13.4 %all-to-all-start.3 = ((f32[32,2,1280]{2,1,0:T(2,128)}), f32[32,2,1280]{2,1,0:T(2,128)S(1)}, u32[]{:S(2)}, u32[]{:S(2)}) async-start(f32[32,2,1280]{2,1,0:T(2,128)} %get-tuple-element.53), calls=%async_computation.3 | async-start | bytes 655360 | tf_op jit(solution)/shard_map/all_to_all | solution.py:456
  99.5 14.8 %all-to-all-start.5 = ((f32[32,2,1408]{2,1,0:T(2,128)}), f32[32,2,1408]{2,1,0:T(2,128)S(1)}, u32[]{:S(2)}, u32[]{:S(2)}) async-start(f32[32,2,1408]{2,1,0:T(2,128)} %get-tuple-element.58), calls=%async_computation.5 | async-start | bytes 720896 | tf_op jit(solution)/shard_map/all_to_all | solution.py:466
  104.4 0.9 copy-start.4
  105.3 0.9 copy-start.12
  106.2 0.8 copy-start.15
  107.1 16.1 %copy-start.13 = (f32[128,128]{1,0:T(8,128)S(1)}, f32[128,128]{1,0:T(8,128)}, u32[]{:S(2)}) copy-start(f32[128,128]{1,0:T(8,128)} %get-tuple-element.63.refs_3_) | copy-start | bytes 196612
  113.6 9.6 %copy-start.11 = (f32[2,128,128]{2,1,0:T(8,128)S(1)}, f32[2,128,128]{2,1,0:T(8,128)}, u32[]{:S(2)}) copy-start(f32[2,128,128]{2,1,0:T(8,128)} %get-tuple-element.62.refs_2_) | copy-start | bytes 393220
  114.3 40.0 %copy-start.17 = (f32[1,8,16]{2,1,0:T(8,128)S(1)}, f32[1,8,16]{2,1,0:T(8,128)}, u32[]{:S(2)}) copy-start(f32[1,8,16]{2,1,0:T(8,128)} %get-tuple-element.57.refs_3_.refs_10_) | copy-start | bytes 1540
  116.3 38.1 %copy-start.14 = (f32[128,128]{1,0:T(8,128)S(1)}, f32[128,128]{1,0:T(8,128)}, u32[]{:S(2)}) copy-start(f32[128,128]{1,0:T(8,128)} %get-tuple-element.71.refs_2_) | copy-start | bytes 196612
  116.3 16.4 %all-to-all-start.6 = ((f32[32,2,1280]{2,1,0:T(2,128)}), f32[32,2,1280]{2,1,0:T(2,128)S(1)}, u32[]{:S(2)}, u32[]{:S(2)}) async-start(f32[32,2,1280]{2,1,0:T(2,128)} %get-tuple-element.59), calls=%async_computation.6 | async-start | bytes 655360 | tf_op jit(solution)/shard_map/all_to_all | solution.py:456
  123.2 0.7 copy-start.20
  148.1 17.6 %all-to-all-start.8 = ((f32[32,2,1408]{2,1,0:T(2,128)}), f32[32,2,1408]{2,1,0:T(2,128)S(1)}, u32[]{:S(2)}, u32[]{:S(2)}) async-start(f32[32,2,1408]{2,1,0:T(2,128)} %get-tuple-element.67), calls=%async_computation.8 | async-start | bytes 720896 | tf_op jit(solution)/shard_map/all_to_all | solution.py:466
  154.3 0.9 copy-start.10
  155.2 0.7 copy-start.18

commit v5 on v4

--- a/solution.py
+++ b/solution.py
@@ -39,7 +39,7 @@
     return np.asarray(kernel, np.float32).astype(jnp.bfloat16).astype(np.float32)
 
 
-def noise_body(white_ref, tie_ref, out_ref, token_ref, rows_in, fill, sems, *, act_dim, blocks, first, parts):
+def noise_body(white_ref, own_ref, out_ref, same_ref, rows_in, fill, sems, *, act_dim, blocks, first, parts):
     count = out_ref.shape[0]
     _, rows, flat = white_ref.shape
     length = flat // act_dim
@@ -74,10 +74,10 @@
             out_ref[one, :, pl.ds(block * 256, 256)] = jnp.dot(
                 rows_in[one], fill[pl.ds(start, flat), :], preferred_element_type=jnp.float32
             )
-    token_ref[...] = out_ref[count - 1, pl.ds(0, 8), pl.ds(0, LANES)]
-
-
-def noise_of(white, first, count, tie, act_dim, horizon):
+    same_ref[...] = own_ref[...]
+
+
+def noise_of(white, first, count, own, act_dim, horizon):
     _, rows, flat = white.shape
     width = horizon * act_dim
     parts = 1
@@ -86,11 +86,11 @@
             noise_body, act_dim=act_dim, blocks=width // 256, first=first, parts=parts
         ),
         grid=(1,),
-        in_specs=[HBM, HBM],
-        out_specs=[VMEM, whole((8, LANES))],
+        in_specs=[HBM, whole(own.shape)],
+        out_specs=[VMEM, VMEM],
         out_shape=[
             jax.ShapeDtypeStruct((count, rows, width), jnp.float32),
-            in_hbm((8, LANES)),
+            jax.ShapeDtypeStruct(own.shape, own.dtype),
         ],
         scratch_shapes=[
             pltpu.VMEM((count, rows, flat), jnp.bfloat16),
@@ -100,7 +100,7 @@
         cost_estimate=pl.CostEstimate(flops=ROLL_FLOPS, bytes_accessed=1 << 20, transcendentals=0),
         compiler_params=pltpu.CompilerParams(vmem_limit_bytes=16 << 20),
         name="noise",
-    )(stay(white), stay(tie))
+    )(stay(white), stay(own))
 
 
 def stats_of(state_ref, envs, half, envs_total):
@@ -208,11 +208,8 @@
     )(noise, elite_idx, mine, stay(tie), *state)
 
 
-def refit_body(parts_ref, own_hbm, tie_ref, slice_ref, peak_ref, own_ref, sem, *, elites):
-    copy = pltpu.make_async_copy(own_hbm, own_ref, sem)
-    copy.start()
+def refit_body(parts_ref, own_ref, slice_ref, peak_ref, *, elites):
     total = jnp.sum(parts_ref[...], axis=0)
-    copy.wait()
     mean = total[0:1] / elites
     variance = jnp.maximum(total[1:2] / elites - mean * mean, 0.0)
     slice_ref[0:1, :] = MOMENTUM * own_ref[0:1, :] + (1.0 - MOMENTUM) * mean
@@ -221,22 +218,21 @@
     peak_ref[...] = jnp.broadcast_to(jnp.max(mixed, axis=1, keepdims=True)[None], peak_ref.shape)
 
 
-def refit(parts, own, tie, elites, groups):
+def refit(parts, own, elites, groups):
     return pl.pallas_call(
         functools.partial(refit_body, elites=elites),
-        in_specs=[VMEM, HBM, HBM],
+        in_specs=[VMEM, VMEM],
         out_specs=[VMEM, VMEM],
         out_shape=[
             jax.ShapeDtypeStruct(own.shape, jnp.float32),
             jax.ShapeDtypeStruct((groups, 1, LANES), jnp.float32),
         ],
-        scratch_shapes=[pltpu.VMEM(own.shape, jnp.float32), pltpu.SemaphoreType.DMA],
         compiler_params=pltpu.CompilerParams(vmem_limit_bytes=4 << 20),
         name="refit",
-    )(parts, stay(own), stay(tie))
-
-
-def spread_body(slice_ref, peak_ref, out_ref, token_ref):
+    )(parts, own)
+
+
+def spread_body(slice_ref, peak_ref, tie_ref, out_ref, token_ref):
     lines = out_ref.shape[0]
     half = slice_ref.shape[1]
     lane = lax.broadcasted_iota(jnp.int32, (1, LANES), 1)
@@ -249,17 +245,17 @@
     out_ref[:, :, pl.ds(half, LANES)] = jnp.broadcast_to(tail[None], (lines, 2, LANES))
 
 
-def to_all(piece, peaks, lines):
+def to_all(piece, peaks, tie, lines):
     half = piece.shape[1]
     return pl.pallas_call(
         spread_body,
         grid=(1,),
-        in_specs=[VMEM, VMEM],
+        in_specs=[VMEM, VMEM, HBM],
         out_specs=[whole((lines, 2, half + LANES)), whole((8, LANES))],
         out_shape=[in_hbm((lines, 2, half + LANES)), in_hbm((8, LANES))],
         compiler_params=pltpu.CompilerParams(vmem_limit_bytes=4 << 20),
         name="to_all",
-    )(piece, peaks)
+    )(piece, peaks, stay(tie))
 
 
 def final_body(state_ref, mean_ref, std_ref, *, envs_total):
@@ -288,7 +284,7 @@
     )(state)
 
 
-def rollout_body(*refs, spans, act_dim, total, earlier):
+def rollout_body(*refs, spans, act_dim, total, earlier, keep):
     refs = list(refs)
     take = lambda n: [refs.pop(0) for _ in range(n)]
     acts = take(len(spans))
@@ -296,8 +292,10 @@
     squares = [take(1)[0] if last == total else None for _, last in spans]
     begin_ref, goal_ref, ws_ref, wa_ref, wout_ref, bin_ref, bout_ref = take(7)
     before = take(earlier)
-    take(1)
+    tie_ref = take(1)[0]
     outs = take(len(spans))
+    if keep:
+        take(1)[0][...] = tie_ref[...]
     moves, win, start, goal, sems = refs
     envs, dim = begin_ref.shape
     rows = acts[0].shape[0]
@@ -334,10 +332,14 @@
     for copy in copies:
         copy.wait()
 
-    def two_steps(k, carry):
+    many = 4 if steps % 4 == 0 else 2
+
+    def some_steps(k, carry):
         state, error = carry
-        pair = moves[:, pl.ds(pl.multiple_of(k * 2 * act_dim, 2 * act_dim), 2 * act_dim)]
-        for parity in range(2):
+        for n in range(many):
+            parity = n % 2
+            at = pl.multiple_of((k * many + n - parity) * act_dim, 2 * act_dim)
+            pair = moves[:, pl.ds(at, 2 * act_dim)]
             joined = jnp.concatenate([state.astype(jnp.bfloat16), pair], axis=1)
             half = jnp.dot(joined, win[parity], preferred_element_type=jnp.float32) + bias_in
             hidden = (half + half * jnp.tanh(half)).astype(jnp.bfloat16)
@@ -347,7 +349,7 @@
             error = error + gap * gap
         return state, error
 
-    state, error = lax.fori_loop(0, steps // 2, two_steps, (start[0], start[1]))
+    state, error = lax.fori_loop(0, steps // many, some_steps, (start[0], start[1]))
     for k, (_, last) in enumerate(spans):
         part = slice(k * rows, (k + 1) * rows)
         if last < total:
@@ -365,7 +367,7 @@
         outs[k][earlier] = table[:, :envs]
 
 
-def rollout(parts, fixed, before, tie, act_dim):
+def rollout(parts, fixed, before, tie, act_dim, keep):
     rows, width = parts[0][0].shape
     envs, dim = fixed[0].shape
     cands = rows // envs
@@ -379,15 +381,20 @@
     shapes = [
         (1 + len(before), cands, envs) if last == total else (2, rows, dim) for _, last in spans
     ]
-    small = len(carried) + len(squares) + len(fixed) + len(before)
+    loose = carried + squares
     return pl.pallas_call(
         functools.partial(
-            rollout_body, spans=spans, act_dim=act_dim, total=total, earlier=len(before)
+            rollout_body, spans=spans, act_dim=act_dim, total=total, earlier=len(before), keep=keep
         ),
         grid=(1,),
-        in_specs=[HBM] * len(acts) + [VMEM] * small + [HBM],
-        out_specs=[whole(shape) for shape in shapes],
-        out_shape=[in_hbm(shape) for shape in shapes],
+        in_specs=[HBM] * len(acts)
+        + [whole(a.shape) for a in loose]
+        + [VMEM] * len(fixed)
+        + [whole(a.shape) for a in before]
+        + [whole(tie.shape) if keep else HBM],
+        out_specs=[whole(shape) for shape in shapes] + [VMEM] * keep,
+        out_shape=[in_hbm(shape) for shape in shapes]
+        + [jax.ShapeDtypeStruct(tie.shape, tie.dtype)] * keep,
         scratch_shapes=[
             pltpu.VMEM((len(parts) * rows, steps * act_dim), jnp.bfloat16),
             pltpu.VMEM((2, dim + 2 * act_dim, fixed[2].shape[1]), jnp.bfloat16),
@@ -398,7 +405,7 @@
         cost_estimate=pl.CostEstimate(flops=ROLL_FLOPS, bytes_accessed=1 << 20, transcendentals=0),
         compiler_params=pltpu.CompilerParams(vmem_limit_bytes=10 << 20),
         name="rollout",
-    )(*map(stay, acts), *carried, *squares, *fixed, *before, stay(tie))
+    )(*map(stay, acts), *map(stay, loose), *fixed, *map(stay, before), stay(tie))
 
 
 def shards(
@@ -438,16 +445,16 @@
     def part(it, first, last):
         return (acts[it], asq[it], held.get(it), first, last)
 
-    def play(parts, tie, before=()):
-        outs = rollout([part(*p) for p in parts], fixed, before, tie, act_dim)
+    def play(parts, tie, before=(), keep=False):
+        outs = rollout([part(*p) for p in parts], fixed, before, tie, act_dim, keep)
         for (it, _, last), out in zip(parts, outs):
             if last < horizon:
                 held[it] = out
             else:
                 costs[it] = out
-        return outs[0]
-
-    noise, _ = noise_of(white, 0, 1, mine, act_dim, horizon)
+        return outs[-1] if keep else outs[0]
+
+    noise, _ = noise_of(white, 0, 1, bias_out[None], act_dim, horizon)
     state, tie = (mean_init, std_init), mine
     for it in range(iters):
         acts[it], asq[it], sums, own = actions_of(
@@ -455,21 +462,22 @@
         )
         parts = mix(sums)
         if it == 0:
-            noise, tie = noise_of(white, 1, iters - 1, own, act_dim, horizon)
+            noise, own = noise_of(white, 1, iters - 1, own, act_dim, horizon)
         elif it == 1:
-            tie = play([(0, 14, 26), (1, 0, 12)], own)
+            own = play([(0, 14, 26), (1, 0, 12)], own, keep=True)
         else:
-            tie = play([(1, 26, horizon), (2, 0, 14)], own)
-        piece, peak = refit(parts, own, tie, elites, groups)
+            own = play([(1, 26, horizon), (2, 0, 14)], own, keep=True)
+        piece, peak = refit(parts, own, elites, groups)
         peaks = lax.all_to_all(peak, "env", 0, 0, tiled=True)
-        spread, token = to_all(piece, peaks, lines)
+        tie = mine if it < iters - 1 else play([(2, 14, 20)], peak)
+        spread, token = to_all(piece, peaks, tie, lines)
         state = (mix(spread),)
         if it == 0:
             tie = play([(0, 0, 14)], token)
         elif it == 1:
             tie = play([(0, 26, horizon), (1, 12, 26)], token)
         else:
-            tie = play([(2, 14, horizon)], token, (costs[0], costs[1]))
+            tie = play([(2, 20, horizon)], token, (costs[0], costs[1]))
     mean, std = finished(state[0], envs, width, envs_total)
     return (mean, std, jnp.swapaxes(costs[iters - 1], 1, 2))
 

time: 168 us -> 166 us (0.988)
  blocking collectives: 51.9 us -> 38 us
  waiting for transfers between devices: 13.2 us -> 21.4 us
  Pallas kernels: 57 us -> 63 us
  local copies, waits for them, and re-layouts: 4.95 us -> 0.06 us
  starting transfers between devices: 38.5 us -> 41.6 us
    all_to_all x3 -> x2, blocking collectives: 51.9 us -> 38 us  [shards(): peaks = lax.all_to_all(peak, 'env', 0, 0, tiled=True)]
    all_to_all x0 -> x1, waiting for transfers between devices: none -> 6.81 us  [shards(): peaks = lax.all_to_all(peak, 'env', 0, 0, tiled=True)]
    pallas_call x5 -> x6, Pallas kernels: 34.7 us -> 40.1 us  [rollout(): pl.pallas_call(functools.partial(rollout_body, spans=spans, act_dim=act_d...]
    unnamed x42 -> x20, local copies, waits for them, and re-layouts: 4.95 us -> 0.06 us
    all_to_all x0 -> x1, starting transfers between devices: none -> 3.47 us  [shards(): peaks = lax.all_to_all(peak, 'env', 0, 0, tiled=True)]
    all_to_all x3, waiting for transfers between devices: 4.48 us -> 7.47 us  [shards(): state = (mix(spread),)]
    all_to_all x3, starting transfers between devices: 21.3 us -> 19.4 us  [shards(): parts = mix(sums)]
  transfers between devices with their start and end apart: 6 -> 7, of which waited for: 5 -> 7; matrix products, arithmetic and copies ran while one was open for 0% -> 0% of each run, Pallas kernels for 25% -> 29%
where the time goes in v5:
time: 166 us; the launch traced here: 165 us
  Pallas kernels  63 us (38%)
  starting transfers between devices  41.6 us (25%)
  blocking collectives  38 us (23%)
  waiting for transfers between devices  21.4 us (13%)
    pallas_call x6, Pallas kernels, rollout(): pl.pallas_call(functools.partial(rollout_body, spans=spans, act_dim=act_d...  40.1 us
    all_to_all x2, blocking collectives, shards(): peaks = lax.all_to_all(peak, 'env', 0, 0, tiled=True)  38 us
    all_to_all x3, starting transfers between devices, shards(): parts = mix(sums)  19.4 us
    all_to_all x3, starting transfers between devices, shards(): state = (mix(spread),)  18.7 us
    pallas_call x2, Pallas kernels, noise_of(): pl.pallas_call(functools.partial(noise_body, act_dim=act_dim, blocks=widt...  12.8 us
    all_to_all x3, waiting for transfers between devices, shards(): state = (mix(spread),)  7.47 us
    all_to_all x3, waiting for transfers between devices, shards(): parts = mix(sums)  7.16 us
    all_to_all x1, waiting for transfers between devices, shards(): peaks = lax.all_to_all(peak, 'env', 0, 0, tiled=True)  6.81 us
  transfers between devices with their start and end apart: 7, of which 7 were waited for; matrix products, arithmetic and copies ran while one was open for 0% of the time, Pallas kernels for 29%

profile of v5, /device:TPU:1, one launch (start us, length us, event | category | flops | bytes accessed | tf_op | source)
XLA Modules:
  0.0 165.1 jit_solution(8055641156327361147)
XLA Ops:
  0.7 5.1 %noise.2 = (f32[1,128,2560]{2,1,0:T(8,128)S(1)}, f32[1,128]{1,0:T(1,128)}) custom-call(bf16[3,128,4096]{2,1,0:T(8,128)(2,1)} %bitcast.22, f32[1,128]{1,0:T(1,128)} %bitcast.15), custom_call_target="tpu_custom_call" | custom-call | flops 268435456 | bytes 1048576 | tf_op jit(solution)/shard_map/noise/pallas_call | solution.py:84
  5.8 0.0 copy-done.5
  5.8 0.0 copy-done.7
  5.8 0.0 copy-done.6
  5.8 1.7 %actions.3 = (bf16[128,2560]{1,0:T(8,128)(2,1)}, f32[128,128]{1,0:T(8,128)}, f32[32,2,1280]{2,1,0:T(2,128)}, f32[2,1280]{1,0:T(2,128)}) custom-call(f32[1,128,2560]{2,1,0:T(8,128)S(1)} %get-tuple-element.40.refs_0_, s32[3,16,25]{2,1,0:T(8,128)S(1)} %bitcast.6, s32[1]{0:T(128)} %bitcast.3.refs_2_.refs_3_.tie_ref, s32[1]{0:T(128)} %bitcast.3.refs_2_.refs_3_.tie_ref, ...), custom_call_target="tpu_custom_call" | custom-call | tf_op jit(solution)/shard_map/actions/pallas_call | solution.py:187
  7.5 0.0 copy-start
  7.5 0.0 copy-start.1
  7.5 0.0 copy-start.2
  7.5 0.0 copy-start.3
  7.5 0.0 copy-start.4
  7.6 0.0 copy-start.8
  7.6 0.0 copy-start.9
  7.6 10.5 %all-to-all-start = ((f32[32,2,1280]{2,1,0:T(2,128)}), f32[32,2,1280]{2,1,0:T(2,128)S(1)}, u32[]{:S(2)}, u32[]{:S(2)}) async-start(f32[32,2,1280]{2,1,0:T(2,128)} %get-tuple-element.44), calls=%async_computation | async-start | bytes 655360 | tf_op jit(solution)/shard_map/all_to_all | solution.py:463
  18.1 7.7 %noise.3 = (f32[2,128,2560]{2,1,0:T(8,128)S(1)}, f32[2,1280]{1,0:T(2,128)S(1)}) custom-call(bf16[3,128,4096]{2,1,0:T(8,128)(2,1)} %bitcast.23, f32[2,1280]{1,0:T(2,128)} %get-tuple-element.41.own_ref), custom_call_target="tpu_custom_call" | custom-call | flops 268435456 | bytes 1048576 | tf_op jit(solution)/shard_map/noise/pallas_call | solution.py:84
  25.8 1.9 %all-to-all-done.parts_ref = f32[32,2,1280]{2,1,0:T(2,128)S(1)} async-done(((f32[32,2,1280]{2,1,0:T(2,128)}), f32[32,2,1280]{2,1,0:T(2,128)S(1)}, u32[]{:S(2)}, u32[]{:S(2)}) %all-to-all-start) | async-done | bytes 327712 | tf_op jit(solution)/shard_map/all_to_all | solution.py:463
  27.7 0.3 refit.3
  28.0 24.2 %all_to_all.45.peak_ref = f32[16,1,128]{2,1,0:T(1,128)S(1)} all-to-all(f32[16,1,128]{2,1,0:T(1,128)S(1)} %get-tuple-element.47), channel_id=1, replica_groups=mesh['env'=16,'cand'=32] {'env'}, dimensions={0} | all-to-all | bytes 16384 | tf_op jit(solution)/shard_map/all_to_all | solution.py:471
  52.2 0.8 to_all.3
  53.0 7.0 %all-to-all-start.2 = ((f32[32,2,1408]{2,1,0:T(2,128)}), f32[32,2,1408]{2,1,0:T(2,128)S(1)}, u32[]{:S(2)}, u32[]{:S(2)}) async-start(f32[32,2,1408]{2,1,0:T(2,128)} %get-tuple-element.49), calls=%async_computation.2 | async-start | bytes 720896 | tf_op jit(solution)/shard_map/all_to_all | solution.py:474
  59.9 0.0 copy-done
  59.9 0.0 copy-done.1
  59.9 0.0 copy-done.2
  60.0 0.0 copy-done.3
  60.0 6.0 %rollout.6.refs_3_.refs_2_ = f32[2,128,128]{2,1,0:T(8,128)} custom-call(bf16[128,2560]{1,0:T(8,128)(2,1)} %get-tuple-element.43.refs_0_, f32[16,128]{1,0:T(8,128)S(1)} %copy-done.3, f32[16,128]{1,0:T(8,128)S(1)} %copy-done.4, bf16[128,512]{1,0:T(8,128)(2,1)S(1)} %copy-done, bf16[64,512]{1,0:T(8,128)(2,1)S(1)} %copy-done.2, bf16[512,128]{1,0:T(8,128)(2,1)S(1)} %copy-done.1, ...), custom_call_target="tpu_custom_call" | custom-call | flops 268435456 | bytes 1048576 | tf_op jit(solution)/shard_map/rollout/pallas_call | solution.py:385
  66.0 3.8 %all-to-all-done.2.refs_4_ = f32[32,2,1408]{2,1,0:T(2,128)S(1)} async-done(((f32[32,2,1408]{2,1,0:T(2,128)}), f32[32,2,1408]{2,1,0:T(2,128)S(1)}, u32[]{:S(2)}, u32[]{:S(2)}) %all-to-all-start.2) | async-done | bytes 360480 | tf_op jit(solution)/shard_map/all_to_all | solution.py:474
  69.8 1.9 %actions.4 = (bf16[128,2560]{1,0:T(8,128)(2,1)}, f32[128,128]{1,0:T(8,128)}, f32[32,2,1280]{2,1,0:T(2,128)}, f32[2,1280]{1,0:T(2,128)}) custom-call(f32[2,128,2560]{2,1,0:T(8,128)S(1)} %get-tuple-element.42.refs_0_, s32[3,16,25]{2,1,0:T(8,128)S(1)} %bitcast.7, s32[1]{0:T(128)} %bitcast.3.refs_2_.refs_3_.tie_ref, f32[2,128,128]{2,1,0:T(8,128)} %rollout.6.refs_3_.refs_2_, ...), custom_call_target="tpu_custom_call" | custom-call | tf_op jit(solution)/shard_map/actions/pallas_call | solution.py:187
  71.7 3.9 %all-to-all-start.3 = ((f32[32,2,1280]{2,1,0:T(2,128)}), f32[32,2,1280]{2,1,0:T(2,128)S(1)}, u32[]{:S(2)}, u32[]{:S(2)}) async-start(f32[32,2,1280]{2,1,0:T(2,128)} %get-tuple-element.55), calls=%async_computation.3 | async-start | bytes 655360 | tf_op jit(solution)/shard_map/all_to_all | solution.py:463
  75.6 6.3 %rollout.7 = (f32[2,128,128]{2,1,0:T(8,128)}, f32[2,128,128]{2,1,0:T(8,128)}, f32[2,1280]{1,0:T(2,128)S(1)}) custom-call(bf16[128,2560]{1,0:T(8,128)(2,1)} %get-tuple-element.43.refs_0_, bf16[128,2560]{1,0:T(8,128)(2,1)} %get-tuple-element.50.refs_1_.refs_0_, f32[2,128,128]{2,1,0:T(8,128)} %rollout.6.refs_3_.refs_2_, f32[16,128]{1,0:T(8,128)S(1)} %copy-done.3, ...), custom_call_target="tpu_custom_call" | custom-call | flops 268435456 | bytes 1048576 | tf_op jit(solution)/shard_map/rollout/pallas_call | solution.py:385
  81.9 3.2 %all-to-all-done.3.parts_ref = f32[32,2,1280]{2,1,0:T(2,128)S(1)} async-done(((f32[32,2,1280]{2,1,0:T(2,128)}), f32[32,2,1280]{2,1,0:T(2,128)S(1)}, u32[]{:S(2)}, u32[]{:S(2)}) %all-to-all-start.3) | async-done | bytes 327712 | tf_op jit(solution)/shard_map/all_to_all | solution.py:463
  85.1 0.3 refit.4
  85.4 13.8 %all_to_all.46.peak_ref = f32[16,1,128]{2,1,0:T(1,128)S(1)} all-to-all(f32[16,1,128]{2,1,0:T(1,128)S(1)} %get-tuple-element.58), channel_id=1, replica_groups=mesh['env'=16,'cand'=32] {'env'}, dimensions={0} | all-to-all | bytes 16384 | tf_op jit(solution)/shard_map/all_to_all | solution.py:471
  99.2 0.8 to_all.4
  100.0 5.3 %all-to-all-start.5 = ((f32[32,2,1408]{2,1,0:T(2,128)}), f32[32,2,1408]{2,1,0:T(2,128)S(1)}, u32[]{:S(2)}, u32[]{:S(2)}) async-start(f32[32,2,1408]{2,1,0:T(2,128)} %get-tuple-element.61), calls=%async_computation.5 | async-start | bytes 720896 | tf_op jit(solution)/shard_map/all_to_all | solution.py:474
  105.4 7.5 %rollout.8 = (f32[1,8,16]{2,1,0:T(8,128)}, f32[2,128,128]{2,1,0:T(8,128)}) custom-call(bf16[128,2560]{1,0:T(8,128)(2,1)} %get-tuple-element.43.refs_0_, bf16[128,2560]{1,0:T(8,128)(2,1)} %get-tuple-element.50.refs_1_.refs_0_, f32[2,128,128]{2,1,0:T(8,128)} %get-tuple-element.52.refs_2_, f32[2,128,128]{2,1,0:T(8,128)} %get-tuple-element.53.refs_3_, ...), custom_call_target="tpu_custom_call" | custom-call | flops 268435456 | bytes 1048576 | tf_op jit(solution)/shard_map/rollout/pallas_call | solution.py:385
  112.8 2.4 %all-to-all-done.5.refs_4_ = f32[32,2,1408]{2,1,0:T(2,128)S(1)} async-done(((f32[32,2,1408]{2,1,0:T(2,128)}), f32[32,2,1408]{2,1,0:T(2,128)S(1)}, u32[]{:S(2)}, u32[]{:S(2)}) %all-to-all-start.5) | async-done | bytes 360480 | tf_op jit(solution)/shard_map/all_to_all | solution.py:474
  115.2 1.9 %actions.5 = (bf16[128,2560]{1,0:T(8,128)(2,1)}, f32[128,128]{1,0:T(8,128)}, f32[32,2,1280]{2,1,0:T(2,128)}, f32[2,1280]{1,0:T(2,128)}) custom-call(f32[2,128,2560]{2,1,0:T(8,128)S(1)} %get-tuple-element.42.refs_0_, s32[3,16,25]{2,1,0:T(8,128)S(1)} %bitcast.8, s32[1]{0:T(128)} %bitcast.3.refs_2_.refs_3_.tie_ref, ...), custom_call_target="tpu_custom_call" | custom-call | tf_op jit(solution)/shard_map/actions/pallas_call | solution.py:187
  117.1 5.0 %all-to-all-start.6 = ((f32[32,2,1280]{2,1,0:T(2,128)}), f32[32,2,1280]{2,1,0:T(2,128)S(1)}, u32[]{:S(2)}, u32[]{:S(2)}) async-start(f32[32,2,1280]{2,1,0:T(2,128)} %get-tuple-element.62), calls=%async_computation.6 | async-start | bytes 655360 | tf_op jit(solution)/shard_map/all_to_all | solution.py:463
  122.2 7.5 %rollout.9 = (f32[1,8,16]{2,1,0:T(8,128)}, f32[2,128,128]{2,1,0:T(8,128)}, f32[2,1280]{1,0:T(2,128)S(1)}) custom-call(bf16[128,2560]{1,0:T(8,128)(2,1)} %get-tuple-element.50.refs_1_.refs_0_, bf16[128,2560]{1,0:T(8,128)(2,1)} %get-tuple-element.63.refs_1_.refs_0_, f32[2,128,128]{2,1,0:T(8,128)} %get-tuple-element.64.refs_2_, ...), custom_call_target="tpu_custom_call" | custom-call | flops 268435456 | bytes 1048576 | tf_op jit(solution)/shard_map/rollout/pallas_call | solution.py:385
  129.6 2.0 %all-to-all-done.6.parts_ref = f32[32,2,1280]{2,1,0:T(2,128)S(1)} async-done(((f32[32,2,1280]{2,1,0:T(2,128)}), f32[32,2,1280]{2,1,0:T(2,128)S(1)}, u32[]{:S(2)}, u32[]{:S(2)}) %all-to-all-start.6) | async-done | bytes 327712 | tf_op jit(solution)/shard_map/all_to_all | solution.py:463
  131.7 0.9 refit.5
  132.6 3.5 %all-to-all-start.7 = ((f32[16,1,128]{2,1,0:T(1,128)}), f32[16,1,128]{2,1,0:T(1,128)S(1)}, u32[]{:S(2)}, u32[]{:S(2)}) async-start(f32[16,1,128]{2,1,0:T(1,128)} %get-tuple-element.69.refs_9_), calls=%async_computation.7 | async-start | bytes 16384 | tf_op jit(solution)/shard_map/all_to_all | solution.py:471
  136.0 4.3 %rollout.10.tie_ref.refs_1_ = f32[2,128,128]{2,1,0:T(8,128)} custom-call(bf16[128,2560]{1,0:T(8,128)(2,1)} %get-tuple-element.63.refs_1_.refs_0_, f32[2,128,128]{2,1,0:T(8,128)} %get-tuple-element.70.refs_1_, f32[16,128]{1,0:T(8,128)S(1)} %copy-done.3, f32[16,128]{1,0:T(8,128)S(1)} %copy-done.4, bf16[128,512]{1,0:T(8,128)(2,1)S(1)} %copy-done, ...), custom_call_target="tpu_custom_call" | custom-call | flops 268435456 | bytes 1048576 | tf_op jit(solution)/shard_map/rollout/pallas_call | solution.py:385
  140.4 6.8 %all-to-all-done.7.peak_ref = f32[16,1,128]{2,1,0:T(1,128)S(1)} async-done(((f32[16,1,128]{2,1,0:T(1,128)}), f32[16,1,128]{2,1,0:T(1,128)S(1)}, u32[]{:S(2)}, u32[]{:S(2)}) %all-to-all-start.7) | async-done | bytes 8224 | tf_op jit(solution)/shard_map/all_to_all | solution.py:471
  147.2 0.8 to_all.5
  148.0 6.5 %all-to-all-start.8 = ((f32[32,2,1408]{2,1,0:T(2,128)}), f32[32,2,1408]{2,1,0:T(2,128)S(1)}, u32[]{:S(2)}, u32[]{:S(2)}) async-start(f32[32,2,1408]{2,1,0:T(2,128)} %get-tuple-element.71), calls=%async_computation.8 | async-start | bytes 720896 | tf_op jit(solution)/shard_map/all_to_all | solution.py:474
  154.4 8.5 %rollout.11 = f32[3,8,16]{2,1,0:T(8,128)} custom-call(bf16[128,2560]{1,0:T(8,128)(2,1)} %get-tuple-element.63.refs_1_.refs_0_, f32[2,128,128]{2,1,0:T(8,128)} %rollout.10.tie_ref.refs_1_, f32[128,128]{1,0:T(8,128)} %get-tuple-element.74.refs_2_, f32[16,128]{1,0:T(8,128)S(1)} %copy-done.3, f32[16,128]{1,0:T(8,128)S(1)} %copy-done.4, ...), custom_call_target="tpu_custom_call" | custom-call | flops 268435456 | bytes 1048576 | tf_op jit(solution)/shard_map/rollout/pallas_call | solution.py:385
  162.9 1.4 all-to-all-done.8.state_ref
  164.3 0.8 finished.1
  (6 shorter events, 0.0 us)
Async XLA Ops:
  0.6 5.1 %copy-start.5 = (s32[16,3,25]{2,0,1:T(8,128)S(1)}, s32[16,3,25]{2,0,1:T(8,128)}, u32[]{:S(2)}) copy-start(s32[16,3,25]{2,0,1:T(8,128)} %param.21) | copy-start | bytes 14404
  0.6 5.1 %copy-start.7 = (f32[16,2560]{1,0:T(8,128)S(1)}, f32[16,2560]{1,0:T(8,128)}, u32[]{:S(2)}) copy-start(f32[16,2560]{1,0:T(8,128)} %refs_5_.7) | copy-start | bytes 491524
  0.7 5.1 %copy-start.6 = (f32[16,2560]{1,0:T(8,128)S(1)}, f32[16,2560]{1,0:T(8,128)}, u32[]{:S(2)}) copy-start(f32[16,2560]{1,0:T(8,128)} %refs_4_.6) | copy-start | bytes 491524
  7.5 52.4 %copy-start = (bf16[128,512]{1,0:T(8,128)(2,1)S(1)}, bf16[128,512]{1,0:T(8,128)(2,1)}, u32[]{:S(2)}) copy-start(bf16[128,512]{1,0:T(8,128)(2,1)} %refs_5_.13) | copy-start | bytes 393220
  7.5 52.4 %copy-start.1 = (bf16[512,128]{1,0:T(8,128)(2,1)S(1)}, bf16[512,128]{1,0:T(8,128)(2,1)}, u32[]{:S(2)}) copy-start(bf16[512,128]{1,0:T(8,128)(2,1)} %refs_7_.7) | copy-start | bytes 393220
  7.5 52.4 %copy-start.2 = (bf16[64,512]{1,0:T(8,128)(2,1)S(1)}, bf16[64,512]{1,0:T(8,128)(2,1)}, u32[]{:S(2)}) copy-start(bf16[64,512]{1,0:T(8,128)(2,1)} %refs_6_.9) | copy-start | bytes 196612
  7.5 52.4 %copy-start.3 = (f32[16,128]{1,0:T(8,128)S(1)}, f32[16,128]{1,0:T(8,128)}, u32[]{:S(2)}) copy-start(f32[16,128]{1,0:T(8,128)} %refs_3_.7) | copy-start | bytes 24580
  7.5 52.4 %copy-start.4 = (f32[16,128]{1,0:T(8,128)S(1)}, f32[16,128]{1,0:T(8,128)}, u32[]{:S(2)}) copy-start(f32[16,128]{1,0:T(8,128)} %refs_4_.11) | copy-start | bytes 24580
  7.6 52.4 %copy-start.8 = (f32[512]{0:T(512)S(1)}, f32[512]{0:T(512)}, u32[]{:S(2)}) copy-start(f32[512]{0:T(512)} %param.19) | copy-start | bytes 6148
  7.6 52.4 %copy-start.9 = (f32[128]{0:T(128)S(1)}, f32[128]{0:T(128)}, u32[]{:S(2)}) copy-start(f32[128]{0:T(128)} %param.20) | copy-start | bytes 1540
  7.6 20.1 %all-to-all-start = ((f32[32,2,1280]{2,1,0:T(2,128)}), f32[32,2,1280]{2,1,0:T(2,128)S(1)}, u32[]{:S(2)}, u32[]{:S(2)}) async-start(f32[32,2,1280]{2,1,0:T(2,128)} %get-tuple-element.44), calls=%async_computation | async-start | bytes 655360 | tf_op jit(solution)/shard_map/all_to_all | solution.py:463
  53.0 16.8 %all-to-all-start.2 = ((f32[32,2,1408]{2,1,0:T(2,128)}), f32[32,2,1408]{2,1,0:T(2,128)S(1)}, u32[]{:S(2)}, u32[]{:S(2)}) async-start(f32[32,2,1408]{2,1,0:T(2,128)} %get-tuple-element.49), calls=%async_computation.2 | async-start | bytes 720896 | tf_op jit(solution)/shard_map/all_to_all | solution.py:474
  71.7 13.4 %all-to-all-start.3 = ((f32[32,2,1280]{2,1,0:T(2,128)}), f32[32,2,1280]{2,1,0:T(2,128)S(1)}, u32[]{:S(2)}, u32[]{:S(2)}) async-start(f32[32,2,1280]{2,1,0:T(2,128)} %get-tuple-element.55), calls=%async_computation.3 | async-start | bytes 655360 | tf_op jit(solution)/shard_map/all_to_all | solution.py:463
  100.0 15.2 %all-to-all-start.5 = ((f32[32,2,1408]{2,1,0:T(2,128)}), f32[32,2,1408]{2,1,0:T(2,128)S(1)}, u32[]{:S(2)}, u32[]{:S(2)}) async-start(f32[32,2,1408]{2,1,0:T(2,128)} %get-tuple-element.61), calls=%async_computation.5 | async-start | bytes 720896 | tf_op jit(solution)/shard_map/all_to_all | solution.py:474
  117.1 14.6 %all-to-all-start.6 = ((f32[32,2,1280]{2,1,0:T(2,128)}), f32[32,2,1280]{2,1,0:T(2,128)S(1)}, u32[]{:S(2)}, u32[]{:S(2)}) async-start(f32[32,2,1280]{2,1,0:T(2,128)} %get-tuple-element.62), calls=%async_computation.6 | async-start | bytes 655360 | tf_op jit(solution)/shard_map/all_to_all | solution.py:463
  132.6 14.6 %all-to-all-start.7 = ((f32[16,1,128]{2,1,0:T(1,128)}), f32[16,1,128]{2,1,0:T(1,128)S(1)}, u32[]{:S(2)}, u32[]{:S(2)}) async-start(f32[16,1,128]{2,1,0:T(1,128)} %get-tuple-element.69.refs_9_), calls=%async_computation.7 | async-start | bytes 16384 | tf_op jit(solution)/shard_map/all_to_all | solution.py:471
  148.0 16.3 %all-to-all-start.8 = ((f32[32,2,1408]{2,1,0:T(2,128)}), f32[32,2,1408]{2,1,0:T(2,128)S(1)}, u32[]{:S(2)}, u32[]{:S(2)}) async-start(f32[32,2,1408]{2,1,0:T(2,128)} %get-tuple-element.71), calls=%async_computation.8 | async-start | bytes 720896 | tf_op jit(solution)/shard_map/all_to_all | solution.py:474

commit v6 on v5

--- a/solution.py
+++ b/solution.py
@@ -13,6 +13,7 @@
 FLOOR_SHARE = 0.1
 ACT_COST = 0.1
 LANES = 128
+SLOTS = 8
 ROLL_FLOPS = 1 << 28
 VMEM = pl.BlockSpec(memory_space=pltpu.VMEM)
 SMEM = pl.BlockSpec(memory_space=pltpu.SMEM)
@@ -39,8 +40,12 @@
     return np.asarray(kernel, np.float32).astype(jnp.bfloat16).astype(np.float32)
 
 
-def noise_body(white_ref, own_ref, out_ref, same_ref, rows_in, fill, sems, *, act_dim, blocks, first, parts):
+def noise_body(*refs, act_dim, blocks, first, parts, keep):
+    white_ref, out_ref, rows_in, fill, sems = refs[0], refs[1 + keep], *refs[-3:]
     count = out_ref.shape[0]
+    if keep:
+        hand = pltpu.make_async_copy(refs[1], refs[3], sems.at[count * parts])
+        hand.start()
     _, rows, flat = white_ref.shape
     length = flat // act_dim
     size = rows // parts
@@ -74,33 +79,34 @@
             out_ref[one, :, pl.ds(block * 256, 256)] = jnp.dot(
                 rows_in[one], fill[pl.ds(start, flat), :], preferred_element_type=jnp.float32
             )
-    same_ref[...] = own_ref[...]
+    if keep:
+        hand.wait()
 
 
 def noise_of(white, first, count, own, act_dim, horizon):
     _, rows, flat = white.shape
     width = horizon * act_dim
     parts = 1
+    keep = own is not None
+    shapes = [jax.ShapeDtypeStruct((count, rows, width), jnp.float32)]
+    if keep:
+        shapes.append(jax.ShapeDtypeStruct(own.shape, own.dtype))
     return pl.pallas_call(
         functools.partial(
-            noise_body, act_dim=act_dim, blocks=width // 256, first=first, parts=parts
+            noise_body, act_dim=act_dim, blocks=width // 256, first=first, parts=parts, keep=keep
         ),
-        grid=(1,),
-        in_specs=[HBM, whole(own.shape)],
-        out_specs=[VMEM, VMEM],
-        out_shape=[
-            jax.ShapeDtypeStruct((count, rows, width), jnp.float32),
-            jax.ShapeDtypeStruct(own.shape, own.dtype),
-        ],
+        in_specs=[HBM] * (1 + keep),
+        out_specs=[VMEM] * (1 + keep),
+        out_shape=shapes,
         scratch_shapes=[
             pltpu.VMEM((count, rows, flat), jnp.bfloat16),
             pltpu.VMEM((2 * flat, 256), jnp.bfloat16),
-            pltpu.SemaphoreType.DMA((count * parts,)),
+            pltpu.SemaphoreType.DMA((count * parts + 1,)),
         ],
         cost_estimate=pl.CostEstimate(flops=ROLL_FLOPS, bytes_accessed=1 << 20, transcendentals=0),
         compiler_params=pltpu.CompilerParams(vmem_limit_bytes=16 << 20),
         name="noise",
-    )(stay(white), stay(own))
+    )(stay(white), *([stay(own)] if keep else []))
 
 
 def stats_of(state_ref, envs, half, envs_total):
@@ -294,9 +300,8 @@
     before = take(earlier)
     tie_ref = take(1)[0]
     outs = take(len(spans))
-    if keep:
-        take(1)[0][...] = tie_ref[...]
-    moves, win, start, goal, sems = refs
+    same_ref = take(1)[0] if keep else None
+    moves, win, start, goal, square, sems = refs
     envs, dim = begin_ref.shape
     rows = acts[0].shape[0]
     cands = rows // envs
@@ -310,7 +315,22 @@
                 sems.at[k],
             )
         )
-        copies[k].start()
+    late = []
+    number = iter(range(len(spans), SLOTS))
+    for k, (_, last) in enumerate(spans):
+        if carried[k] is not None:
+            target = start.at[:, pl.ds(k * rows, rows), :]
+            copies.append(pltpu.make_async_copy(carried[k], target, sems.at[next(number)]))
+        if last == total:
+            late.append(pltpu.make_async_copy(squares[k], square, sems.at[next(number)]))
+            for n in range(earlier):
+                late.append(
+                    pltpu.make_async_copy(before[n].at[0], outs[k].at[n], sems.at[next(number)])
+                )
+    if keep:
+        late.append(pltpu.make_async_copy(tie_ref, same_ref, sems.at[next(number)]))
+    for copy in copies + late:
+        copy.start()
     zeros = jnp.zeros(wa_ref.shape, jnp.bfloat16)
     for parity in range(2):
         win[parity, pl.ds(0, dim), :] = ws_ref[...] * jnp.bfloat16(0.5)
@@ -325,9 +345,6 @@
         at = pl.ds(k * rows, rows)
         if carried[k] is None:
             start[1, at, :] = jnp.zeros((rows, dim), jnp.float32)
-        else:
-            start[0, at, :] = carried[k][0]
-            start[1, at, :] = carried[k][1]
     bias_in = bin_ref[...] * 0.5
     for copy in copies:
         copy.wait()
@@ -350,20 +367,20 @@
         return state, error
 
     state, error = lax.fori_loop(0, steps // many, some_steps, (start[0], start[1]))
+    for copy in late:
+        copy.wait()
     for k, (_, last) in enumerate(spans):
         part = slice(k * rows, (k + 1) * rows)
         if last < total:
             outs[k][0] = state[part]
             outs[k][1] = error[part]
             continue
-        both = error[part] / (dim * total) + squares[k][...] * (ACT_COST / (act_dim * total))
+        both = error[part] / (dim * total) + square[...] * (ACT_COST / (act_dim * total))
         cost = jnp.broadcast_to(jnp.sum(both, axis=1, keepdims=True), (rows, LANES))
         lane = lax.broadcasted_iota(jnp.int32, (cands, LANES), 1)
         table = jnp.zeros((cands, LANES), jnp.float32)
         for env in range(envs):
             table = jnp.where(lane == env, cost[env * cands : (env + 1) * cands], table)
-        for n in range(earlier):
-            outs[k][n] = before[n][0]
         outs[k][earlier] = table[:, :envs]
 
 
@@ -382,16 +399,15 @@
         (1 + len(before), cands, envs) if last == total else (2, rows, dim) for _, last in spans
     ]
     loose = carried + squares
+    assert len(squares) <= 1
     return pl.pallas_call(
         functools.partial(
             rollout_body, spans=spans, act_dim=act_dim, total=total, earlier=len(before), keep=keep
         ),
         grid=(1,),
-        in_specs=[HBM] * len(acts)
-        + [whole(a.shape) for a in loose]
+        in_specs=[HBM] * (len(acts) + len(loose))
         + [VMEM] * len(fixed)
-        + [whole(a.shape) for a in before]
-        + [whole(tie.shape) if keep else HBM],
+        + [HBM] * (len(before) + 1),
         out_specs=[whole(shape) for shape in shapes] + [VMEM] * keep,
         out_shape=[in_hbm(shape) for shape in shapes]
         + [jax.ShapeDtypeStruct(tie.shape, tie.dtype)] * keep,
@@ -400,7 +416,8 @@
             pltpu.VMEM((2, dim + 2 * act_dim, fixed[2].shape[1]), jnp.bfloat16),
             pltpu.VMEM((2, len(parts) * rows, dim), jnp.float32),
             pltpu.VMEM((len(parts) * rows, dim), jnp.float32),
-            pltpu.SemaphoreType.DMA((len(parts),)),
+            pltpu.VMEM((rows, LANES), jnp.float32),
+            pltpu.SemaphoreType.DMA((SLOTS,)),
         ],
         cost_estimate=pl.CostEstimate(flops=ROLL_FLOPS, bytes_accessed=1 << 20, transcendentals=0),
         compiler_params=pltpu.CompilerParams(vmem_limit_bytes=10 << 20),
@@ -454,7 +471,7 @@
                 costs[it] = out
         return outs[-1] if keep else outs[0]
 
-    noise, _ = noise_of(white, 0, 1, bias_out[None], act_dim, horizon)
+    (noise,) = noise_of(white, 0, 1, None, act_dim, horizon)
     state, tie = (mean_init, std_init), mine
     for it in range(iters):
         acts[it], asq[it], sums, own = actions_of(

time: 166 us -> 163 us (0.982)
  Pallas kernels: 63 us -> 57.6 us
  waiting for transfers between devices: 21.4 us -> 26 us
  starting transfers between devices: 41.6 us -> 39 us
    pallas_call x6, Pallas kernels: 40.1 us -> 36.3 us  [rollout(): pl.pallas_call(functools.partial(rollout_body, spans=spans, act_dim=act_d...]
    all_to_all x3, waiting for transfers between devices: 7.16 us -> 9.36 us  [shards(): parts = mix(sums)]
    all_to_all x3, starting transfers between devices: 18.7 us -> 16.8 us  [shards(): state = (mix(spread),)]
  transfers between devices with their start and end apart: 7 -> 7, of which waited for: 7 -> 7; matrix products, arithmetic and copies ran while one was open for 0% -> 0% of each run, Pallas kernels for 29% -> 27%
where the time goes in v6:
time: 163 us; the launch traced here: 162 us
  Pallas kernels  57.6 us (35%)
  starting transfers between devices  39 us (24%)
  blocking collectives  38 us (23%)
  waiting for transfers between devices  26 us (16%)
    all_to_all x2, blocking collectives, shards(): peaks = lax.all_to_all(peak, 'env', 0, 0, tiled=True)  38 us
    pallas_call x6, Pallas kernels, rollout(): pl.pallas_call(functools.partial(rollout_body, spans=spans, act_dim=act_d...  36.3 us
    all_to_all x3, starting transfers between devices, shards(): parts = mix(sums)  18.7 us
    all_to_all x3, starting transfers between devices, shards(): state = (mix(spread),)  16.8 us
    pallas_call x2, Pallas kernels, noise_of(): pl.pallas_call(functools.partial(noise_body, act_dim=act_dim, blocks=widt...  11.2 us
    all_to_all x3, waiting for transfers between devices, shards(): parts = mix(sums)  9.36 us
    all_to_all x3, waiting for transfers between devices, shards(): state = (mix(spread),)  9.06 us
    all_to_all x1, waiting for transfers between devices, shards(): peaks = lax.all_to_all(peak, 'env', 0, 0, tiled=True)  7.59 us
  transfers between devices with their start and end apart: 7, of which 7 were waited for; matrix products, arithmetic and copies ran while one was open for 0% of the time, Pallas kernels for 27%

profile of v6, /device:TPU:1, one launch (start us, length us, event | category | flops | bytes accessed | tf_op | source)
XLA Modules:
  0.0 161.6 jit_solution(15519589399889375073)
XLA Ops:
  0.6 0.0 copy-start.5
  0.6 0.0 copy-start.7
  0.7 0.0 copy-start.6
  0.7 4.2 %noise.2.refs_0_ = f32[1,128,2560]{2,1,0:T(8,128)S(1)} custom-call(bf16[3,128,4096]{2,1,0:T(8,128)(2,1)} %bitcast.21), custom_call_target="tpu_custom_call" | custom-call | flops 268435456 | bytes 1048576 | tf_op jit(solution)/shard_map/noise/pallas_call | solution.py:94
  4.8 0.0 copy-done.5
  4.8 0.0 copy-done.7
  4.8 0.0 copy-done.6
  4.9 1.7 %actions.3 = (bf16[128,2560]{1,0:T(8,128)(2,1)}, f32[128,128]{1,0:T(8,128)}, f32[32,2,1280]{2,1,0:T(2,128)}, f32[2,1280]{1,0:T(2,128)}) custom-call(f32[1,128,2560]{2,1,0:T(8,128)S(1)} %noise.2.refs_0_, s32[3,16,25]{2,1,0:T(8,128)S(1)} %bitcast.6, s32[1]{0:T(128)} %bitcast.2.refs_2_.refs_3_.tie_ref, s32[1]{0:T(128)} %bitcast.2.refs_2_.refs_3_.tie_ref, ...), custom_call_target="tpu_custom_call" | custom-call | tf_op jit(solution)/shard_map/actions/pallas_call | solution.py:193
  6.6 0.0 copy-start
  6.6 0.0 copy-start.1
  6.6 0.0 copy-start.2
  6.6 0.0 copy-start.3
  6.6 0.0 copy-start.4
  6.6 0.0 copy-start.8
  6.6 0.0 copy-start.9
  6.7 10.5 %all-to-all-start = ((f32[32,2,1280]{2,1,0:T(2,128)}), f32[32,2,1280]{2,1,0:T(2,128)S(1)}, u32[]{:S(2)}, u32[]{:S(2)}) async-start(f32[32,2,1280]{2,1,0:T(2,128)} %get-tuple-element.42), calls=%async_computation | async-start | bytes 655360 | tf_op jit(solution)/shard_map/all_to_all | solution.py:480
  17.2 7.0 %noise.3 = (f32[2,128,2560]{2,1,0:T(8,128)S(1)}, f32[2,1280]{1,0:T(2,128)S(1)}) custom-call(bf16[3,128,4096]{2,1,0:T(8,128)(2,1)} %bitcast.22, f32[2,1280]{1,0:T(2,128)} %get-tuple-element.39.refs_1_), custom_call_target="tpu_custom_call" | custom-call | flops 268435456 | bytes 1048576 | tf_op jit(solution)/shard_map/noise/pallas_call | solution.py:94
  24.2 2.6 %all-to-all-done.parts_ref = f32[32,2,1280]{2,1,0:T(2,128)S(1)} async-done(((f32[32,2,1280]{2,1,0:T(2,128)}), f32[32,2,1280]{2,1,0:T(2,128)S(1)}, u32[]{:S(2)}, u32[]{:S(2)}) %all-to-all-start) | async-done | bytes 327712 | tf_op jit(solution)/shard_map/all_to_all | solution.py:480
  26.8 0.3 refit.3
  27.1 24.2 %all_to_all.45.peak_ref = f32[16,1,128]{2,1,0:T(1,128)S(1)} all-to-all(f32[16,1,128]{2,1,0:T(1,128)S(1)} %get-tuple-element.45), channel_id=1, replica_groups=mesh['env'=16,'cand'=32] {'env'}, dimensions={0} | all-to-all | bytes 16384 | tf_op jit(solution)/shard_map/all_to_all | solution.py:488
  51.3 0.8 to_all.3
  52.0 6.3 %all-to-all-start.2 = ((f32[32,2,1408]{2,1,0:T(2,128)}), f32[32,2,1408]{2,1,0:T(2,128)S(1)}, u32[]{:S(2)}, u32[]{:S(2)}) async-start(f32[32,2,1408]{2,1,0:T(2,128)} %get-tuple-element.47), calls=%async_computation.2 | async-start | bytes 720896 | tf_op jit(solution)/shard_map/all_to_all | solution.py:491
  58.3 0.0 copy-done
  58.4 6.1 %rollout.6.refs_3_.refs_2_ = f32[2,128,128]{2,1,0:T(8,128)} custom-call(bf16[128,2560]{1,0:T(8,128)(2,1)} %get-tuple-element.41.refs_0_, f32[16,128]{1,0:T(8,128)S(1)} %copy-done.3, f32[16,128]{1,0:T(8,128)S(1)} %copy-done.4, bf16[128,512]{1,0:T(8,128)(2,1)S(1)} %copy-done, bf16[64,512]{1,0:T(8,128)(2,1)S(1)} %copy-done.2, bf16[512,128]{1,0:T(8,128)(2,1)S(1)} %copy-done.1, ...), custom_call_target="tpu_custom_call" | custom-call | flops 268435456 | bytes 1048576 | tf_op jit(solution)/shard_map/rollout/pallas_call | solution.py:403
  64.5 3.7 %all-to-all-done.2.refs_4_ = f32[32,2,1408]{2,1,0:T(2,128)S(1)} async-done(((f32[32,2,1408]{2,1,0:T(2,128)}), f32[32,2,1408]{2,1,0:T(2,128)S(1)}, u32[]{:S(2)}, u32[]{:S(2)}) %all-to-all-start.2) | async-done | bytes 360480 | tf_op jit(solution)/shard_map/all_to_all | solution.py:491
  68.2 1.9 %actions.4 = (bf16[128,2560]{1,0:T(8,128)(2,1)}, f32[128,128]{1,0:T(8,128)}, f32[32,2,1280]{2,1,0:T(2,128)}, f32[2,1280]{1,0:T(2,128)}) custom-call(f32[2,128,2560]{2,1,0:T(8,128)S(1)} %get-tuple-element.40.refs_0_, s32[3,16,25]{2,1,0:T(8,128)S(1)} %bitcast.7, s32[1]{0:T(128)} %bitcast.2.refs_2_.refs_3_.tie_ref, f32[2,128,128]{2,1,0:T(8,128)} %rollout.6.refs_3_.refs_2_, ...), custom_call_target="tpu_custom_call" | custom-call | tf_op jit(solution)/shard_map/actions/pallas_call | solution.py:193
  70.1 3.9 %all-to-all-start.3 = ((f32[32,2,1280]{2,1,0:T(2,128)}), f32[32,2,1280]{2,1,0:T(2,128)S(1)}, u32[]{:S(2)}, u32[]{:S(2)}) async-start(f32[32,2,1280]{2,1,0:T(2,128)} %get-tuple-element.53), calls=%async_computation.3 | async-start | bytes 655360 | tf_op jit(solution)/shard_map/all_to_all | solution.py:480
  73.9 5.6 %rollout.7 = (f32[2,128,128]{2,1,0:T(8,128)}, f32[2,128,128]{2,1,0:T(8,128)}, f32[2,1280]{1,0:T(2,128)S(1)}) custom-call(bf16[128,2560]{1,0:T(8,128)(2,1)} %get-tuple-element.41.refs_0_, bf16[128,2560]{1,0:T(8,128)(2,1)} %get-tuple-element.48.refs_1_.refs_0_, f32[2,128,128]{2,1,0:T(8,128)} %rollout.6.refs_3_.refs_2_, f32[16,128]{1,0:T(8,128)S(1)} %copy-done.3, ...), custom_call_target="tpu_custom_call" | custom-call | flops 268435456 | bytes 1048576 | tf_op jit(solution)/shard_map/rollout/pallas_call | solution.py:403
  79.5 4.0 %all-to-all-done.3.parts_ref = f32[32,2,1280]{2,1,0:T(2,128)S(1)} async-done(((f32[32,2,1280]{2,1,0:T(2,128)}), f32[32,2,1280]{2,1,0:T(2,128)S(1)}, u32[]{:S(2)}, u32[]{:S(2)}) %all-to-all-start.3) | async-done | bytes 327712 | tf_op jit(solution)/shard_map/all_to_all | solution.py:480
  83.5 0.3 refit.4
  83.8 13.8 %all_to_all.46.peak_ref = f32[16,1,128]{2,1,0:T(1,128)S(1)} all-to-all(f32[16,1,128]{2,1,0:T(1,128)S(1)} %get-tuple-element.56), channel_id=1, replica_groups=mesh['env'=16,'cand'=32] {'env'}, dimensions={0} | all-to-all | bytes 16384 | tf_op jit(solution)/shard_map/all_to_all | solution.py:488
  97.6 0.8 to_all.4
  98.4 4.9 %all-to-all-start.5 = ((f32[32,2,1408]{2,1,0:T(2,128)}), f32[32,2,1408]{2,1,0:T(2,128)S(1)}, u32[]{:S(2)}, u32[]{:S(2)}) async-start(f32[32,2,1408]{2,1,0:T(2,128)} %get-tuple-element.59), calls=%async_computation.5 | async-start | bytes 720896 | tf_op jit(solution)/shard_map/all_to_all | solution.py:491
  103.3 6.7 %rollout.8 = (f32[1,8,16]{2,1,0:T(8,128)}, f32[2,128,128]{2,1,0:T(8,128)}) custom-call(bf16[128,2560]{1,0:T(8,128)(2,1)} %get-tuple-element.41.refs_0_, bf16[128,2560]{1,0:T(8,128)(2,1)} %get-tuple-element.48.refs_1_.refs_0_, f32[2,128,128]{2,1,0:T(8,128)} %get-tuple-element.50.refs_2_, f32[2,128,128]{2,1,0:T(8,128)} %get-tuple-element.51.refs_3_, ...), custom_call_target="tpu_custom_call" | custom-call | flops 268435456 | bytes 1048576 | tf_op jit(solution)/shard_map/rollout/pallas_call | solution.py:403
  110.0 3.2 %all-to-all-done.5.refs_4_ = f32[32,2,1408]{2,1,0:T(2,128)S(1)} async-done(((f32[32,2,1408]{2,1,0:T(2,128)}), f32[32,2,1408]{2,1,0:T(2,128)S(1)}, u32[]{:S(2)}, u32[]{:S(2)}) %all-to-all-start.5) | async-done | bytes 360480 | tf_op jit(solution)/shard_map/all_to_all | solution.py:491
  113.2 1.9 %actions.5 = (bf16[128,2560]{1,0:T(8,128)(2,1)}, f32[128,128]{1,0:T(8,128)}, f32[32,2,1280]{2,1,0:T(2,128)}, f32[2,1280]{1,0:T(2,128)}) custom-call(f32[2,128,2560]{2,1,0:T(8,128)S(1)} %get-tuple-element.40.refs_0_, s32[3,16,25]{2,1,0:T(8,128)S(1)} %bitcast.8, s32[1]{0:T(128)} %bitcast.2.refs_2_.refs_3_.tie_ref, ...), custom_call_target="tpu_custom_call" | custom-call | tf_op jit(solution)/shard_map/actions/pallas_call | solution.py:193
  115.1 4.3 %all-to-all-start.6 = ((f32[32,2,1280]{2,1,0:T(2,128)}), f32[32,2,1280]{2,1,0:T(2,128)S(1)}, u32[]{:S(2)}, u32[]{:S(2)}) async-start(f32[32,2,1280]{2,1,0:T(2,128)} %get-tuple-element.60), calls=%async_computation.6 | async-start | bytes 655360 | tf_op jit(solution)/shard_map/all_to_all | solution.py:480
  119.5 6.7 %rollout.9 = (f32[1,8,16]{2,1,0:T(8,128)}, f32[2,128,128]{2,1,0:T(8,128)}, f32[2,1280]{1,0:T(2,128)S(1)}) custom-call(bf16[128,2560]{1,0:T(8,128)(2,1)} %get-tuple-element.48.refs_1_.refs_0_, bf16[128,2560]{1,0:T(8,128)(2,1)} %get-tuple-element.61.refs_1_.refs_0_, f32[2,128,128]{2,1,0:T(8,128)} %get-tuple-element.62.refs_2_, ...), custom_call_target="tpu_custom_call" | custom-call | flops 268435456 | bytes 1048576 | tf_op jit(solution)/shard_map/rollout/pallas_call | solution.py:403
  126.2 2.8 %all-to-all-done.6.parts_ref = f32[32,2,1280]{2,1,0:T(2,128)S(1)} async-done(((f32[32,2,1280]{2,1,0:T(2,128)}), f32[32,2,1280]{2,1,0:T(2,128)S(1)}, u32[]{:S(2)}, u32[]{:S(2)}) %all-to-all-start.6) | async-done | bytes 327712 | tf_op jit(solution)/shard_map/all_to_all | solution.py:480
  129.0 0.9 refit.5
  129.8 3.5 %all-to-all-start.7 = ((f32[16,1,128]{2,1,0:T(1,128)}), f32[16,1,128]{2,1,0:T(1,128)S(1)}, u32[]{:S(2)}, u32[]{:S(2)}) async-start(f32[16,1,128]{2,1,0:T(1,128)} %get-tuple-element.67.refs_9_), calls=%async_computation.7 | async-start | bytes 16384 | tf_op jit(solution)/shard_map/all_to_all | solution.py:488
  133.3 3.6 %rollout.10.tie_ref.refs_1_ = f32[2,128,128]{2,1,0:T(8,128)} custom-call(bf16[128,2560]{1,0:T(8,128)(2,1)} %get-tuple-element.61.refs_1_.refs_0_, f32[2,128,128]{2,1,0:T(8,128)} %get-tuple-element.68.refs_1_, f32[16,128]{1,0:T(8,128)S(1)} %copy-done.3, f32[16,128]{1,0:T(8,128)S(1)} %copy-done.4, bf16[128,512]{1,0:T(8,128)(2,1)S(1)} %copy-done, ...), custom_call_target="tpu_custom_call" | custom-call | flops 268435456 | bytes 1048576 | tf_op jit(solution)/shard_map/rollout/pallas_call | solution.py:403
  136.9 7.6 %all-to-all-done.7.peak_ref = f32[16,1,128]{2,1,0:T(1,128)S(1)} async-done(((f32[16,1,128]{2,1,0:T(1,128)}), f32[16,1,128]{2,1,0:T(1,128)S(1)}, u32[]{:S(2)}, u32[]{:S(2)}) %all-to-all-start.7) | async-done | bytes 8224 | tf_op jit(solution)/shard_map/all_to_all | solution.py:488
  144.5 0.8 to_all.5
  145.3 5.7 %all-to-all-start.8 = ((f32[32,2,1408]{2,1,0:T(2,128)}), f32[32,2,1408]{2,1,0:T(2,128)S(1)}, u32[]{:S(2)}, u32[]{:S(2)}) async-start(f32[32,2,1408]{2,1,0:T(2,128)} %get-tuple-element.69), calls=%async_computation.8 | async-start | bytes 720896 | tf_op jit(solution)/shard_map/all_to_all | solution.py:491
  150.9 7.6 %rollout.11 = f32[3,8,16]{2,1,0:T(8,128)} custom-call(bf16[128,2560]{1,0:T(8,128)(2,1)} %get-tuple-element.61.refs_1_.refs_0_, f32[2,128,128]{2,1,0:T(8,128)} %rollout.10.tie_ref.refs_1_, f32[128,128]{1,0:T(8,128)} %get-tuple-element.72.refs_2_, f32[16,128]{1,0:T(8,128)S(1)} %copy-done.3, f32[16,128]{1,0:T(8,128)S(1)} %copy-done.4, ...), custom_call_target="tpu_custom_call" | custom-call | flops 268435456 | bytes 1048576 | tf_op jit(solution)/shard_map/rollout/pallas_call | solution.py:403
  158.6 2.2 %all-to-all-done.8.state_ref = f32[32,2,1408]{2,1,0:T(2,128)S(1)} async-done(((f32[32,2,1408]{2,1,0:T(2,128)}), f32[32,2,1408]{2,1,0:T(2,128)S(1)}, u32[]{:S(2)}, u32[]{:S(2)}) %all-to-all-start.8) | async-done | bytes 360480 | tf_op jit(solution)/shard_map/all_to_all | solution.py:491
  160.8 0.8 finished.1
  (6 shorter events, 0.0 us)
Async XLA Ops:
  0.6 4.2 %copy-start.5 = (s32[16,3,25]{2,0,1:T(8,128)S(1)}, s32[16,3,25]{2,0,1:T(8,128)}, u32[]{:S(2)}) copy-start(s32[16,3,25]{2,0,1:T(8,128)} %param.21) | copy-start | bytes 14404
  0.6 4.2 %copy-start.7 = (f32[16,2560]{1,0:T(8,128)S(1)}, f32[16,2560]{1,0:T(8,128)}, u32[]{:S(2)}) copy-start(f32[16,2560]{1,0:T(8,128)} %refs_5_.7) | copy-start | bytes 491524
  0.7 4.2 %copy-start.6 = (f32[16,2560]{1,0:T(8,128)S(1)}, f32[16,2560]{1,0:T(8,128)}, u32[]{:S(2)}) copy-start(f32[16,2560]{1,0:T(8,128)} %refs_4_.6) | copy-start | bytes 491524
  6.6 51.8 %copy-start = (bf16[128,512]{1,0:T(8,128)(2,1)S(1)}, bf16[128,512]{1,0:T(8,128)(2,1)}, u32[]{:S(2)}) copy-start(bf16[128,512]{1,0:T(8,128)(2,1)} %refs_5_.13) | copy-start | bytes 393220
  6.6 51.8 %copy-start.1 = (bf16[512,128]{1,0:T(8,128)(2,1)S(1)}, bf16[512,128]{1,0:T(8,128)(2,1)}, u32[]{:S(2)}) copy-start(bf16[512,128]{1,0:T(8,128)(2,1)} %refs_7_.7) | copy-start | bytes 393220
  6.6 51.8 %copy-start.2 = (bf16[64,512]{1,0:T(8,128)(2,1)S(1)}, bf16[64,512]{1,0:T(8,128)(2,1)}, u32[]{:S(2)}) copy-start(bf16[64,512]{1,0:T(8,128)(2,1)} %refs_6_.9) | copy-start | bytes 196612
  6.6 51.8 %copy-start.3 = (f32[16,128]{1,0:T(8,128)S(1)}, f32[16,128]{1,0:T(8,128)}, u32[]{:S(2)}) copy-start(f32[16,128]{1,0:T(8,128)} %refs_3_.7) | copy-start | bytes 24580
  6.6 51.7 %copy-start.4 = (f32[16,128]{1,0:T(8,128)S(1)}, f32[16,128]{1,0:T(8,128)}, u32[]{:S(2)}) copy-start(f32[16,128]{1,0:T(8,128)} %refs_4_.11) | copy-start | bytes 24580
  6.6 51.7 %copy-start.8 = (f32[512]{0:T(512)S(1)}, f32[512]{0:T(512)}, u32[]{:S(2)}) copy-start(f32[512]{0:T(512)} %param.19) | copy-start | bytes 6148
  6.6 51.7 %copy-start.9 = (f32[128]{0:T(128)S(1)}, f32[128]{0:T(128)}, u32[]{:S(2)}) copy-start(f32[128]{0:T(128)} %param.20) | copy-start | bytes 1540
  6.7 20.1 %all-to-all-start = ((f32[32,2,1280]{2,1,0:T(2,128)}), f32[32,2,1280]{2,1,0:T(2,128)S(1)}, u32[]{:S(2)}, u32[]{:S(2)}) async-start(f32[32,2,1280]{2,1,0:T(2,128)} %get-tuple-element.42), calls=%async_computation | async-start | bytes 655360 | tf_op jit(solution)/shard_map/all_to_all | solution.py:480
  52.0 16.1 %all-to-all-start.2 = ((f32[32,2,1408]{2,1,0:T(2,128)}), f32[32,2,1408]{2,1,0:T(2,128)S(1)}, u32[]{:S(2)}, u32[]{:S(2)}) async-start(f32[32,2,1408]{2,1,0:T(2,128)} %get-tuple-element.47), calls=%async_computation.2 | async-start | bytes 720896 | tf_op jit(solution)/shard_map/all_to_all | solution.py:491
  70.1 13.4 %all-to-all-start.3 = ((f32[32,2,1280]{2,1,0:T(2,128)}), f32[32,2,1280]{2,1,0:T(2,128)S(1)}, u32[]{:S(2)}, u32[]{:S(2)}) async-start(f32[32,2,1280]{2,1,0:T(2,128)} %get-tuple-element.53), calls=%async_computation.3 | async-start | bytes 655360 | tf_op jit(solution)/shard_map/all_to_all | solution.py:480
  98.4 14.8 %all-to-all-start.5 = ((f32[32,2,1408]{2,1,0:T(2,128)}), f32[32,2,1408]{2,1,0:T(2,128)S(1)}, u32[]{:S(2)}, u32[]{:S(2)}) async-start(f32[32,2,1408]{2,1,0:T(2,128)} %get-tuple-element.59), calls=%async_computation.5 | async-start | bytes 720896 | tf_op jit(solution)/shard_map/all_to_all | solution.py:491
  115.1 13.9 %all-to-all-start.6 = ((f32[32,2,1280]{2,1,0:T(2,128)}), f32[32,2,1280]{2,1,0:T(2,128)S(1)}, u32[]{:S(2)}, u32[]{:S(2)}) async-start(f32[32,2,1280]{2,1,0:T(2,128)} %get-tuple-element.60), calls=%async_computation.6 | async-start | bytes 655360 | tf_op jit(solution)/shard_map/all_to_all | solution.py:480
  129.8 14.6 %all-to-all-start.7 = ((f32[16,1,128]{2,1,0:T(1,128)}), f32[16,1,128]{2,1,0:T(1,128)S(1)}, u32[]{:S(2)}, u32[]{:S(2)}) async-start(f32[16,1,128]{2,1,0:T(1,128)} %get-tuple-element.67.refs_9_), calls=%async_computation.7 | async-start | bytes 16384 | tf_op jit(solution)/shard_map/all_to_all | solution.py:488
  145.3 15.5 %all-to-all-start.8 = ((f32[32,2,1408]{2,1,0:T(2,128)}), f32[32,2,1408]{2,1,0:T(2,128)S(1)}, u32[]{:S(2)}, u32[]{:S(2)}) async-start(f32[32,2,1408]{2,1,0:T(2,128)} %get-tuple-element.69), calls=%async_computation.8 | async-start | bytes 720896 | tf_op jit(solution)/shard_map/all_to_all | solution.py:491

commit v7 on v6

--- a/solution.py
+++ b/solution.py
@@ -40,45 +40,65 @@
     return np.asarray(kernel, np.float32).astype(jnp.bfloat16).astype(np.float32)
 
 
-def noise_body(*refs, act_dim, blocks, first, parts, keep):
-    white_ref, out_ref, rows_in, fill, sems = refs[0], refs[1 + keep], *refs[-3:]
-    count = out_ref.shape[0]
+def noise_body(*refs, act_dim, first, keep):
+    white_ref, out_ref = refs[0], refs[1 + keep]
+    rows_in, packed, fill, sems = refs[-4:]
+    count, _, width = out_ref.shape
+    flat = white_ref.shape[2]
+    length = flat // act_dim
+    group = act_dim // 2
+    per = 256 // group
+    part = length * group
+
+    def fetch(one):
+        return pltpu.make_async_copy(white_ref.at[first + one], rows_in.at[one], sems.at[one])
+
+    for one in range(count):
+        fetch(one).start()
     if keep:
-        hand = pltpu.make_async_copy(refs[1], refs[3], sems.at[count * parts])
+        hand = pltpu.make_async_copy(refs[1], refs[3], sems.at[count])
         hand.start()
-    _, rows, flat = white_ref.shape
-    length = flat // act_dim
-    size = rows // parts
-
-    def fetch(one, part):
-        at = pl.ds(part * size, size)
-        return pltpu.make_async_copy(
-            white_ref.at[first + one, at, :], rows_in.at[one, at, :], sems.at[one * parts + part]
-        )
+    kernel = color_kernel(length)
+    row = lax.broadcasted_iota(jnp.int32, (group, 256), 0)
+    hit = lax.broadcasted_iota(jnp.int32, (group, 256), 1) % group == row
+    spot = lax.broadcasted_iota(jnp.int32, (1, 256), 1) // group
+
+    def step_at(n):
+        return n // 4 * 4 + (0, 2, 1, 3)[n % 4]
+
+    for n in range(length):
+        band = jnp.full((1, 256), float(kernel[-step_at(n) % length]), jnp.float32)
+        for q in range(1, per):
+            band = jnp.where(spot == q, float(kernel[(step_at(q) - step_at(n)) % length]), band)
+        tile = jnp.where(hit, band, 0.0).astype(jnp.bfloat16)
+        fill[pl.ds(n * group, group), :] = tile
+        fill[pl.ds(part + n * group, group), :] = tile
+    even = lax.broadcasted_iota(jnp.int32, (1, LANES), 1) // group % 2 == 0
+
+    def swap(a, b):
+        low = jnp.where(even, a, pltpu.roll(b, group, 1))
+        return low, jnp.where(even, pltpu.roll(a, LANES - group, 1), b)
 
     for one in range(count):
-        for part in range(parts):
-            fetch(one, part).start()
-    kernel = color_kernel(length)
-    row = lax.broadcasted_iota(jnp.int32, (act_dim, 256), 0)
-    lane = lax.broadcasted_iota(jnp.int32, (act_dim, 256), 1)
-    hit = lane % act_dim == row
-    quarter = lax.broadcasted_iota(jnp.int32, (1, 256), 1) // act_dim
-    for j in range(length):
-        band = jnp.full((1, 256), float(kernel[-j % length]), jnp.float32)
-        for q in range(1, 256 // act_dim):
-            band = jnp.where(quarter == q, float(kernel[(q - j) % length]), band)
-        tile = jnp.where(hit, band, 0.0).astype(jnp.bfloat16)
-        fill[pl.ds(j * act_dim, act_dim), :] = tile
-        fill[pl.ds(flat + j * act_dim, act_dim), :] = tile
-    for one in range(count):
-        for part in range(parts):
-            fetch(one, part).wait()
-        for block in range(blocks):
-            start = (flat - block * 256) % flat
-            out_ref[one, :, pl.ds(block * 256, 256)] = jnp.dot(
-                rows_in[one], fill[pl.ds(start, flat), :], preferred_element_type=jnp.float32
-            )
+        fetch(one).wait()
+        for k in range(flat // 256):
+            pair = [
+                rows_in[one, :, pl.ds(k * 256 + side * LANES, LANES)].astype(jnp.float32)
+                for side in range(2)
+            ]
+            for side, piece in enumerate(swap(*pair)):
+                packed[side, :, pl.ds(k * LANES, LANES)] = piece.astype(jnp.bfloat16)
+        for block in range(width // (per * act_dim)):
+            weights = fill[pl.ds((part - block * 256) % part, part), :]
+            sides = [
+                jnp.dot(packed[side], weights, preferred_element_type=jnp.float32)
+                for side in range(2)
+            ]
+            for h in range(2):
+                pair = [side[:, h * LANES : (h + 1) * LANES] for side in sides]
+                at = block * 512 + h * 256
+                for side, piece in enumerate(swap(*pair)):
+                    out_ref[one, :, pl.ds(at + side * LANES, LANES)] = piece
     if keep:
         hand.wait()
 
@@ -86,22 +106,21 @@
 def noise_of(white, first, count, own, act_dim, horizon):
     _, rows, flat = white.shape
     width = horizon * act_dim
-    parts = 1
     keep = own is not None
+    assert act_dim == 64 and horizon % 8 == 0
     shapes = [jax.ShapeDtypeStruct((count, rows, width), jnp.float32)]
     if keep:
         shapes.append(jax.ShapeDtypeStruct(own.shape, own.dtype))
     return pl.pallas_call(
-        functools.partial(
-            noise_body, act_dim=act_dim, blocks=width // 256, first=first, parts=parts, keep=keep
-        ),
+        functools.partial(noise_body, act_dim=act_dim, first=first, keep=keep),
         in_specs=[HBM] * (1 + keep),
         out_specs=[VMEM] * (1 + keep),
         out_shape=shapes,
         scratch_shapes=[
             pltpu.VMEM((count, rows, flat), jnp.bfloat16),
-            pltpu.VMEM((2 * flat, 256), jnp.bfloat16),
-            pltpu.SemaphoreType.DMA((count * parts + 1,)),
+            pltpu.VMEM((2, rows, flat // 2), jnp.bfloat16),
+            pltpu.VMEM((flat, 256), jnp.bfloat16),
+            pltpu.SemaphoreType.DMA((count + 1,)),
         ],
         cost_estimate=pl.CostEstimate(flops=ROLL_FLOPS, bytes_accessed=1 << 20, transcendentals=0),
         compiler_params=pltpu.CompilerParams(vmem_limit_bytes=16 << 20),
@@ -481,7 +500,7 @@
         if it == 0:
             noise, own = noise_of(white, 1, iters - 1, own, act_dim, horizon)
         elif it == 1:
-            own = play([(0, 14, 26), (1, 0, 12)], own, keep=True)
+            own = play([(0, 14, 28), (1, 0, 14)], own, keep=True)
         else:
             own = play([(1, 26, horizon), (2, 0, 14)], own, keep=True)
         piece, peak = refit(parts, own, elites, groups)
@@ -492,7 +511,7 @@
         if it == 0:
             tie = play([(0, 0, 14)], token)
         elif it == 1:
-            tie = play([(0, 26, horizon), (1, 12, 26)], token)
+            tie = play([(0, 28, horizon), (1, 14, 26)], token)
         else:
             tie = play([(2, 20, horizon)], token, (costs[0], costs[1]))
     mean, std = finished(state[0], envs, width, envs_total)

time: 163 us -> 161 us (0.988)
  Pallas kernels: 57.6 us -> 54.5 us
  waiting for transfers between devices: 26 us -> 28.3 us
    pallas_call x2, Pallas kernels: 11.2 us -> 8.1 us  [noise_of(): pl.pallas_call(functools.partial(noise_body, act_dim=act_dim, first=first...]
  transfers between devices with their start and end apart: 7 -> 7, of which waited for: 7 -> 7; matrix products, arithmetic and copies ran while one was open for 0% -> 0% of each run, Pallas kernels for 27% -> 26%
where the time goes in v7:
time: 161 us; the launch traced here: 160 us
  Pallas kernels  54.5 us (34%)
  starting transfers between devices  38 us (24%)
  blocking collectives  38 us (24%)
  waiting for transfers between devices  28.3 us (18%)
    all_to_all x2, blocking collectives, shards(): peaks = lax.all_to_all(peak, 'env', 0, 0, tiled=True)  38 us
    pallas_call x6, Pallas kernels, rollout(): pl.pallas_call(functools.partial(rollout_body, spans=spans, act_dim=act_d...  36.3 us
    all_to_all x3, starting transfers between devices, shards(): parts = mix(sums)  18.1 us
    all_to_all x3, starting transfers between devices, shards(): state = (mix(spread),)  16.5 us
    all_to_all x3, waiting for transfers between devices, shards(): parts = mix(sums)  10.5 us
    all_to_all x3, waiting for transfers between devices, shards(): state = (mix(spread),)  10.2 us
    pallas_call x2, Pallas kernels, noise_of(): pl.pallas_call(functools.partial(noise_body, act_dim=act_dim, first=first...  8.1 us
    all_to_all x1, waiting for transfers between devices, shards(): peaks = lax.all_to_all(peak, 'env', 0, 0, tiled=True)  7.58 us
  transfers between devices with their start and end apart: 7, of which 7 were waited for; matrix products, arithmetic and copies ran while one was open for 0% of the time, Pallas kernels for 26%

profile of v7, /device:TPU:1, one launch (start us, length us, event | category | flops | bytes accessed | tf_op | source)
XLA Modules:
  0.0 159.8 jit_solution(1280453283940163297)
XLA Ops:
  0.7 3.1 %noise.2.refs_0_ = f32[1,128,2560]{2,1,0:T(8,128)S(1)} custom-call(bf16[3,128,4096]{2,1,0:T(8,128)(2,1)} %bitcast.21), custom_call_target="tpu_custom_call" | custom-call | flops 268435456 | bytes 1048576 | tf_op jit(solution)/shard_map/noise/pallas_call | solution.py:114
  3.8 1.7 %actions.3 = (bf16[128,2560]{1,0:T(8,128)(2,1)}, f32[128,128]{1,0:T(8,128)}, f32[32,2,1280]{2,1,0:T(2,128)}, f32[2,1280]{1,0:T(2,128)}) custom-call(f32[1,128,2560]{2,1,0:T(8,128)S(1)} %noise.2.refs_0_, s32[3,16,25]{2,1,0:T(8,128)S(1)} %bitcast.6, s32[1]{0:T(128)} %bitcast.2.refs_2_.refs_3_.tie_ref, s32[1]{0:T(128)} %bitcast.2.refs_2_.refs_3_.tie_ref, ...), custom_call_target="tpu_custom_call" | custom-call | tf_op jit(solution)/shard_map/actions/pallas_call | solution.py:212
  5.6 0.0 copy-start
  5.6 0.0 copy-start.1
  5.6 0.0 copy-start.2
  5.6 0.0 copy-start.3
  5.6 0.0 copy-start.4
  5.6 0.0 copy-start.8
  5.6 0.0 copy-start.9
  5.6 10.5 %all-to-all-start = ((f32[32,2,1280]{2,1,0:T(2,128)}), f32[32,2,1280]{2,1,0:T(2,128)S(1)}, u32[]{:S(2)}, u32[]{:S(2)}) async-start(f32[32,2,1280]{2,1,0:T(2,128)} %get-tuple-element.42), calls=%async_computation | async-start | bytes 655360 | tf_op jit(solution)/shard_map/all_to_all | solution.py:499
  16.2 5.0 %noise.3 = (f32[2,128,2560]{2,1,0:T(8,128)S(1)}, f32[2,1280]{1,0:T(2,128)S(1)}) custom-call(bf16[3,128,4096]{2,1,0:T(8,128)(2,1)} %bitcast.22, f32[2,1280]{1,0:T(2,128)} %get-tuple-element.39.refs_1_), custom_call_target="tpu_custom_call" | custom-call | flops 268435456 | bytes 1048576 | tf_op jit(solution)/shard_map/noise/pallas_call | solution.py:114
  21.1 4.7 %all-to-all-done.parts_ref = f32[32,2,1280]{2,1,0:T(2,128)S(1)} async-done(((f32[32,2,1280]{2,1,0:T(2,128)}), f32[32,2,1280]{2,1,0:T(2,128)S(1)}, u32[]{:S(2)}, u32[]{:S(2)}) %all-to-all-start) | async-done | bytes 327712 | tf_op jit(solution)/shard_map/all_to_all | solution.py:499
  25.8 0.3 refit.3
  26.1 24.2 %all_to_all.45.peak_ref = f32[16,1,128]{2,1,0:T(1,128)S(1)} all-to-all(f32[16,1,128]{2,1,0:T(1,128)S(1)} %get-tuple-element.45), channel_id=1, replica_groups=mesh['env'=16,'cand'=32] {'env'}, dimensions={0} | all-to-all | bytes 16384 | tf_op jit(solution)/shard_map/all_to_all | solution.py:507
  50.2 0.8 to_all.3
  51.0 5.1 %all-to-all-start.2 = ((f32[32,2,1408]{2,1,0:T(2,128)}), f32[32,2,1408]{2,1,0:T(2,128)S(1)}, u32[]{:S(2)}, u32[]{:S(2)}) async-start(f32[32,2,1408]{2,1,0:T(2,128)} %get-tuple-element.47), calls=%async_computation.2 | async-start | bytes 720896 | tf_op jit(solution)/shard_map/all_to_all | solution.py:510
  56.1 0.0 copy-done
  56.1 0.0 copy-done.1
  56.2 0.0 copy-done.2
  56.2 0.0 copy-done.3
  56.2 0.0 copy-done.4
  56.2 0.0 copy-done.8
  56.2 0.0 copy-done.9
  56.2 6.1 %rollout.6.refs_3_.refs_2_ = f32[2,128,128]{2,1,0:T(8,128)} custom-call(bf16[128,2560]{1,0:T(8,128)(2,1)} %get-tuple-element.41.refs_0_, f32[16,128]{1,0:T(8,128)S(1)} %copy-done.3, f32[16,128]{1,0:T(8,128)S(1)} %copy-done.4, bf16[128,512]{1,0:T(8,128)(2,1)S(1)} %copy-done, bf16[64,512]{1,0:T(8,128)(2,1)S(1)} %copy-done.2, bf16[512,128]{1,0:T(8,128)(2,1)S(1)} %copy-done.1, ...), custom_call_target="tpu_custom_call" | custom-call | flops 268435456 | bytes 1048576 | tf_op jit(solution)/shard_map/rollout/pallas_call | solution.py:422
  62.3 3.8 %all-to-all-done.2.refs_4_ = f32[32,2,1408]{2,1,0:T(2,128)S(1)} async-done(((f32[32,2,1408]{2,1,0:T(2,128)}), f32[32,2,1408]{2,1,0:T(2,128)S(1)}, u32[]{:S(2)}, u32[]{:S(2)}) %all-to-all-start.2) | async-done | bytes 360480 | tf_op jit(solution)/shard_map/all_to_all | solution.py:510
  66.1 1.9 %actions.4 = (bf16[128,2560]{1,0:T(8,128)(2,1)}, f32[128,128]{1,0:T(8,128)}, f32[32,2,1280]{2,1,0:T(2,128)}, f32[2,1280]{1,0:T(2,128)}) custom-call(f32[2,128,2560]{2,1,0:T(8,128)S(1)} %get-tuple-element.40.refs_0_, s32[3,16,25]{2,1,0:T(8,128)S(1)} %bitcast.7, s32[1]{0:T(128)} %bitcast.2.refs_2_.refs_3_.tie_ref, f32[2,128,128]{2,1,0:T(8,128)} %rollout.6.refs_3_.refs_2_, ...), custom_call_target="tpu_custom_call" | custom-call | tf_op jit(solution)/shard_map/actions/pallas_call | solution.py:212
  68.0 3.8 %all-to-all-start.3 = ((f32[32,2,1280]{2,1,0:T(2,128)}), f32[32,2,1280]{2,1,0:T(2,128)S(1)}, u32[]{:S(2)}, u32[]{:S(2)}) async-start(f32[32,2,1280]{2,1,0:T(2,128)} %get-tuple-element.53), calls=%async_computation.3 | async-start | bytes 655360 | tf_op jit(solution)/shard_map/all_to_all | solution.py:499
  71.8 6.7 %rollout.7 = (f32[2,128,128]{2,1,0:T(8,128)}, f32[2,128,128]{2,1,0:T(8,128)}, f32[2,1280]{1,0:T(2,128)S(1)}) custom-call(bf16[128,2560]{1,0:T(8,128)(2,1)} %get-tuple-element.41.refs_0_, bf16[128,2560]{1,0:T(8,128)(2,1)} %get-tuple-element.48.refs_1_.refs_0_, f32[2,128,128]{2,1,0:T(8,128)} %rollout.6.refs_3_.refs_2_, f32[16,128]{1,0:T(8,128)S(1)} %copy-done.3, ...), custom_call_target="tpu_custom_call" | custom-call | flops 268435456 | bytes 1048576 | tf_op jit(solution)/shard_map/rollout/pallas_call | solution.py:422
  78.5 2.9 %all-to-all-done.3.parts_ref = f32[32,2,1280]{2,1,0:T(2,128)S(1)} async-done(((f32[32,2,1280]{2,1,0:T(2,128)}), f32[32,2,1280]{2,1,0:T(2,128)S(1)}, u32[]{:S(2)}, u32[]{:S(2)}) %all-to-all-start.3) | async-done | bytes 327712 | tf_op jit(solution)/shard_map/all_to_all | solution.py:499
  81.4 0.3 refit.4
  81.7 13.8 %all_to_all.46.peak_ref = f32[16,1,128]{2,1,0:T(1,128)S(1)} all-to-all(f32[16,1,128]{2,1,0:T(1,128)S(1)} %get-tuple-element.56), channel_id=1, replica_groups=mesh['env'=16,'cand'=32] {'env'}, dimensions={0} | all-to-all | bytes 16384 | tf_op jit(solution)/shard_map/all_to_all | solution.py:507
  95.5 0.8 to_all.4
  96.3 5.7 %all-to-all-start.5 = ((f32[32,2,1408]{2,1,0:T(2,128)}), f32[32,2,1408]{2,1,0:T(2,128)S(1)}, u32[]{:S(2)}, u32[]{:S(2)}) async-start(f32[32,2,1408]{2,1,0:T(2,128)} %get-tuple-element.59), calls=%async_computation.5 | async-start | bytes 720896 | tf_op jit(solution)/shard_map/all_to_all | solution.py:510
  102.0 5.6 %rollout.8 = (f32[1,8,16]{2,1,0:T(8,128)}, f32[2,128,128]{2,1,0:T(8,128)}) custom-call(bf16[128,2560]{1,0:T(8,128)(2,1)} %get-tuple-element.41.refs_0_, bf16[128,2560]{1,0:T(8,128)(2,1)} %get-tuple-element.48.refs_1_.refs_0_, f32[2,128,128]{2,1,0:T(8,128)} %get-tuple-element.50.refs_2_, f32[2,128,128]{2,1,0:T(8,128)} %get-tuple-element.51.refs_3_, ...), custom_call_target="tpu_custom_call" | custom-call | flops 268435456 | bytes 1048576 | tf_op jit(solution)/shard_map/rollout/pallas_call | solution.py:422
  107.7 4.2 %all-to-all-done.5.refs_4_ = f32[32,2,1408]{2,1,0:T(2,128)S(1)} async-done(((f32[32,2,1408]{2,1,0:T(2,128)}), f32[32,2,1408]{2,1,0:T(2,128)S(1)}, u32[]{:S(2)}, u32[]{:S(2)}) %all-to-all-start.5) | async-done | bytes 360480 | tf_op jit(solution)/shard_map/all_to_all | solution.py:510
  111.8 1.9 %actions.5 = (bf16[128,2560]{1,0:T(8,128)(2,1)}, f32[128,128]{1,0:T(8,128)}, f32[32,2,1280]{2,1,0:T(2,128)}, f32[2,1280]{1,0:T(2,128)}) custom-call(f32[2,128,2560]{2,1,0:T(8,128)S(1)} %get-tuple-element.40.refs_0_, s32[3,16,25]{2,1,0:T(8,128)S(1)} %bitcast.8, s32[1]{0:T(128)} %bitcast.2.refs_2_.refs_3_.tie_ref, ...), custom_call_target="tpu_custom_call" | custom-call | tf_op jit(solution)/shard_map/actions/pallas_call | solution.py:212
  113.8 3.8 %all-to-all-start.6 = ((f32[32,2,1280]{2,1,0:T(2,128)}), f32[32,2,1280]{2,1,0:T(2,128)S(1)}, u32[]{:S(2)}, u32[]{:S(2)}) async-start(f32[32,2,1280]{2,1,0:T(2,128)} %get-tuple-element.60), calls=%async_computation.6 | async-start | bytes 655360 | tf_op jit(solution)/shard_map/all_to_all | solution.py:499
  117.5 6.7 %rollout.9 = (f32[1,8,16]{2,1,0:T(8,128)}, f32[2,128,128]{2,1,0:T(8,128)}, f32[2,1280]{1,0:T(2,128)S(1)}) custom-call(bf16[128,2560]{1,0:T(8,128)(2,1)} %get-tuple-element.48.refs_1_.refs_0_, bf16[128,2560]{1,0:T(8,128)(2,1)} %get-tuple-element.61.refs_1_.refs_0_, f32[2,128,128]{2,1,0:T(8,128)} %get-tuple-element.62.refs_2_, ...), custom_call_target="tpu_custom_call" | custom-call | flops 268435456 | bytes 1048576 | tf_op jit(solution)/shard_map/rollout/pallas_call | solution.py:422
  124.2 2.9 %all-to-all-done.6.parts_ref = f32[32,2,1280]{2,1,0:T(2,128)S(1)} async-done(((f32[32,2,1280]{2,1,0:T(2,128)}), f32[32,2,1280]{2,1,0:T(2,128)S(1)}, u32[]{:S(2)}, u32[]{:S(2)}) %all-to-all-start.6) | async-done | bytes 327712 | tf_op jit(solution)/shard_map/all_to_all | solution.py:499
  127.2 0.9 refit.5
  128.0 3.5 %all-to-all-start.7 = ((f32[16,1,128]{2,1,0:T(1,128)}), f32[16,1,128]{2,1,0:T(1,128)S(1)}, u32[]{:S(2)}, u32[]{:S(2)}) async-start(f32[16,1,128]{2,1,0:T(1,128)} %get-tuple-element.67.refs_9_), calls=%async_computation.7 | async-start | bytes 16384 | tf_op jit(solution)/shard_map/all_to_all | solution.py:507
  131.5 3.6 %rollout.10.tie_ref.refs_1_ = f32[2,128,128]{2,1,0:T(8,128)} custom-call(bf16[128,2560]{1,0:T(8,128)(2,1)} %get-tuple-element.61.refs_1_.refs_0_, f32[2,128,128]{2,1,0:T(8,128)} %get-tuple-element.68.refs_1_, f32[16,128]{1,0:T(8,128)S(1)} %copy-done.3, f32[16,128]{1,0:T(8,128)S(1)} %copy-done.4, bf16[128,512]{1,0:T(8,128)(2,1)S(1)} %copy-done, ...), custom_call_target="tpu_custom_call" | custom-call | flops 268435456 | bytes 1048576 | tf_op jit(solution)/shard_map/rollout/pallas_call | solution.py:422
  135.1 7.6 %all-to-all-done.7.peak_ref = f32[16,1,128]{2,1,0:T(1,128)S(1)} async-done(((f32[16,1,128]{2,1,0:T(1,128)}), f32[16,1,128]{2,1,0:T(1,128)S(1)}, u32[]{:S(2)}, u32[]{:S(2)}) %all-to-all-start.7) | async-done | bytes 8224 | tf_op jit(solution)/shard_map/all_to_all | solution.py:507
  142.7 0.8 to_all.5
  143.5 5.7 %all-to-all-start.8 = ((f32[32,2,1408]{2,1,0:T(2,128)}), f32[32,2,1408]{2,1,0:T(2,128)S(1)}, u32[]{:S(2)}, u32[]{:S(2)}) async-start(f32[32,2,1408]{2,1,0:T(2,128)} %get-tuple-element.69), calls=%async_computation.8 | async-start | bytes 720896 | tf_op jit(solution)/shard_map/all_to_all | solution.py:510
  149.2 7.6 %rollout.11 = f32[3,8,16]{2,1,0:T(8,128)} custom-call(bf16[128,2560]{1,0:T(8,128)(2,1)} %get-tuple-element.61.refs_1_.refs_0_, f32[2,128,128]{2,1,0:T(8,128)} %rollout.10.tie_ref.refs_1_, f32[128,128]{1,0:T(8,128)} %get-tuple-element.72.refs_2_, f32[16,128]{1,0:T(8,128)S(1)} %copy-done.3, f32[16,128]{1,0:T(8,128)S(1)} %copy-done.4, ...), custom_call_target="tpu_custom_call" | custom-call | flops 268435456 | bytes 1048576 | tf_op jit(solution)/shard_map/rollout/pallas_call | solution.py:422
  156.8 2.2 %all-to-all-done.8.state_ref = f32[32,2,1408]{2,1,0:T(2,128)S(1)} async-done(((f32[32,2,1408]{2,1,0:T(2,128)}), f32[32,2,1408]{2,1,0:T(2,128)S(1)}, u32[]{:S(2)}, u32[]{:S(2)}) %all-to-all-start.8) | async-done | bytes 360480 | tf_op jit(solution)/shard_map/all_to_all | solution.py:510
  159.0 0.8 finished.1
  (6 shorter events, 0.0 us)
Async XLA Ops:
  0.6 3.2 %copy-start.5 = (s32[16,3,25]{2,0,1:T(8,128)S(1)}, s32[16,3,25]{2,0,1:T(8,128)}, u32[]{:S(2)}) copy-start(s32[16,3,25]{2,0,1:T(8,128)} %param.21) | copy-start | bytes 14404
  0.6 3.2 %copy-start.7 = (f32[16,2560]{1,0:T(8,128)S(1)}, f32[16,2560]{1,0:T(8,128)}, u32[]{:S(2)}) copy-start(f32[16,2560]{1,0:T(8,128)} %refs_5_.7) | copy-start | bytes 491524
  0.7 3.2 %copy-start.6 = (f32[16,2560]{1,0:T(8,128)S(1)}, f32[16,2560]{1,0:T(8,128)}, u32[]{:S(2)}) copy-start(f32[16,2560]{1,0:T(8,128)} %refs_4_.6) | copy-start | bytes 491524
  5.6 50.6 %copy-start = (bf16[128,512]{1,0:T(8,128)(2,1)S(1)}, bf16[128,512]{1,0:T(8,128)(2,1)}, u32[]{:S(2)}) copy-start(bf16[128,512]{1,0:T(8,128)(2,1)} %refs_5_.13) | copy-start | bytes 393220
  5.6 50.6 %copy-start.1 = (bf16[512,128]{1,0:T(8,128)(2,1)S(1)}, bf16[512,128]{1,0:T(8,128)(2,1)}, u32[]{:S(2)}) copy-start(bf16[512,128]{1,0:T(8,128)(2,1)} %refs_7_.7) | copy-start | bytes 393220
  5.6 50.6 %copy-start.2 = (bf16[64,512]{1,0:T(8,128)(2,1)S(1)}, bf16[64,512]{1,0:T(8,128)(2,1)}, u32[]{:S(2)}) copy-start(bf16[64,512]{1,0:T(8,128)(2,1)} %refs_6_.9) | copy-start | bytes 196612
  5.6 50.6 %copy-start.3 = (f32[16,128]{1,0:T(8,128)S(1)}, f32[16,128]{1,0:T(8,128)}, u32[]{:S(2)}) copy-start(f32[16,128]{1,0:T(8,128)} %refs_3_.7) | copy-start | bytes 24580
  5.6 50.6 %copy-start.4 = (f32[16,128]{1,0:T(8,128)S(1)}, f32[16,128]{1,0:T(8,128)}, u32[]{:S(2)}) copy-start(f32[16,128]{1,0:T(8,128)} %refs_4_.11) | copy-start | bytes 24580
  5.6 50.6 %copy-start.8 = (f32[512]{0:T(512)S(1)}, f32[512]{0:T(512)}, u32[]{:S(2)}) copy-start(f32[512]{0:T(512)} %param.19) | copy-start | bytes 6148
  5.6 50.6 %copy-start.9 = (f32[128]{0:T(128)S(1)}, f32[128]{0:T(128)}, u32[]{:S(2)}) copy-start(f32[128]{0:T(128)} %param.20) | copy-start | bytes 1540
  5.6 20.1 %all-to-all-start = ((f32[32,2,1280]{2,1,0:T(2,128)}), f32[32,2,1280]{2,1,0:T(2,128)S(1)}, u32[]{:S(2)}, u32[]{:S(2)}) async-start(f32[32,2,1280]{2,1,0:T(2,128)} %get-tuple-element.42), calls=%async_computation | async-start | bytes 655360 | tf_op jit(solution)/shard_map/all_to_all | solution.py:499
  51.0 15.1 %all-to-all-start.2 = ((f32[32,2,1408]{2,1,0:T(2,128)}), f32[32,2,1408]{2,1,0:T(2,128)S(1)}, u32[]{:S(2)}, u32[]{:S(2)}) async-start(f32[32,2,1408]{2,1,0:T(2,128)} %get-tuple-element.47), calls=%async_computation.2 | async-start | bytes 720896 | tf_op jit(solution)/shard_map/all_to_all | solution.py:510
  68.0 13.4 %all-to-all-start.3 = ((f32[32,2,1280]{2,1,0:T(2,128)}), f32[32,2,1280]{2,1,0:T(2,128)S(1)}, u32[]{:S(2)}, u32[]{:S(2)}) async-start(f32[32,2,1280]{2,1,0:T(2,128)} %get-tuple-element.53), calls=%async_computation.3 | async-start | bytes 655360 | tf_op jit(solution)/shard_map/all_to_all | solution.py:499
  96.3 15.5 %all-to-all-start.5 = ((f32[32,2,1408]{2,1,0:T(2,128)}), f32[32,2,1408]{2,1,0:T(2,128)S(1)}, u32[]{:S(2)}, u32[]{:S(2)}) async-start(f32[32,2,1408]{2,1,0:T(2,128)} %get-tuple-element.59), calls=%async_computation.5 | async-start | bytes 720896 | tf_op jit(solution)/shard_map/all_to_all | solution.py:510
  113.8 13.4 %all-to-all-start.6 = ((f32[32,2,1280]{2,1,0:T(2,128)}), f32[32,2,1280]{2,1,0:T(2,128)S(1)}, u32[]{:S(2)}, u32[]{:S(2)}) async-start(f32[32,2,1280]{2,1,0:T(2,128)} %get-tuple-element.60), calls=%async_computation.6 | async-start | bytes 655360 | tf_op jit(solution)/shard_map/all_to_all | solution.py:499
  128.0 14.6 %all-to-all-start.7 = ((f32[16,1,128]{2,1,0:T(1,128)}), f32[16,1,128]{2,1,0:T(1,128)S(1)}, u32[]{:S(2)}, u32[]{:S(2)}) async-start(f32[16,1,128]{2,1,0:T(1,128)} %get-tuple-element.67.refs_9_), calls=%async_computation.7 | async-start | bytes 16384 | tf_op jit(solution)/shard_map/all_to_all | solution.py:507
  143.5 15.5 %all-to-all-start.8 = ((f32[32,2,1408]{2,1,0:T(2,128)}), f32[32,2,1408]{2,1,0:T(2,128)S(1)}, u32[]{:S(2)}, u32[]{:S(2)}) async-start(f32[32,2,1408]{2,1,0:T(2,128)} %get-tuple-element.69), calls=%async_computation.8 | async-start | bytes 720896 | tf_op jit(solution)/shard_map/all_to_all | solution.py:510

commit v8 on v7

--- a/solution.py
+++ b/solution.py
@@ -500,18 +500,18 @@
         if it == 0:
             noise, own = noise_of(white, 1, iters - 1, own, act_dim, horizon)
         elif it == 1:
-            own = play([(0, 14, 28), (1, 0, 14)], own, keep=True)
+            own = play([(0, 16, 28), (1, 0, 12)], own, keep=True)
         else:
-            own = play([(1, 26, horizon), (2, 0, 14)], own, keep=True)
+            own = play([(1, 24, horizon), (2, 0, 16)], own, keep=True)
         piece, peak = refit(parts, own, elites, groups)
         peaks = lax.all_to_all(peak, "env", 0, 0, tiled=True)
-        tie = mine if it < iters - 1 else play([(2, 14, 20)], peak)
+        tie = mine if it < iters - 1 else play([(2, 16, 20)], peak)
         spread, token = to_all(piece, peaks, tie, lines)
         state = (mix(spread),)
         if it == 0:
-            tie = play([(0, 0, 14)], token)
+            tie = play([(0, 0, 16)], token)
         elif it == 1:
-            tie = play([(0, 28, horizon), (1, 14, 26)], token)
+            tie = play([(0, 28, horizon), (1, 12, 24)], token)
         else:
             tie = play([(2, 20, horizon)], token, (costs[0], costs[1]))
     mean, std = finished(state[0], envs, width, envs_total)

time: 161 us -> 160 us (level)
  transfers between devices with their start and end apart: 7 -> 7, of which waited for: 7 -> 7; matrix products, arithmetic and copies ran while one was open for 0% -> 0% of each run, Pallas kernels for 26% -> 25%
where the time goes in v8:
time: 160 us; the launch traced here: 159 us
  Pallas kernels  53.1 us (33%)
  blocking collectives  38 us (24%)
  starting transfers between devices  37.7 us (24%)
  waiting for transfers between devices  29.7 us (19%)
    all_to_all x2, blocking collectives, shards(): peaks = lax.all_to_all(peak, 'env', 0, 0, tiled=True)  38 us
    pallas_call x6, Pallas kernels, rollout(): pl.pallas_call(functools.partial(rollout_body, spans=spans, act_dim=act_d...  34.8 us
    all_to_all x3, starting transfers between devices, shards(): parts = mix(sums)  18.3 us
    all_to_all x3, starting transfers between devices, shards(): state = (mix(spread),)  15.9 us
    all_to_all x3, waiting for transfers between devices, shards(): parts = mix(sums)  11.4 us
    all_to_all x3, waiting for transfers between devices, shards(): state = (mix(spread),)  9.99 us
    all_to_all x1, waiting for transfers between devices, shards(): peaks = lax.all_to_all(peak, 'env', 0, 0, tiled=True)  8.32 us
    pallas_call x2, Pallas kernels, noise_of(): pl.pallas_call(functools.partial(noise_body, act_dim=act_dim, first=first...  8.1 us
  transfers between devices with their start and end apart: 7, of which 7 were waited for; matrix products, arithmetic and copies ran while one was open for 0% of the time, Pallas kernels for 25%

profile of v8, /device:TPU:1, one launch (start us, length us, event | category | flops | bytes accessed | tf_op | source)
XLA Modules:
  0.0 159.5 jit_solution(7952910660626798561)
XLA Ops:
  0.7 3.1 %noise.2.refs_0_ = f32[1,128,2560]{2,1,0:T(8,128)S(1)} custom-call(bf16[3,128,4096]{2,1,0:T(8,128)(2,1)} %bitcast.21), custom_call_target="tpu_custom_call" | custom-call | flops 268435456 | bytes 1048576 | tf_op jit(solution)/shard_map/noise/pallas_call | solution.py:114
  3.8 1.7 %actions.3 = (bf16[128,2560]{1,0:T(8,128)(2,1)}, f32[128,128]{1,0:T(8,128)}, f32[32,2,1280]{2,1,0:T(2,128)}, f32[2,1280]{1,0:T(2,128)}) custom-call(f32[1,128,2560]{2,1,0:T(8,128)S(1)} %noise.2.refs_0_, s32[3,16,25]{2,1,0:T(8,128)S(1)} %bitcast.6, s32[1]{0:T(128)} %bitcast.2.refs_2_.refs_3_.tie_ref, s32[1]{0:T(128)} %bitcast.2.refs_2_.refs_3_.tie_ref, ...), custom_call_target="tpu_custom_call" | custom-call | tf_op jit(solution)/shard_map/actions/pallas_call | solution.py:212
  5.6 0.0 copy-start
  5.6 0.0 copy-start.1
  5.6 0.0 copy-start.2
  5.6 0.0 copy-start.3
  5.6 0.0 copy-start.4
  5.6 0.0 copy-start.8
  5.6 0.0 copy-start.9
  5.6 10.5 %all-to-all-start = ((f32[32,2,1280]{2,1,0:T(2,128)}), f32[32,2,1280]{2,1,0:T(2,128)S(1)}, u32[]{:S(2)}, u32[]{:S(2)}) async-start(f32[32,2,1280]{2,1,0:T(2,128)} %get-tuple-element.42), calls=%async_computation | async-start | bytes 655360 | tf_op jit(solution)/shard_map/all_to_all | solution.py:499
  16.2 5.0 %noise.3 = (f32[2,128,2560]{2,1,0:T(8,128)S(1)}, f32[2,1280]{1,0:T(2,128)S(1)}) custom-call(bf16[3,128,4096]{2,1,0:T(8,128)(2,1)} %bitcast.22, f32[2,1280]{1,0:T(2,128)} %get-tuple-element.39.refs_1_), custom_call_target="tpu_custom_call" | custom-call | flops 268435456 | bytes 1048576 | tf_op jit(solution)/shard_map/noise/pallas_call | solution.py:114
  21.1 4.7 %all-to-all-done.parts_ref = f32[32,2,1280]{2,1,0:T(2,128)S(1)} async-done(((f32[32,2,1280]{2,1,0:T(2,128)}), f32[32,2,1280]{2,1,0:T(2,128)S(1)}, u32[]{:S(2)}, u32[]{:S(2)}) %all-to-all-start) | async-done | bytes 327712 | tf_op jit(solution)/shard_map/all_to_all | solution.py:499
  25.8 0.3 refit.3
  26.1 24.2 %all_to_all.45.peak_ref = f32[16,1,128]{2,1,0:T(1,128)S(1)} all-to-all(f32[16,1,128]{2,1,0:T(1,128)S(1)} %get-tuple-element.45), channel_id=1, replica_groups=mesh['env'=16,'cand'=32] {'env'}, dimensions={0} | all-to-all | bytes 16384 | tf_op jit(solution)/shard_map/all_to_all | solution.py:507
  50.2 0.8 to_all.3
  51.0 5.1 %all-to-all-start.2 = ((f32[32,2,1408]{2,1,0:T(2,128)}), f32[32,2,1408]{2,1,0:T(2,128)S(1)}, u32[]{:S(2)}, u32[]{:S(2)}) async-start(f32[32,2,1408]{2,1,0:T(2,128)} %get-tuple-element.47), calls=%async_computation.2 | async-start | bytes 720896 | tf_op jit(solution)/shard_map/all_to_all | solution.py:510
  56.1 0.0 copy-done
  56.1 0.0 copy-done.1
  56.2 0.0 copy-done.2
  56.2 0.0 copy-done.3
  56.2 0.0 copy-done.4
  56.2 0.0 copy-done.8
  56.2 0.0 copy-done.9
  56.2 6.4 %rollout.6.refs_3_.refs_2_ = f32[2,128,128]{2,1,0:T(8,128)} custom-call(bf16[128,2560]{1,0:T(8,128)(2,1)} %get-tuple-element.41.refs_0_, f32[16,128]{1,0:T(8,128)S(1)} %copy-done.3, f32[16,128]{1,0:T(8,128)S(1)} %copy-done.4, bf16[128,512]{1,0:T(8,128)(2,1)S(1)} %copy-done, bf16[64,512]{1,0:T(8,128)(2,1)S(1)} %copy-done.2, bf16[512,128]{1,0:T(8,128)(2,1)S(1)} %copy-done.1, ...), custom_call_target="tpu_custom_call" | custom-call | flops 268435456 | bytes 1048576 | tf_op jit(solution)/shard_map/rollout/pallas_call | solution.py:422
  62.6 3.5 %all-to-all-done.2.refs_4_ = f32[32,2,1408]{2,1,0:T(2,128)S(1)} async-done(((f32[32,2,1408]{2,1,0:T(2,128)}), f32[32,2,1408]{2,1,0:T(2,128)S(1)}, u32[]{:S(2)}, u32[]{:S(2)}) %all-to-all-start.2) | async-done | bytes 360480 | tf_op jit(solution)/shard_map/all_to_all | solution.py:510
  66.1 1.9 %actions.4 = (bf16[128,2560]{1,0:T(8,128)(2,1)}, f32[128,128]{1,0:T(8,128)}, f32[32,2,1280]{2,1,0:T(2,128)}, f32[2,1280]{1,0:T(2,128)}) custom-call(f32[2,128,2560]{2,1,0:T(8,128)S(1)} %get-tuple-element.40.refs_0_, s32[3,16,25]{2,1,0:T(8,128)S(1)} %bitcast.7, s32[1]{0:T(128)} %bitcast.2.refs_2_.refs_3_.tie_ref, f32[2,128,128]{2,1,0:T(8,128)} %rollout.6.refs_3_.refs_2_, ...), custom_call_target="tpu_custom_call" | custom-call | tf_op jit(solution)/shard_map/actions/pallas_call | solution.py:212
  68.0 4.0 %all-to-all-start.3 = ((f32[32,2,1280]{2,1,0:T(2,128)}), f32[32,2,1280]{2,1,0:T(2,128)S(1)}, u32[]{:S(2)}, u32[]{:S(2)}) async-start(f32[32,2,1280]{2,1,0:T(2,128)} %get-tuple-element.53), calls=%async_computation.3 | async-start | bytes 655360 | tf_op jit(solution)/shard_map/all_to_all | solution.py:499
  72.0 5.6 %rollout.7 = (f32[2,128,128]{2,1,0:T(8,128)}, f32[2,128,128]{2,1,0:T(8,128)}, f32[2,1280]{1,0:T(2,128)S(1)}) custom-call(bf16[128,2560]{1,0:T(8,128)(2,1)} %get-tuple-element.41.refs_0_, bf16[128,2560]{1,0:T(8,128)(2,1)} %get-tuple-element.48.refs_1_.refs_0_, f32[2,128,128]{2,1,0:T(8,128)} %rollout.6.refs_3_.refs_2_, f32[16,128]{1,0:T(8,128)S(1)} %copy-done.3, ...), custom_call_target="tpu_custom_call" | custom-call | flops 268435456 | bytes 1048576 | tf_op jit(solution)/shard_map/rollout/pallas_call | solution.py:422
  77.6 3.9 %all-to-all-done.3.parts_ref = f32[32,2,1280]{2,1,0:T(2,128)S(1)} async-done(((f32[32,2,1280]{2,1,0:T(2,128)}), f32[32,2,1280]{2,1,0:T(2,128)S(1)}, u32[]{:S(2)}, u32[]{:S(2)}) %all-to-all-start.3) | async-done | bytes 327712 | tf_op jit(solution)/shard_map/all_to_all | solution.py:499
  81.5 0.3 refit.4
  81.8 13.8 %all_to_all.46.peak_ref = f32[16,1,128]{2,1,0:T(1,128)S(1)} all-to-all(f32[16,1,128]{2,1,0:T(1,128)S(1)} %get-tuple-element.56), channel_id=1, replica_groups=mesh['env'=16,'cand'=32] {'env'}, dimensions={0} | all-to-all | bytes 16384 | tf_op jit(solution)/shard_map/all_to_all | solution.py:507
  95.6 0.8 to_all.4
  96.4 5.0 %all-to-all-start.5 = ((f32[32,2,1408]{2,1,0:T(2,128)}), f32[32,2,1408]{2,1,0:T(2,128)S(1)}, u32[]{:S(2)}, u32[]{:S(2)}) async-start(f32[32,2,1408]{2,1,0:T(2,128)} %get-tuple-element.59), calls=%async_computation.5 | async-start | bytes 720896 | tf_op jit(solution)/shard_map/all_to_all | solution.py:510
  101.5 5.6 %rollout.8 = (f32[1,8,16]{2,1,0:T(8,128)}, f32[2,128,128]{2,1,0:T(8,128)}) custom-call(bf16[128,2560]{1,0:T(8,128)(2,1)} %get-tuple-element.41.refs_0_, bf16[128,2560]{1,0:T(8,128)(2,1)} %get-tuple-element.48.refs_1_.refs_0_, f32[2,128,128]{2,1,0:T(8,128)} %get-tuple-element.50.refs_2_, f32[2,128,128]{2,1,0:T(8,128)} %get-tuple-element.51.refs_3_, ...), custom_call_target="tpu_custom_call" | custom-call | flops 268435456 | bytes 1048576 | tf_op jit(solution)/shard_map/rollout/pallas_call | solution.py:422
  107.1 4.3 %all-to-all-done.5.refs_4_ = f32[32,2,1408]{2,1,0:T(2,128)S(1)} async-done(((f32[32,2,1408]{2,1,0:T(2,128)}), f32[32,2,1408]{2,1,0:T(2,128)S(1)}, u32[]{:S(2)}, u32[]{:S(2)}) %all-to-all-start.5) | async-done | bytes 360480 | tf_op jit(solution)/shard_map/all_to_all | solution.py:510
  111.4 1.9 %actions.5 = (bf16[128,2560]{1,0:T(8,128)(2,1)}, f32[128,128]{1,0:T(8,128)}, f32[32,2,1280]{2,1,0:T(2,128)}, f32[2,1280]{1,0:T(2,128)}) custom-call(f32[2,128,2560]{2,1,0:T(8,128)S(1)} %get-tuple-element.40.refs_0_, s32[3,16,25]{2,1,0:T(8,128)S(1)} %bitcast.8, s32[1]{0:T(128)} %bitcast.2.refs_2_.refs_3_.tie_ref, ...), custom_call_target="tpu_custom_call" | custom-call | tf_op jit(solution)/shard_map/actions/pallas_call | solution.py:212
  113.3 3.8 %all-to-all-start.6 = ((f32[32,2,1280]{2,1,0:T(2,128)}), f32[32,2,1280]{2,1,0:T(2,128)S(1)}, u32[]{:S(2)}, u32[]{:S(2)}) async-start(f32[32,2,1280]{2,1,0:T(2,128)} %get-tuple-element.60), calls=%async_computation.6 | async-start | bytes 655360 | tf_op jit(solution)/shard_map/all_to_all | solution.py:499
  117.1 6.8 %rollout.9 = (f32[1,8,16]{2,1,0:T(8,128)}, f32[2,128,128]{2,1,0:T(8,128)}, f32[2,1280]{1,0:T(2,128)S(1)}) custom-call(bf16[128,2560]{1,0:T(8,128)(2,1)} %get-tuple-element.48.refs_1_.refs_0_, bf16[128,2560]{1,0:T(8,128)(2,1)} %get-tuple-element.61.refs_1_.refs_0_, f32[2,128,128]{2,1,0:T(8,128)} %get-tuple-element.62.refs_2_, ...), custom_call_target="tpu_custom_call" | custom-call | flops 268435456 | bytes 1048576 | tf_op jit(solution)/shard_map/rollout/pallas_call | solution.py:422
  123.9 2.8 %all-to-all-done.6.parts_ref = f32[32,2,1280]{2,1,0:T(2,128)S(1)} async-done(((f32[32,2,1280]{2,1,0:T(2,128)}), f32[32,2,1280]{2,1,0:T(2,128)S(1)}, u32[]{:S(2)}, u32[]{:S(2)}) %all-to-all-start.6) | async-done | bytes 327712 | tf_op jit(solution)/shard_map/all_to_all | solution.py:499
  126.7 0.9 refit.5
  127.6 3.5 %all-to-all-start.7 = ((f32[16,1,128]{2,1,0:T(1,128)}), f32[16,1,128]{2,1,0:T(1,128)S(1)}, u32[]{:S(2)}, u32[]{:S(2)}) async-start(f32[16,1,128]{2,1,0:T(1,128)} %get-tuple-element.67.refs_9_), calls=%async_computation.7 | async-start | bytes 16384 | tf_op jit(solution)/shard_map/all_to_all | solution.py:507
  131.1 2.8 %rollout.10.tie_ref.refs_1_ = f32[2,128,128]{2,1,0:T(8,128)} custom-call(bf16[128,2560]{1,0:T(8,128)(2,1)} %get-tuple-element.61.refs_1_.refs_0_, f32[2,128,128]{2,1,0:T(8,128)} %get-tuple-element.68.refs_1_, f32[16,128]{1,0:T(8,128)S(1)} %copy-done.3, f32[16,128]{1,0:T(8,128)S(1)} %copy-done.4, bf16[128,512]{1,0:T(8,128)(2,1)S(1)} %copy-done, ...), custom_call_target="tpu_custom_call" | custom-call | flops 268435456 | bytes 1048576 | tf_op jit(solution)/shard_map/rollout/pallas_call | solution.py:422
  133.9 8.3 %all-to-all-done.7.peak_ref = f32[16,1,128]{2,1,0:T(1,128)S(1)} async-done(((f32[16,1,128]{2,1,0:T(1,128)}), f32[16,1,128]{2,1,0:T(1,128)S(1)}, u32[]{:S(2)}, u32[]{:S(2)}) %all-to-all-start.7) | async-done | bytes 8224 | tf_op jit(solution)/shard_map/all_to_all | solution.py:507
  142.3 0.8 to_all.5
  143.0 5.8 %all-to-all-start.8 = ((f32[32,2,1408]{2,1,0:T(2,128)}), f32[32,2,1408]{2,1,0:T(2,128)S(1)}, u32[]{:S(2)}, u32[]{:S(2)}) async-start(f32[32,2,1408]{2,1,0:T(2,128)} %get-tuple-element.69), calls=%async_computation.8 | async-start | bytes 720896 | tf_op jit(solution)/shard_map/all_to_all | solution.py:510
  148.8 7.6 %rollout.11 = f32[3,8,16]{2,1,0:T(8,128)} custom-call(bf16[128,2560]{1,0:T(8,128)(2,1)} %get-tuple-element.61.refs_1_.refs_0_, f32[2,128,128]{2,1,0:T(8,128)} %rollout.10.tie_ref.refs_1_, f32[128,128]{1,0:T(8,128)} %get-tuple-element.72.refs_2_, f32[16,128]{1,0:T(8,128)S(1)} %copy-done.3, f32[16,128]{1,0:T(8,128)S(1)} %copy-done.4, ...), custom_call_target="tpu_custom_call" | custom-call | flops 268435456 | bytes 1048576 | tf_op jit(solution)/shard_map/rollout/pallas_call | solution.py:422
  156.4 2.2 %all-to-all-done.8.state_ref = f32[32,2,1408]{2,1,0:T(2,128)S(1)} async-done(((f32[32,2,1408]{2,1,0:T(2,128)}), f32[32,2,1408]{2,1,0:T(2,128)S(1)}, u32[]{:S(2)}, u32[]{:S(2)}) %all-to-all-start.8) | async-done | bytes 360480 | tf_op jit(solution)/shard_map/all_to_all | solution.py:510
  158.6 0.8 finished.1
  (6 shorter events, 0.0 us)
Async XLA Ops:
  0.6 3.2 %copy-start.5 = (s32[16,3,25]{2,0,1:T(8,128)S(1)}, s32[16,3,25]{2,0,1:T(8,128)}, u32[]{:S(2)}) copy-start(s32[16,3,25]{2,0,1:T(8,128)} %param.21) | copy-start | bytes 14404
  0.6 3.2 %copy-start.7 = (f32[16,2560]{1,0:T(8,128)S(1)}, f32[16,2560]{1,0:T(8,128)}, u32[]{:S(2)}) copy-start(f32[16,2560]{1,0:T(8,128)} %refs_5_.7) | copy-start | bytes 491524
  0.7 3.2 %copy-start.6 = (f32[16,2560]{1,0:T(8,128)S(1)}, f32[16,2560]{1,0:T(8,128)}, u32[]{:S(2)}) copy-start(f32[16,2560]{1,0:T(8,128)} %refs_4_.6) | copy-start | bytes 491524
  5.6 50.6 %copy-start = (bf16[128,512]{1,0:T(8,128)(2,1)S(1)}, bf16[128,512]{1,0:T(8,128)(2,1)}, u32[]{:S(2)}) copy-start(bf16[128,512]{1,0:T(8,128)(2,1)} %refs_5_.13) | copy-start | bytes 393220
  5.6 50.6 %copy-start.1 = (bf16[512,128]{1,0:T(8,128)(2,1)S(1)}, bf16[512,128]{1,0:T(8,128)(2,1)}, u32[]{:S(2)}) copy-start(bf16[512,128]{1,0:T(8,128)(2,1)} %refs_7_.7) | copy-start | bytes 393220
  5.6 50.6 %copy-start.2 = (bf16[64,512]{1,0:T(8,128)(2,1)S(1)}, bf16[64,512]{1,0:T(8,128)(2,1)}, u32[]{:S(2)}) copy-start(bf16[64,512]{1,0:T(8,128)(2,1)} %refs_6_.9) | copy-start | bytes 196612
  5.6 50.6 %copy-start.3 = (f32[16,128]{1,0:T(8,128)S(1)}, f32[16,128]{1,0:T(8,128)}, u32[]{:S(2)}) copy-start(f32[16,128]{1,0:T(8,128)} %refs_3_.7) | copy-start | bytes 24580
  5.6 50.6 %copy-start.4 = (f32[16,128]{1,0:T(8,128)S(1)}, f32[16,128]{1,0:T(8,128)}, u32[]{:S(2)}) copy-start(f32[16,128]{1,0:T(8,128)} %refs_4_.11) | copy-start | bytes 24580
  5.6 50.6 %copy-start.8 = (f32[512]{0:T(512)S(1)}, f32[512]{0:T(512)}, u32[]{:S(2)}) copy-start(f32[512]{0:T(512)} %param.19) | copy-start | bytes 6148
  5.6 50.6 %copy-start.9 = (f32[128]{0:T(128)S(1)}, f32[128]{0:T(128)}, u32[]{:S(2)}) copy-start(f32[128]{0:T(128)} %param.20) | copy-start | bytes 1540
  5.6 20.1 %all-to-all-start = ((f32[32,2,1280]{2,1,0:T(2,128)}), f32[32,2,1280]{2,1,0:T(2,128)S(1)}, u32[]{:S(2)}, u32[]{:S(2)}) async-start(f32[32,2,1280]{2,1,0:T(2,128)} %get-tuple-element.42), calls=%async_computation | async-start | bytes 655360 | tf_op jit(solution)/shard_map/all_to_all | solution.py:499
  51.0 15.1 %all-to-all-start.2 = ((f32[32,2,1408]{2,1,0:T(2,128)}), f32[32,2,1408]{2,1,0:T(2,128)S(1)}, u32[]{:S(2)}, u32[]{:S(2)}) async-start(f32[32,2,1408]{2,1,0:T(2,128)} %get-tuple-element.47), calls=%async_computation.2 | async-start | bytes 720896 | tf_op jit(solution)/shard_map/all_to_all | solution.py:510
  68.0 13.5 %all-to-all-start.3 = ((f32[32,2,1280]{2,1,0:T(2,128)}), f32[32,2,1280]{2,1,0:T(2,128)S(1)}, u32[]{:S(2)}, u32[]{:S(2)}) async-start(f32[32,2,1280]{2,1,0:T(2,128)} %get-tuple-element.53), calls=%async_computation.3 | async-start | bytes 655360 | tf_op jit(solution)/shard_map/all_to_all | solution.py:499
  96.4 15.0 %all-to-all-start.5 = ((f32[32,2,1408]{2,1,0:T(2,128)}), f32[32,2,1408]{2,1,0:T(2,128)S(1)}, u32[]{:S(2)}, u32[]{:S(2)}) async-start(f32[32,2,1408]{2,1,0:T(2,128)} %get-tuple-element.59), calls=%async_computation.5 | async-start | bytes 720896 | tf_op jit(solution)/shard_map/all_to_all | solution.py:510
  113.3 13.4 %all-to-all-start.6 = ((f32[32,2,1280]{2,1,0:T(2,128)}), f32[32,2,1280]{2,1,0:T(2,128)S(1)}, u32[]{:S(2)}, u32[]{:S(2)}) async-start(f32[32,2,1280]{2,1,0:T(2,128)} %get-tuple-element.60), calls=%async_computation.6 | async-start | bytes 655360 | tf_op jit(solution)/shard_map/all_to_all | solution.py:499
  127.6 14.6 %all-to-all-start.7 = ((f32[16,1,128]{2,1,0:T(1,128)}), f32[16,1,128]{2,1,0:T(1,128)S(1)}, u32[]{:S(2)}, u32[]{:S(2)}) async-start(f32[16,1,128]{2,1,0:T(1,128)} %get-tuple-element.67.refs_9_), calls=%async_computation.7 | async-start | bytes 16384 | tf_op jit(solution)/shard_map/all_to_all | solution.py:507
  143.0 15.6 %all-to-all-start.8 = ((f32[32,2,1408]{2,1,0:T(2,128)}), f32[32,2,1408]{2,1,0:T(2,128)S(1)}, u32[]{:S(2)}, u32[]{:S(2)}) async-start(f32[32,2,1408]{2,1,0:T(2,128)} %get-tuple-element.69), calls=%async_computation.8 | async-start | bytes 720896 | tf_op jit(solution)/shard_map/all_to_all | solution.py:510

commit v9 on v8

--- a/solution.py
+++ b/solution.py
@@ -129,7 +129,7 @@
 
 
 def stats_of(state_ref, envs, half, envs_total):
-    peaks = state_ref[:, 0, pl.ds(half, LANES)]
+    peaks = state_ref[:, 0, pl.ds(2 * half, LANES)]
     pair = jnp.max(peaks.reshape(envs, 2, LANES), axis=1)
     peak = jnp.max(pair, axis=(0, 1), keepdims=True)
     total = jnp.sum(jnp.sum(pair, axis=0, keepdims=True), axis=1, keepdims=True)
@@ -154,9 +154,8 @@
         own_ref[1:2, :] = std_ref[pl.ds(me // 2, 1), lanes]
     else:
         floor, gain = stats_of(state_ref, envs, half, envs_total)
-        own = state_ref[me, :, pl.ds(0, half)]
-        own_ref[0:1, :] = own[0:1]
-        own_ref[1:2, :] = jnp.maximum(own[1:2], floor) * gain
+        own_ref[0:1, :] = state_ref[me, 0:1, pl.ds(0, half)]
+        own_ref[1:2, :] = jnp.maximum(state_ref[me, 0:1, pl.ds(half, half)], floor) * gain
     per = 4
 
     def send(part):
@@ -190,7 +189,8 @@
                     spread = std_ref[pl.ds(env, 1), whole]
                 else:
                     center = state_ref[line, 0:1, lanes]
-                    spread = jnp.maximum(state_ref[line, 1:2, lanes], floor) * gain
+                    mixed = state_ref[line, 0:1, pl.ds(half + step * LANES, LANES)]
+                    spread = jnp.maximum(mixed, floor) * gain
                 action = jnp.clip(center + spread * noise_ref[0, at, whole], -1.0, 1.0)
                 acts_ref[at, whole] = action.astype(jnp.bfloat16)
                 both = action * action
@@ -264,10 +264,11 @@
     tail = jnp.zeros((1, LANES), jnp.float32)
     for group in range(peak_ref.shape[0]):
         tail = jnp.where(lane == group, peak_ref[group], tail)
-    main = jnp.broadcast_to(slice_ref[...][None], (lines, 2, half))
-    out_ref[:, :, pl.ds(0, half)] = main
+    for side in range(2):
+        main = jnp.broadcast_to(slice_ref[side : side + 1, :][None], (lines, 1, half))
+        out_ref[:, :, pl.ds(side * half, half)] = main
     token_ref[...] = jnp.broadcast_to(tail, token_ref.shape)
-    out_ref[:, :, pl.ds(half, LANES)] = jnp.broadcast_to(tail[None], (lines, 2, LANES))
+    out_ref[:, :, pl.ds(2 * half, LANES)] = jnp.broadcast_to(tail[None], (lines, 1, LANES))
 
 
 def to_all(piece, peaks, tie, lines):
@@ -276,8 +277,8 @@
         spread_body,
         grid=(1,),
         in_specs=[VMEM, VMEM, HBM],
-        out_specs=[whole((lines, 2, half + LANES)), whole((8, LANES))],
-        out_shape=[in_hbm((lines, 2, half + LANES)), in_hbm((8, LANES))],
+        out_specs=[whole((lines, 1, 2 * half + LANES)), whole((8, LANES))],
+        out_shape=[in_hbm((lines, 1, 2 * half + LANES)), in_hbm((8, LANES))],
         compiler_params=pltpu.CompilerParams(vmem_limit_bytes=4 << 20),
         name="to_all",
     )(piece, peaks, stay(tie))
@@ -293,7 +294,7 @@
             line = 2 * env + side
             mean_ref[pl.ds(env, 1), lanes] = state_ref[line, 0:1, pl.ds(0, half)]
             std_ref[pl.ds(env, 1), lanes] = (
-                jnp.maximum(state_ref[line, 1:2, pl.ds(0, half)], floor) * gain
+                jnp.maximum(state_ref[line, 0:1, pl.ds(half, half)], floor) * gain
             )
 
 

time: 160 us -> 160 us (level)
  no operation moved by 1% of the time
where the time goes in v9:
time: 160 us; the launch traced here: 159 us
  Pallas kernels  53.1 us (33%)
  blocking collectives  38 us (24%)
  starting transfers between devices  37.8 us (24%)
  waiting for transfers between devices  29.2 us (18%)
    all_to_all x2, blocking collectives, shards(): peaks = lax.all_to_all(peak, 'env', 0, 0, tiled=True)  38 us
    pallas_call x6, Pallas kernels, rollout(): pl.pallas_call(functools.partial(rollout_body, spans=spans, act_dim=act_d...  34.8 us
    all_to_all x3, starting transfers between devices, shards(): parts = mix(sums)  18.4 us
    all_to_all x3, starting transfers between devices, shards(): state = (mix(spread),)  15.9 us
    all_to_all x3, waiting for transfers between devices, shards(): parts = mix(sums)  11.4 us
    all_to_all x3, waiting for transfers between devices, shards(): state = (mix(spread),)  9.51 us
    all_to_all x1, waiting for transfers between devices, shards(): peaks = lax.all_to_all(peak, 'env', 0, 0, tiled=True)  8.31 us
    pallas_call x2, Pallas kernels, noise_of(): pl.pallas_call(functools.partial(noise_body, act_dim=act_dim, first=first...  8.1 us
  transfers between devices with their start and end apart: 7, of which 7 were waited for; matrix products, arithmetic and copies ran while one was open for 0% of the time, Pallas kernels for 25%

profile of v9, /device:TPU:1, one launch (start us, length us, event | category | flops | bytes accessed | tf_op | source)
XLA Modules:
  0.0 159.1 jit_solution(15095651997548613286)
XLA Ops:
  0.7 3.1 %noise.2.refs_0_ = f32[1,128,2560]{2,1,0:T(8,128)S(1)} custom-call(bf16[3,128,4096]{2,1,0:T(8,128)(2,1)} %bitcast.21), custom_call_target="tpu_custom_call" | custom-call | flops 268435456 | bytes 1048576 | tf_op jit(solution)/shard_map/noise/pallas_call | solution.py:114
  3.8 0.0 copy-done.5
  3.8 0.0 copy-done.7
  3.8 0.0 copy-done.6
  3.8 1.7 %actions.3 = (bf16[128,2560]{1,0:T(8,128)(2,1)}, f32[128,128]{1,0:T(8,128)}, f32[32,2,1280]{2,1,0:T(2,128)}, f32[2,1280]{1,0:T(2,128)}) custom-call(f32[1,128,2560]{2,1,0:T(8,128)S(1)} %noise.2.refs_0_, s32[3,16,25]{2,1,0:T(8,128)S(1)} %bitcast.6, s32[1]{0:T(128)} %bitcast.2.refs_2_.refs_3_.tie_ref, s32[1]{0:T(128)} %bitcast.2.refs_2_.refs_3_.tie_ref, ...), custom_call_target="tpu_custom_call" | custom-call | tf_op jit(solution)/shard_map/actions/pallas_call | solution.py:212
  5.6 0.0 copy-start
  5.6 0.0 copy-start.1
  5.6 0.0 copy-start.2
  5.6 0.0 copy-start.3
  5.6 0.0 copy-start.4
  5.6 0.0 copy-start.8
  5.6 0.0 copy-start.9
  5.6 10.5 %all-to-all-start = ((f32[32,2,1280]{2,1,0:T(2,128)}), f32[32,2,1280]{2,1,0:T(2,128)S(1)}, u32[]{:S(2)}, u32[]{:S(2)}) async-start(f32[32,2,1280]{2,1,0:T(2,128)} %get-tuple-element.42), calls=%async_computation | async-start | bytes 655360 | tf_op jit(solution)/shard_map/all_to_all | solution.py:500
  16.2 5.0 %noise.3 = (f32[2,128,2560]{2,1,0:T(8,128)S(1)}, f32[2,1280]{1,0:T(2,128)S(1)}) custom-call(bf16[3,128,4096]{2,1,0:T(8,128)(2,1)} %bitcast.22, f32[2,1280]{1,0:T(2,128)} %get-tuple-element.39.refs_1_), custom_call_target="tpu_custom_call" | custom-call | flops 268435456 | bytes 1048576 | tf_op jit(solution)/shard_map/noise/pallas_call | solution.py:114
  21.1 4.7 %all-to-all-done.parts_ref = f32[32,2,1280]{2,1,0:T(2,128)S(1)} async-done(((f32[32,2,1280]{2,1,0:T(2,128)}), f32[32,2,1280]{2,1,0:T(2,128)S(1)}, u32[]{:S(2)}, u32[]{:S(2)}) %all-to-all-start) | async-done | bytes 327712 | tf_op jit(solution)/shard_map/all_to_all | solution.py:500
  25.8 0.3 refit.3
  26.1 24.2 %all_to_all.45.peak_ref = f32[16,1,128]{2,1,0:T(1,128)S(1)} all-to-all(f32[16,1,128]{2,1,0:T(1,128)S(1)} %get-tuple-element.45), channel_id=1, replica_groups=mesh['env'=16,'cand'=32] {'env'}, dimensions={0} | all-to-all | bytes 16384 | tf_op jit(solution)/shard_map/all_to_all | solution.py:508
  50.2 0.8 to_all.3
  51.0 5.1 %all-to-all-start.2 = ((f32[32,1,2688]{2,1,0:T(1,128)}), f32[32,1,2688]{2,1,0:T(1,128)S(1)}, u32[]{:S(2)}, u32[]{:S(2)}) async-start(f32[32,1,2688]{2,1,0:T(1,128)} %get-tuple-element.47), calls=%async_computation.2 | async-start | bytes 688128 | tf_op jit(solution)/shard_map/all_to_all | solution.py:511
  56.1 0.0 copy-done
  56.1 0.0 copy-done.1
  56.1 0.0 copy-done.2
  56.2 0.0 copy-done.3
  56.2 6.4 %rollout.6.refs_3_.refs_2_ = f32[2,128,128]{2,1,0:T(8,128)} custom-call(bf16[128,2560]{1,0:T(8,128)(2,1)} %get-tuple-element.41.refs_0_, f32[16,128]{1,0:T(8,128)S(1)} %copy-done.3, f32[16,128]{1,0:T(8,128)S(1)} %copy-done.4, bf16[128,512]{1,0:T(8,128)(2,1)S(1)} %copy-done, bf16[64,512]{1,0:T(8,128)(2,1)S(1)} %copy-done.2, bf16[512,128]{1,0:T(8,128)(2,1)S(1)} %copy-done.1, ...), custom_call_target="tpu_custom_call" | custom-call | flops 268435456 | bytes 1048576 | tf_op jit(solution)/shard_map/rollout/pallas_call | solution.py:423
  62.6 3.3 %all-to-all-done.2.refs_4_ = f32[32,1,2688]{2,1,0:T(1,128)S(1)} async-done(((f32[32,1,2688]{2,1,0:T(1,128)}), f32[32,1,2688]{2,1,0:T(1,128)S(1)}, u32[]{:S(2)}, u32[]{:S(2)}) %all-to-all-start.2) | async-done | bytes 344096 | tf_op jit(solution)/shard_map/all_to_all | solution.py:511
  65.9 1.9 %actions.4 = (bf16[128,2560]{1,0:T(8,128)(2,1)}, f32[128,128]{1,0:T(8,128)}, f32[32,2,1280]{2,1,0:T(2,128)}, f32[2,1280]{1,0:T(2,128)}) custom-call(f32[2,128,2560]{2,1,0:T(8,128)S(1)} %get-tuple-element.40.refs_0_, s32[3,16,25]{2,1,0:T(8,128)S(1)} %bitcast.7, s32[1]{0:T(128)} %bitcast.2.refs_2_.refs_3_.tie_ref, f32[2,128,128]{2,1,0:T(8,128)} %rollout.6.refs_3_.refs_2_, ...), custom_call_target="tpu_custom_call" | custom-call | tf_op jit(solution)/shard_map/actions/pallas_call | solution.py:212
  67.8 4.2 %all-to-all-start.3 = ((f32[32,2,1280]{2,1,0:T(2,128)}), f32[32,2,1280]{2,1,0:T(2,128)S(1)}, u32[]{:S(2)}, u32[]{:S(2)}) async-start(f32[32,2,1280]{2,1,0:T(2,128)} %get-tuple-element.53), calls=%async_computation.3 | async-start | bytes 655360 | tf_op jit(solution)/shard_map/all_to_all | solution.py:500
  72.0 5.6 %rollout.7 = (f32[2,128,128]{2,1,0:T(8,128)}, f32[2,128,128]{2,1,0:T(8,128)}, f32[2,1280]{1,0:T(2,128)S(1)}) custom-call(bf16[128,2560]{1,0:T(8,128)(2,1)} %get-tuple-element.41.refs_0_, bf16[128,2560]{1,0:T(8,128)(2,1)} %get-tuple-element.48.refs_1_.refs_0_, f32[2,128,128]{2,1,0:T(8,128)} %rollout.6.refs_3_.refs_2_, f32[16,128]{1,0:T(8,128)S(1)} %copy-done.3, ...), custom_call_target="tpu_custom_call" | custom-call | flops 268435456 | bytes 1048576 | tf_op jit(solution)/shard_map/rollout/pallas_call | solution.py:423
  77.6 3.9 %all-to-all-done.3.parts_ref = f32[32,2,1280]{2,1,0:T(2,128)S(1)} async-done(((f32[32,2,1280]{2,1,0:T(2,128)}), f32[32,2,1280]{2,1,0:T(2,128)S(1)}, u32[]{:S(2)}, u32[]{:S(2)}) %all-to-all-start.3) | async-done | bytes 327712 | tf_op jit(solution)/shard_map/all_to_all | solution.py:500
  81.5 0.3 refit.4
  81.8 13.8 %all_to_all.46.peak_ref = f32[16,1,128]{2,1,0:T(1,128)S(1)} all-to-all(f32[16,1,128]{2,1,0:T(1,128)S(1)} %get-tuple-element.56), channel_id=1, replica_groups=mesh['env'=16,'cand'=32] {'env'}, dimensions={0} | all-to-all | bytes 16384 | tf_op jit(solution)/shard_map/all_to_all | solution.py:508
  95.6 0.8 to_all.4
  96.4 5.0 %all-to-all-start.5 = ((f32[32,1,2688]{2,1,0:T(1,128)}), f32[32,1,2688]{2,1,0:T(1,128)S(1)}, u32[]{:S(2)}, u32[]{:S(2)}) async-start(f32[32,1,2688]{2,1,0:T(1,128)} %get-tuple-element.59), calls=%async_computation.5 | async-start | bytes 688128 | tf_op jit(solution)/shard_map/all_to_all | solution.py:511
  101.4 5.6 %rollout.8 = (f32[1,8,16]{2,1,0:T(8,128)}, f32[2,128,128]{2,1,0:T(8,128)}) custom-call(bf16[128,2560]{1,0:T(8,128)(2,1)} %get-tuple-element.41.refs_0_, bf16[128,2560]{1,0:T(8,128)(2,1)} %get-tuple-element.48.refs_1_.refs_0_, f32[2,128,128]{2,1,0:T(8,128)} %get-tuple-element.50.refs_2_, f32[2,128,128]{2,1,0:T(8,128)} %get-tuple-element.51.refs_3_, ...), custom_call_target="tpu_custom_call" | custom-call | flops 268435456 | bytes 1048576 | tf_op jit(solution)/shard_map/rollout/pallas_call | solution.py:423
  107.1 4.1 %all-to-all-done.5.refs_4_ = f32[32,1,2688]{2,1,0:T(1,128)S(1)} async-done(((f32[32,1,2688]{2,1,0:T(1,128)}), f32[32,1,2688]{2,1,0:T(1,128)S(1)}, u32[]{:S(2)}, u32[]{:S(2)}) %all-to-all-start.5) | async-done | bytes 344096 | tf_op jit(solution)/shard_map/all_to_all | solution.py:511
  111.2 1.9 %actions.5 = (bf16[128,2560]{1,0:T(8,128)(2,1)}, f32[128,128]{1,0:T(8,128)}, f32[32,2,1280]{2,1,0:T(2,128)}, f32[2,1280]{1,0:T(2,128)}) custom-call(f32[2,128,2560]{2,1,0:T(8,128)S(1)} %get-tuple-element.40.refs_0_, s32[3,16,25]{2,1,0:T(8,128)S(1)} %bitcast.8, s32[1]{0:T(128)} %bitcast.2.refs_2_.refs_3_.tie_ref, ...), custom_call_target="tpu_custom_call" | custom-call | tf_op jit(solution)/shard_map/actions/pallas_call | solution.py:212
  113.2 3.8 %all-to-all-start.6 = ((f32[32,2,1280]{2,1,0:T(2,128)}), f32[32,2,1280]{2,1,0:T(2,128)S(1)}, u32[]{:S(2)}, u32[]{:S(2)}) async-start(f32[32,2,1280]{2,1,0:T(2,128)} %get-tuple-element.60), calls=%async_computation.6 | async-start | bytes 655360 | tf_op jit(solution)/shard_map/all_to_all | solution.py:500
  116.9 6.8 %rollout.9 = (f32[1,8,16]{2,1,0:T(8,128)}, f32[2,128,128]{2,1,0:T(8,128)}, f32[2,1280]{1,0:T(2,128)S(1)}) custom-call(bf16[128,2560]{1,0:T(8,128)(2,1)} %get-tuple-element.48.refs_1_.refs_0_, bf16[128,2560]{1,0:T(8,128)(2,1)} %get-tuple-element.61.refs_1_.refs_0_, f32[2,128,128]{2,1,0:T(8,128)} %get-tuple-element.62.refs_2_, ...), custom_call_target="tpu_custom_call" | custom-call | flops 268435456 | bytes 1048576 | tf_op jit(solution)/shard_map/rollout/pallas_call | solution.py:423
  123.7 2.8 %all-to-all-done.6.parts_ref = f32[32,2,1280]{2,1,0:T(2,128)S(1)} async-done(((f32[32,2,1280]{2,1,0:T(2,128)}), f32[32,2,1280]{2,1,0:T(2,128)S(1)}, u32[]{:S(2)}, u32[]{:S(2)}) %all-to-all-start.6) | async-done | bytes 327712 | tf_op jit(solution)/shard_map/all_to_all | solution.py:500
  126.5 0.9 refit.5
  127.4 3.5 %all-to-all-start.7 = ((f32[16,1,128]{2,1,0:T(1,128)}), f32[16,1,128]{2,1,0:T(1,128)S(1)}, u32[]{:S(2)}, u32[]{:S(2)}) async-start(f32[16,1,128]{2,1,0:T(1,128)} %get-tuple-element.67.refs_9_), calls=%async_computation.7 | async-start | bytes 16384 | tf_op jit(solution)/shard_map/all_to_all | solution.py:508
  130.9 2.8 %rollout.10.tie_ref.refs_1_ = f32[2,128,128]{2,1,0:T(8,128)} custom-call(bf16[128,2560]{1,0:T(8,128)(2,1)} %get-tuple-element.61.refs_1_.refs_0_, f32[2,128,128]{2,1,0:T(8,128)} %get-tuple-element.68.refs_1_, f32[16,128]{1,0:T(8,128)S(1)} %copy-done.3, f32[16,128]{1,0:T(8,128)S(1)} %copy-done.4, bf16[128,512]{1,0:T(8,128)(2,1)S(1)} %copy-done, ...), custom_call_target="tpu_custom_call" | custom-call | flops 268435456 | bytes 1048576 | tf_op jit(solution)/shard_map/rollout/pallas_call | solution.py:423
  133.8 8.3 %all-to-all-done.7.peak_ref = f32[16,1,128]{2,1,0:T(1,128)S(1)} async-done(((f32[16,1,128]{2,1,0:T(1,128)}), f32[16,1,128]{2,1,0:T(1,128)S(1)}, u32[]{:S(2)}, u32[]{:S(2)}) %all-to-all-start.7) | async-done | bytes 8224 | tf_op jit(solution)/shard_map/all_to_all | solution.py:508
  142.1 0.8 to_all.5
  142.8 5.8 %all-to-all-start.8 = ((f32[32,1,2688]{2,1,0:T(1,128)}), f32[32,1,2688]{2,1,0:T(1,128)S(1)}, u32[]{:S(2)}, u32[]{:S(2)}) async-start(f32[32,1,2688]{2,1,0:T(1,128)} %get-tuple-element.69), calls=%async_computation.8 | async-start | bytes 688128 | tf_op jit(solution)/shard_map/all_to_all | solution.py:511
  148.6 7.6 %rollout.11 = f32[3,8,16]{2,1,0:T(8,128)} custom-call(bf16[128,2560]{1,0:T(8,128)(2,1)} %get-tuple-element.61.refs_1_.refs_0_, f32[2,128,128]{2,1,0:T(8,128)} %rollout.10.tie_ref.refs_1_, f32[128,128]{1,0:T(8,128)} %get-tuple-element.72.refs_2_, f32[16,128]{1,0:T(8,128)S(1)} %copy-done.3, f32[16,128]{1,0:T(8,128)S(1)} %copy-done.4, ...), custom_call_target="tpu_custom_call" | custom-call | flops 268435456 | bytes 1048576 | tf_op jit(solution)/shard_map/rollout/pallas_call | solution.py:423
  156.2 2.0 %all-to-all-done.8.state_ref = f32[32,1,2688]{2,1,0:T(1,128)S(1)} async-done(((f32[32,1,2688]{2,1,0:T(1,128)}), f32[32,1,2688]{2,1,0:T(1,128)S(1)}, u32[]{:S(2)}, u32[]{:S(2)}) %all-to-all-start.8) | async-done | bytes 344096 | tf_op jit(solution)/shard_map/all_to_all | solution.py:511
  158.3 0.8 finished.1
  (6 shorter events, 0.0 us)
Async XLA Ops:
  0.6 3.2 %copy-start.5 = (s32[16,3,25]{2,0,1:T(8,128)S(1)}, s32[16,3,25]{2,0,1:T(8,128)}, u32[]{:S(2)}) copy-start(s32[16,3,25]{2,0,1:T(8,128)} %param.21) | copy-start | bytes 14404
  0.6 3.2 %copy-start.7 = (f32[16,2560]{1,0:T(8,128)S(1)}, f32[16,2560]{1,0:T(8,128)}, u32[]{:S(2)}) copy-start(f32[16,2560]{1,0:T(8,128)} %refs_5_.7) | copy-start | bytes 491524
  0.7 3.2 %copy-start.6 = (f32[16,2560]{1,0:T(8,128)S(1)}, f32[16,2560]{1,0:T(8,128)}, u32[]{:S(2)}) copy-start(f32[16,2560]{1,0:T(8,128)} %refs_4_.6) | copy-start | bytes 491524
  5.6 50.6 %copy-start = (bf16[128,512]{1,0:T(8,128)(2,1)S(1)}, bf16[128,512]{1,0:T(8,128)(2,1)}, u32[]{:S(2)}) copy-start(bf16[128,512]{1,0:T(8,128)(2,1)} %refs_5_.13) | copy-start | bytes 393220
  5.6 50.6 %copy-start.1 = (bf16[512,128]{1,0:T(8,128)(2,1)S(1)}, bf16[512,128]{1,0:T(8,128)(2,1)}, u32[]{:S(2)}) copy-start(bf16[512,128]{1,0:T(8,128)(2,1)} %refs_7_.7) | copy-start | bytes 393220
  5.6 50.6 %copy-start.2 = (bf16[64,512]{1,0:T(8,128)(2,1)S(1)}, bf16[64,512]{1,0:T(8,128)(2,1)}, u32[]{:S(2)}) copy-start(bf16[64,512]{1,0:T(8,128)(2,1)} %refs_6_.9) | copy-start | bytes 196612
  5.6 50.6 %copy-start.3 = (f32[16,128]{1,0:T(8,128)S(1)}, f32[16,128]{1,0:T(8,128)}, u32[]{:S(2)}) copy-start(f32[16,128]{1,0:T(8,128)} %refs_3_.7) | copy-start | bytes 24580
  5.6 50.6 %copy-start.4 = (f32[16,128]{1,0:T(8,128)S(1)}, f32[16,128]{1,0:T(8,128)}, u32[]{:S(2)}) copy-start(f32[16,128]{1,0:T(8,128)} %refs_4_.11) | copy-start | bytes 24580
  5.6 50.6 %copy-start.8 = (f32[512]{0:T(512)S(1)}, f32[512]{0:T(512)}, u32[]{:S(2)}) copy-start(f32[512]{0:T(512)} %param.19) | copy-start | bytes 6148
  5.6 50.6 %copy-start.9 = (f32[128]{0:T(128)S(1)}, f32[128]{0:T(128)}, u32[]{:S(2)}) copy-start(f32[128]{0:T(128)} %param.20) | copy-start | bytes 1540
  5.6 20.1 %all-to-all-start = ((f32[32,2,1280]{2,1,0:T(2,128)}), f32[32,2,1280]{2,1,0:T(2,128)S(1)}, u32[]{:S(2)}, u32[]{:S(2)}) async-start(f32[32,2,1280]{2,1,0:T(2,128)} %get-tuple-element.42), calls=%async_computation | async-start | bytes 655360 | tf_op jit(solution)/shard_map/all_to_all | solution.py:500
  51.0 14.9 %all-to-all-start.2 = ((f32[32,1,2688]{2,1,0:T(1,128)}), f32[32,1,2688]{2,1,0:T(1,128)S(1)}, u32[]{:S(2)}, u32[]{:S(2)}) async-start(f32[32,1,2688]{2,1,0:T(1,128)} %get-tuple-element.47), calls=%async_computation.2 | async-start | bytes 688128 | tf_op jit(solution)/shard_map/all_to_all | solution.py:511
  67.8 13.7 %all-to-all-start.3 = ((f32[32,2,1280]{2,1,0:T(2,128)}), f32[32,2,1280]{2,1,0:T(2,128)S(1)}, u32[]{:S(2)}, u32[]{:S(2)}) async-start(f32[32,2,1280]{2,1,0:T(2,128)} %get-tuple-element.53), calls=%async_computation.3 | async-start | bytes 655360 | tf_op jit(solution)/shard_map/all_to_all | solution.py:500
  96.4 14.8 %all-to-all-start.5 = ((f32[32,1,2688]{2,1,0:T(1,128)}), f32[32,1,2688]{2,1,0:T(1,128)S(1)}, u32[]{:S(2)}, u32[]{:S(2)}) async-start(f32[32,1,2688]{2,1,0:T(1,128)} %get-tuple-element.59), calls=%async_computation.5 | async-start | bytes 688128 | tf_op jit(solution)/shard_map/all_to_all | solution.py:511
  113.2 13.4 %all-to-all-start.6 = ((f32[32,2,1280]{2,1,0:T(2,128)}), f32[32,2,1280]{2,1,0:T(2,128)S(1)}, u32[]{:S(2)}, u32[]{:S(2)}) async-start(f32[32,2,1280]{2,1,0:T(2,128)} %get-tuple-element.60), calls=%async_computation.6 | async-start | bytes 655360 | tf_op jit(solution)/shard_map/all_to_all | solution.py:500
  127.4 14.6 %all-to-all-start.7 = ((f32[16,1,128]{2,1,0:T(1,128)}), f32[16,1,128]{2,1,0:T(1,128)S(1)}, u32[]{:S(2)}, u32[]{:S(2)}) async-start(f32[16,1,128]{2,1,0:T(1,128)} %get-tuple-element.67.refs_9_), calls=%async_computation.7 | async-start | bytes 16384 | tf_op jit(solution)/shard_map/all_to_all | solution.py:508
  142.8 15.4 %all-to-all-start.8 = ((f32[32,1,2688]{2,1,0:T(1,128)}), f32[32,1,2688]{2,1,0:T(1,128)S(1)}, u32[]{:S(2)}, u32[]{:S(2)}) async-start(f32[32,1,2688]{2,1,0:T(1,128)} %get-tuple-element.69), calls=%async_computation.8 | async-start | bytes 688128 | tf_op jit(solution)/shard_map/all_to_all | solution.py:511
